TPU v7x, 256 devices: a whole 4x4x8 slice. The times are simulated.
256 devices in a mesh: row: 64 (over x, z, core), col: 4 (over y).
Axes of the slice: x: 4, y: 4, z: 8, core: 2. Of those that a mesh axis runs over, the one named last changes fastest.
Arguments:
- eigvecs: float32 [16384, 512], P('row', 'col'), may hold values from -6 to 6
- reflectors: float32 [8, 256, 128, 64], P(None, ('row', 'col')), may hold values from -2 to 2, as said below
- factors: float32 [8, 256, 64, 64], P(None, ('row', 'col')), may hold values from -3 to 3, as said below
- order: int32 [8], replicated, may hold values from 0 to 7, each once
- offsets: int32 [8], replicated, may hold values from 0 to 63
Outputs:
- rotated: float32 [16384, 512], P('row', 'col')
Inputs may be any that keep to these rules, and one draw needn't show every extreme that they name: `order`: a permutation of 0 .. 7. Every block map is orthogonal: with V the block of reflectors and T the block of factors, T is upper triangular and T^-1 + T^-T = V^T V. `factors`: upper triangular, paired with reflectors as promised there.
All inputs are finite; a program needn't handle non-finite values.
Results may differ from a plain program's by a relative error of at most 0.0003.
Values sent between devices are 32-bit elements; how exact they have to be, the bound alone decides.
No kernel may reach another device: no remote copies, remote signals or barrier semaphores. Data moves between devices by JAX's collectives and lax.ppermute only.
A program may use at most 64 MiB of HBM per device.

v0:
```python
import jax
import jax.numpy as jnp
from jax import lax
from jax.sharding import Mesh
from jax.sharding import PartitionSpec as P

ROW = ("row_0", "row_1", "row_2")
ROW_COL = ("row_0", "row_1", "row_2", "col")


highest = lax.Precision.HIGHEST


def passed_along(block, axis, distance):
    devices = range(lax.axis_size(axis))
    route = [(i - distance, i) for i in devices if i - distance in devices]
    return lax.ppermute(block, axis, route)


def nothing_yet(array, identity):
    return jax.tree.map(
        lambda part, zero: jnp.zeros_like(part) + jnp.asarray(zero, part.dtype), array, identity
    )


def carried_in(array, axes, combine, identity):
    before = start = nothing_yet(array, identity)
    subtotal = array
    for axis in reversed(axes):
        size, position = (lax.axis_size(axis), lax.axis_index(axis))
        pieces = jax.tree.map(lambda part: lax.all_gather(part, axis), subtotal)
        inside, subtotal = (start, start)
        for k in range(size):
            passed = k < position
            subtotal = combine(subtotal, jax.tree.map(lambda part: part[k], pieces))
            inside = jax.tree.map(lambda new, old: jnp.where(passed, new, old), subtotal, inside)
        before = combine(inside, before)
    return before


def reflect(segment, householder, triangle):
    inner = jnp.dot(householder.T, segment, precision=highest, preferred_element_type=jnp.float32)
    inner = jnp.dot(triangle, inner, precision=highest, preferred_element_type=jnp.float32)
    return segment - jnp.dot(
        householder, inner, precision=highest, preferred_element_type=jnp.float32
    )


def sweep_apply(extended, house_set, tri_set, offset):
    block_width = house_set.shape[-1]

    def advance(number, current):
        start = offset + number * block_width
        segment = lax.dynamic_slice_in_dim(current, start, 2 * block_width, 0)
        householder = lax.dynamic_index_in_dim(house_set, number, 0, keepdims=False)
        triangle = lax.dynamic_index_in_dim(tri_set, number, 0, keepdims=False)
        return lax.dynamic_update_slice_in_dim(
            current, reflect(segment, householder, triangle), start, 0
        )

    return lax.fori_loop(0, house_set.shape[0], advance, extended)


def compose(earlier, later):
    first_map = jnp.dot(later[0], earlier[0], precision=highest, preferred_element_type=jnp.float32)
    shifted = (
        jnp.dot(later[0], earlier[1], precision=highest, preferred_element_type=jnp.float32)
        + later[1]
    )
    return (first_map, shifted)


def local(eigvecs, reflectors, factors, order, offsets):
    height = eigvecs.shape[0]
    columns = eigvecs.shape[1]
    block_width = reflectors.shape[-1]
    span_rows = 2 * block_width
    leading = lax.axis_index(ROW) == 0
    identity = jnp.eye(span_rows, dtype=jnp.float32)
    probe = jnp.concatenate([identity, jnp.zeros((height, span_rows), jnp.float32)], 0)
    every_house, every_tri = (
        lax.all_gather(reflectors, "col", axis=1, tiled=True),
        lax.all_gather(factors, "col", axis=1, tiled=True),
    )
    vectors = eigvecs
    for position in range(order.shape[0]):
        stored = order[position]
        offset = offsets[stored]
        house_set = lax.dynamic_index_in_dim(every_house, stored, 0, keepdims=False)
        tri_set = lax.dynamic_index_in_dim(every_tri, stored, 0, keepdims=False)
        next_rows = passed_along(vectors[:span_rows], ROW, -1)
        top_rows = jnp.where(leading, vectors[:span_rows], 0.0)
        extended = jnp.concatenate([top_rows, vectors[span_rows:], next_rows], 0)
        joined = sweep_apply(jnp.concatenate([extended, probe], 1), house_set, tri_set, offset)
        partial_value = joined[:, :columns]
        response = joined[:, columns:]
        transfer = jnp.where(leading, 0.0, response[height:])
        empty = jnp.zeros((span_rows, columns), jnp.float32)
        composed = carried_in((transfer, partial_value[height:]), ROW, compose, (identity, empty))
        incoming = composed[1]
        vectors = partial_value[:height] + jnp.dot(
            response[:height], incoming, precision=highest, preferred_element_type=jnp.float32
        )
    return vectors


def solution(mesh):
    torus = Mesh(
        mesh.devices.reshape(4, 8, 2, mesh.shape["col"]), ("row_0", "row_1", "row_2", "col")
    )
    placed = (P(ROW, "col"), P(None, ROW_COL, None, None), P(None, ROW_COL, None, None), P(), P())
    return jax.shard_map(
        local, mesh=torus, in_specs=placed, out_specs=P(ROW, "col"), check_vma=False
    )
```

profile of v0, /device:TPU:2, one launch (start us, length us, event | category | flops | bytes accessed | tf_op | source)
XLA Modules:
  0.0 850.5 jit_solution(460673301519701262)
XLA Ops:
  7.5 7.2 collective-permute-start
  31.2 16.9 %all_gather.295 = f32[8,4,64,64]{3,2,1,0:T(8,128)S(1)} all-gather(f32[8,1,64,64]{3,2,1,0:T(8,128)S(1)} %copy-done), channel_id=1, replica_groups=mesh['row_0'=4,'row_1'=8,'row_2'=2,'col'=4] {'col'}, dimensions={1}, use_global_device_ids=true | all-gather | bytes 655360 | tf_op jit(solution)/shard_map/all_gather | solution.py:83
  49.7 9.6 %while.104 = (s32[]{:T(128)}, f32[384,256]{1,0:T(8,128)S(1)}, s32[]{:T(128)}, f32[4,128,64]{2,1,0:T(8,128)S(1)}, f32[4,64,64]{2,1,0:T(8,128)S(1)}, /*index=5*/s32[]{:T(128)}, s32[]{:T(128)}, s32[]{:T(128)}, s32[]{:T(128)}) while((s32[]{:T(128)}, f32[384,256]{1,0:T(8,128)S(1)}, s32[]{:T(128)}, f32[4,128,64]{2,1,0:T(8,128)S(1)}, ...), condition=%wide.region_1.2_spmd, body=%wide.region_0.1_spmd.sunk | while | flops 62947336 | bytes 1081519 | solution.py:61
  63.7 25.9 %all-gather.4 = f32[1024,128]{1,0:T(8,128)S(1)} all-gather(f32[128,128]{1,0:T(8,128)S(1)} %convolution_add_fusion.124), channel_id=6, replica_groups=mesh['row_0'=4,'row_1'=8,'row_2'=2,'col'=4] {'row_1'}, dimensions={0}, use_global_device_ids=true | all-gather | bytes 589824 | tf_op jit(solution)/shard_map/all_gather | solution.py:31
  89.8 25.4 %all-gather.1 = f32[1024,128]{1,0:T(8,128)S(1)} all-gather(f32[128,128]{1,0:T(8,128)S(1)} %fusion.582), channel_id=3, replica_groups=mesh['row_0'=4,'row_1'=8,'row_2'=2,'col'=4] {'row_1'}, dimensions={0}, use_global_device_ids=true | all-gather | bytes 589824 | tf_op jit(solution)/shard_map/all_gather | solution.py:31
  117.2 12.5 %all-gather.5 = f32[512,128]{1,0:T(8,128)S(1)} all-gather(f32[128,128]{1,0:T(8,128)S(1)} %convolution_add_fusion.117), channel_id=7, replica_groups=mesh['row_0'=4,'row_1'=8,'row_2'=2,'col'=4] {'row_0'}, dimensions={0}, use_global_device_ids=true | all-gather | bytes 327680 | tf_op jit(solution)/shard_map/all_gather | solution.py:31
  131.2 12.3 %all-gather.2 = f32[512,128]{1,0:T(8,128)S(1)} all-gather(f32[128,128]{1,0:T(8,128)S(1)} %fusion.577), channel_id=4, replica_groups=mesh['row_0'=4,'row_1'=8,'row_2'=2,'col'=4] {'row_0'}, dimensions={0}, use_global_device_ids=true | all-gather | bytes 327680 | tf_op jit(solution)/shard_map/all_gather | solution.py:31
  149.5 9.6 %while.105 = (s32[]{:T(128)}, f32[384,256]{1,0:T(8,128)S(1)}, s32[]{:T(128)}, f32[4,128,64]{2,1,0:T(8,128)S(1)}, f32[4,64,64]{2,1,0:T(8,128)S(1)}, /*index=5*/s32[]{:T(128)}, s32[]{:T(128)}, s32[]{:T(128)}, s32[]{:T(128)}) while((s32[]{:T(128)}, f32[384,256]{1,0:T(8,128)S(1)}, s32[]{:T(128)}, f32[4,128,64]{2,1,0:T(8,128)S(1)}, ...), condition=%wide.region_3.4_spmd, body=%wide.region_2.3_spmd.sunk | while | flops 62947336 | bytes 1081519 | solution.py:61
  159.2 2.2 all-gather.6
  161.7 25.3 %all-gather.7 = f32[1024,128]{1,0:T(8,128)S(1)} all-gather(f32[128,128]{1,0:T(8,128)S(1)} %fusion.554), channel_id=9, replica_groups=mesh['row_0'=4,'row_1'=8,'row_2'=2,'col'=4] {'row_1'}, dimensions={0}, use_global_device_ids=true | all-gather | bytes 589824 | tf_op jit(solution)/shard_map/all_gather | solution.py:31
  189.6 25.3 %all-gather.10 = f32[1024,128]{1,0:T(8,128)S(1)} all-gather(f32[128,128]{1,0:T(8,128)S(1)} %convolution_add_fusion.109), channel_id=12, replica_groups=mesh['row_0'=4,'row_1'=8,'row_2'=2,'col'=4] {'row_1'}, dimensions={0}, use_global_device_ids=true | all-gather | bytes 589824 | tf_op jit(solution)/shard_map/all_gather | solution.py:31
  216.7 12.6 %all-gather.11 = f32[512,128]{1,0:T(8,128)S(1)} all-gather(f32[128,128]{1,0:T(8,128)S(1)} %convolution_add_fusion.102), channel_id=13, replica_groups=mesh['row_0'=4,'row_1'=8,'row_2'=2,'col'=4] {'row_0'}, dimensions={0}, use_global_device_ids=true | all-gather | bytes 327680 | tf_op jit(solution)/shard_map/all_gather | solution.py:31
  231.0 12.3 %all-gather.8 = f32[512,128]{1,0:T(8,128)S(1)} all-gather(f32[128,128]{1,0:T(8,128)S(1)} %fusion.549), channel_id=10, replica_groups=mesh['row_0'=4,'row_1'=8,'row_2'=2,'col'=4] {'row_0'}, dimensions={0}, use_global_device_ids=true | all-gather | bytes 327680 | tf_op jit(solution)/shard_map/all_gather | solution.py:31
  248.9 8.8 %while.106 = (s32[]{:T(128)}, f32[384,256]{1,0:T(8,128)S(1)}, s32[]{:T(128)}, f32[4,128,64]{2,1,0:T(8,128)S(1)}, f32[4,64,64]{2,1,0:T(8,128)S(1)}, /*index=5*/s32[]{:T(128)}, s32[]{:T(128)}, s32[]{:T(128)}, s32[]{:T(128)}) while((s32[]{:T(128)}, f32[384,256]{1,0:T(8,128)S(1)}, s32[]{:T(128)}, f32[4,128,64]{2,1,0:T(8,128)S(1)}, ...), condition=%wide.region_5.6_spmd, body=%wide.region_4.5_spmd.sunk | while | flops 62947336 | bytes 1081519 | solution.py:61
  257.7 3.7 all-gather.12
  261.8 25.4 %all-gather.13 = f32[1024,128]{1,0:T(8,128)S(1)} all-gather(f32[128,128]{1,0:T(8,128)S(1)} %fusion.526), channel_id=15, replica_groups=mesh['row_0'=4,'row_1'=8,'row_2'=2,'col'=4] {'row_1'}, dimensions={0}, use_global_device_ids=true | all-gather | bytes 589824 | tf_op jit(solution)/shard_map/all_gather | solution.py:31
  289.7 25.8 %all-gather.16 = f32[1024,128]{1,0:T(8,128)S(1)} all-gather(f32[128,128]{1,0:T(8,128)S(1)} %convolution_add_fusion.94), channel_id=18, replica_groups=mesh['row_0'=4,'row_1'=8,'row_2'=2,'col'=4] {'row_1'}, dimensions={0}, use_global_device_ids=true | all-gather | bytes 589824 | tf_op jit(solution)/shard_map/all_gather | solution.py:31
  317.4 12.1 %all-gather.17 = f32[512,128]{1,0:T(8,128)S(1)} all-gather(f32[128,128]{1,0:T(8,128)S(1)} %convolution_add_fusion.87), channel_id=19, replica_groups=mesh['row_0'=4,'row_1'=8,'row_2'=2,'col'=4] {'row_0'}, dimensions={0}, use_global_device_ids=true | all-gather | bytes 327680 | tf_op jit(solution)/shard_map/all_gather | solution.py:31
  331.1 12.3 %all-gather.14 = f32[512,128]{1,0:T(8,128)S(1)} all-gather(f32[128,128]{1,0:T(8,128)S(1)} %fusion.521), channel_id=16, replica_groups=mesh['row_0'=4,'row_1'=8,'row_2'=2,'col'=4] {'row_0'}, dimensions={0}, use_global_device_ids=true | all-gather | bytes 327680 | tf_op jit(solution)/shard_map/all_gather | solution.py:31
  349.0 9.1 %while.107 = (s32[]{:T(128)}, f32[384,256]{1,0:T(8,128)S(1)}, s32[]{:T(128)}, f32[4,128,64]{2,1,0:T(8,128)S(1)}, f32[4,64,64]{2,1,0:T(8,128)S(1)}, /*index=5*/s32[]{:T(128)}, s32[]{:T(128)}, s32[]{:T(128)}, s32[]{:T(128)}) while((s32[]{:T(128)}, f32[384,256]{1,0:T(8,128)S(1)}, s32[]{:T(128)}, f32[4,128,64]{2,1,0:T(8,128)S(1)}, ...), condition=%wide.region_7.8_spmd, body=%wide.region_6.7_spmd.sunk | while | flops 62947336 | bytes 1081519 | solution.py:61
  358.1 2.4 all-gather.18
  360.9 25.3 %all-gather.19 = f32[1024,128]{1,0:T(8,128)S(1)} all-gather(f32[128,128]{1,0:T(8,128)S(1)} %fusion.498), channel_id=21, replica_groups=mesh['row_0'=4,'row_1'=8,'row_2'=2,'col'=4] {'row_1'}, dimensions={0}, use_global_device_ids=true | all-gather | bytes 589824 | tf_op jit(solution)/shard_map/all_gather | solution.py:31
  388.7 25.5 %all-gather.22 = f32[1024,128]{1,0:T(8,128)S(1)} all-gather(f32[128,128]{1,0:T(8,128)S(1)} %convolution_add_fusion.79), channel_id=24, replica_groups=mesh['row_0'=4,'row_1'=8,'row_2'=2,'col'=4] {'row_1'}, dimensions={0}, use_global_device_ids=true | all-gather | bytes 589824 | tf_op jit(solution)/shard_map/all_gather | solution.py:31
  416.0 12.4 %all-gather.23 = f32[512,128]{1,0:T(8,128)S(1)} all-gather(f32[128,128]{1,0:T(8,128)S(1)} %convolution_add_fusion.72), channel_id=25, replica_groups=mesh['row_0'=4,'row_1'=8,'row_2'=2,'col'=4] {'row_0'}, dimensions={0}, use_global_device_ids=true | all-gather | bytes 327680 | tf_op jit(solution)/shard_map/all_gather | solution.py:31
  430.1 12.3 %all-gather.20 = f32[512,128]{1,0:T(8,128)S(1)} all-gather(f32[128,128]{1,0:T(8,128)S(1)} %fusion.493), channel_id=22, replica_groups=mesh['row_0'=4,'row_1'=8,'row_2'=2,'col'=4] {'row_0'}, dimensions={0}, use_global_device_ids=true | all-gather | bytes 327680 | tf_op jit(solution)/shard_map/all_gather | solution.py:31
  448.0 9.4 %while.108 = (s32[]{:T(128)}, f32[384,256]{1,0:T(8,128)S(1)}, s32[]{:T(128)}, f32[4,128,64]{2,1,0:T(8,128)S(1)}, f32[4,64,64]{2,1,0:T(8,128)S(1)}, /*index=5*/s32[]{:T(128)}, s32[]{:T(128)}, s32[]{:T(128)}, s32[]{:T(128)}) while((s32[]{:T(128)}, f32[384,256]{1,0:T(8,128)S(1)}, s32[]{:T(128)}, f32[4,128,64]{2,1,0:T(8,128)S(1)}, ...), condition=%wide.region_9.10_spmd, body=%wide.region_8.9_spmd.sunk | while | flops 62947336 | bytes 1081519 | solution.py:61
  457.5 2.8 all-gather.24
  460.6 25.8 %all-gather.25 = f32[1024,128]{1,0:T(8,128)S(1)} all-gather(f32[128,128]{1,0:T(8,128)S(1)} %fusion.470), channel_id=27, replica_groups=mesh['row_0'=4,'row_1'=8,'row_2'=2,'col'=4] {'row_1'}, dimensions={0}, use_global_device_ids=true | all-gather | bytes 589824 | tf_op jit(solution)/shard_map/all_gather | solution.py:31
  488.9 25.3 %all-gather.28 = f32[1024,128]{1,0:T(8,128)S(1)} all-gather(f32[128,128]{1,0:T(8,128)S(1)} %convolution_add_fusion.64), channel_id=30, replica_groups=mesh['row_0'=4,'row_1'=8,'row_2'=2,'col'=4] {'row_1'}, dimensions={0}, use_global_device_ids=true | all-gather | bytes 589824 | tf_op jit(solution)/shard_map/all_gather | solution.py:31
  516.1 12.8 %all-gather.29 = f32[512,128]{1,0:T(8,128)S(1)} all-gather(f32[128,128]{1,0:T(8,128)S(1)} %convolution_add_fusion.57), channel_id=31, replica_groups=mesh['row_0'=4,'row_1'=8,'row_2'=2,'col'=4] {'row_0'}, dimensions={0}, use_global_device_ids=true | all-gather | bytes 327680 | tf_op jit(solution)/shard_map/all_gather | solution.py:31
  530.6 12.5 %all-gather.26 = f32[512,128]{1,0:T(8,128)S(1)} all-gather(f32[128,128]{1,0:T(8,128)S(1)} %fusion.465), channel_id=28, replica_groups=mesh['row_0'=4,'row_1'=8,'row_2'=2,'col'=4] {'row_0'}, dimensions={0}, use_global_device_ids=true | all-gather | bytes 327680 | tf_op jit(solution)/shard_map/all_gather | solution.py:31
  548.6 9.2 %while.109 = (s32[]{:T(128)}, f32[384,256]{1,0:T(8,128)S(1)}, s32[]{:T(128)}, f32[4,128,64]{2,1,0:T(8,128)S(1)}, f32[4,64,64]{2,1,0:T(8,128)S(1)}, /*index=5*/s32[]{:T(128)}, s32[]{:T(128)}, s32[]{:T(128)}, s32[]{:T(128)}) while((s32[]{:T(128)}, f32[384,256]{1,0:T(8,128)S(1)}, s32[]{:T(128)}, f32[4,128,64]{2,1,0:T(8,128)S(1)}, ...), condition=%wide.region_11.12_spmd, body=%wide.region_10.11_spmd.sunk | while | flops 62947336 | bytes 1081519 | solution.py:61
  560.2 25.6 %all-gather.31 = f32[1024,128]{1,0:T(8,128)S(1)} all-gather(f32[128,128]{1,0:T(8,128)S(1)} %fusion.442), channel_id=33, replica_groups=mesh['row_0'=4,'row_1'=8,'row_2'=2,'col'=4] {'row_1'}, dimensions={0}, use_global_device_ids=true | all-gather | bytes 589824 | tf_op jit(solution)/shard_map/all_gather | solution.py:31
  588.2 25.3 %all-gather.34 = f32[1024,128]{1,0:T(8,128)S(1)} all-gather(f32[128,128]{1,0:T(8,128)S(1)} %convolution_add_fusion.49), channel_id=36, replica_groups=mesh['row_0'=4,'row_1'=8,'row_2'=2,'col'=4] {'row_1'}, dimensions={0}, use_global_device_ids=true | all-gather | bytes 589824 | tf_op jit(solution)/shard_map/all_gather | solution.py:31
  615.4 12.3 %all-gather.35 = f32[512,128]{1,0:T(8,128)S(1)} all-gather(f32[128,128]{1,0:T(8,128)S(1)} %convolution_add_fusion.42), channel_id=37, replica_groups=mesh['row_0'=4,'row_1'=8,'row_2'=2,'col'=4] {'row_0'}, dimensions={0}, use_global_device_ids=true | all-gather | bytes 327680 | tf_op jit(solution)/shard_map/all_gather | solution.py:31
  629.4 12.3 %all-gather.32 = f32[512,128]{1,0:T(8,128)S(1)} all-gather(f32[128,128]{1,0:T(8,128)S(1)} %fusion.437), channel_id=34, replica_groups=mesh['row_0'=4,'row_1'=8,'row_2'=2,'col'=4] {'row_0'}, dimensions={0}, use_global_device_ids=true | all-gather | bytes 327680 | tf_op jit(solution)/shard_map/all_gather | solution.py:31
  647.2 9.4 %while.110 = (s32[]{:T(128)}, f32[384,256]{1,0:T(8,128)S(1)}, s32[]{:T(128)}, f32[4,128,64]{2,1,0:T(8,128)S(1)}, f32[4,64,64]{2,1,0:T(8,128)S(1)}, /*index=5*/s32[]{:T(128)}, s32[]{:T(128)}, s32[]{:T(128)}, s32[]{:T(128)}) while((s32[]{:T(128)}, f32[384,256]{1,0:T(8,128)S(1)}, s32[]{:T(128)}, f32[4,128,64]{2,1,0:T(8,128)S(1)}, ...), condition=%wide.region_13.14_spmd, body=%wide.region_12.13_spmd.sunk | while | flops 62947336 | bytes 1081519 | solution.py:61
  656.7 2.8 all-gather.36
  659.9 25.5 %all-gather.37 = f32[1024,128]{1,0:T(8,128)S(1)} all-gather(f32[128,128]{1,0:T(8,128)S(1)} %fusion.414), channel_id=39, replica_groups=mesh['row_0'=4,'row_1'=8,'row_2'=2,'col'=4] {'row_1'}, dimensions={0}, use_global_device_ids=true | all-gather | bytes 589824 | tf_op jit(solution)/shard_map/all_gather | solution.py:31
  687.9 25.3 %all-gather.40 = f32[1024,128]{1,0:T(8,128)S(1)} all-gather(f32[128,128]{1,0:T(8,128)S(1)} %convolution_add_fusion.34), channel_id=42, replica_groups=mesh['row_0'=4,'row_1'=8,'row_2'=2,'col'=4] {'row_1'}, dimensions={0}, use_global_device_ids=true | all-gather | bytes 589824 | tf_op jit(solution)/shard_map/all_gather | solution.py:31
  715.0 12.5 %all-gather.41 = f32[512,128]{1,0:T(8,128)S(1)} all-gather(f32[128,128]{1,0:T(8,128)S(1)} %convolution_add_fusion.27), channel_id=43, replica_groups=mesh['row_0'=4,'row_1'=8,'row_2'=2,'col'=4] {'row_0'}, dimensions={0}, use_global_device_ids=true | all-gather | bytes 327680 | tf_op jit(solution)/shard_map/all_gather | solution.py:31
  729.2 12.3 %all-gather.38 = f32[512,128]{1,0:T(8,128)S(1)} all-gather(f32[128,128]{1,0:T(8,128)S(1)} %fusion.409), channel_id=40, replica_groups=mesh['row_0'=4,'row_1'=8,'row_2'=2,'col'=4] {'row_0'}, dimensions={0}, use_global_device_ids=true | all-gather | bytes 327680 | tf_op jit(solution)/shard_map/all_gather | solution.py:31
  747.1 8.9 %while.111 = (s32[]{:T(128)}, f32[384,256]{1,0:T(8,128)S(1)}, s32[]{:T(128)}, f32[4,128,64]{2,1,0:T(8,128)S(1)}, f32[4,64,64]{2,1,0:T(8,128)S(1)}, /*index=5*/s32[]{:T(128)}, s32[]{:T(128)}, s32[]{:T(128)}, s32[]{:T(128)}) while((s32[]{:T(128)}, f32[384,256]{1,0:T(8,128)S(1)}, s32[]{:T(128)}, f32[4,128,64]{2,1,0:T(8,128)S(1)}, ...), condition=%wide.region_15.16_spmd, body=%wide.region_14.15_spmd.sunk | while | flops 62947336 | bytes 1081519 | solution.py:61
  756.0 2.4 all-gather.42
  758.8 25.9 %all-gather.43 = f32[1024,128]{1,0:T(8,128)S(1)} all-gather(f32[128,128]{1,0:T(8,128)S(1)} %fusion.386), channel_id=45, replica_groups=mesh['row_0'=4,'row_1'=8,'row_2'=2,'col'=4] {'row_1'}, dimensions={0}, use_global_device_ids=true | all-gather | bytes 589824 | tf_op jit(solution)/shard_map/all_gather | solution.py:31
  787.2 25.5 %all-gather.46 = f32[1024,128]{1,0:T(8,128)S(1)} all-gather(f32[128,128]{1,0:T(8,128)S(1)} %convolution_add_fusion.19), channel_id=48, replica_groups=mesh['row_0'=4,'row_1'=8,'row_2'=2,'col'=4] {'row_1'}, dimensions={0}, use_global_device_ids=true | all-gather | bytes 589824 | tf_op jit(solution)/shard_map/all_gather | solution.py:31
  814.6 12.3 %all-gather.47 = f32[512,128]{1,0:T(8,128)S(1)} all-gather(f32[128,128]{1,0:T(8,128)S(1)} %convolution_add_fusion.12), channel_id=49, replica_groups=mesh['row_0'=4,'row_1'=8,'row_2'=2,'col'=4] {'row_0'}, dimensions={0}, use_global_device_ids=true | all-gather | bytes 327680 | tf_op jit(solution)/shard_map/all_gather | solution.py:31
  828.6 12.3 %all-gather.44 = f32[512,128]{1,0:T(8,128)S(1)} all-gather(f32[128,128]{1,0:T(8,128)S(1)} %fusion.381), channel_id=46, replica_groups=mesh['row_0'=4,'row_1'=8,'row_2'=2,'col'=4] {'row_0'}, dimensions={0}, use_global_device_ids=true | all-gather | bytes 327680 | tf_op jit(solution)/shard_map/all_gather | solution.py:31
  (441 shorter events, 151.7 us)
Async XLA Ops:
  6.5 0.9 copy-start.1
  6.5 41.7 %all-gather.50.cloned.1.call-start = ((), (), s32[]{:S(2)}) async-start(), calls=%async_computation | async-start | bytes 1310720 | tf_op jit(solution)/shard_map/all_gather | solution.py:82
  7.3 23.9 %copy-start = (f32[8,1,64,64]{3,2,1,0:T(8,128)S(1)}, f32[8,1,64,64]{3,2,1,0:T(8,128)}, u32[]{:S(2)}) copy-start(f32[8,1,64,64]{3,2,1,0:T(8,128)} %param.23) | copy-start | bytes 393220
  7.5 7.2 copy-start.3
  7.5 40.7 %collective-permute-start = (f32[128,128]{1,0:T(8,128)S(1)}, f32[128,128]{1,0:T(8,128)S(1)}, u32[]{:S(2)}, u32[]{:S(2)}) collective-permute-start(f32[128,128]{1,0:T(8,128)S(1)} %get-tuple-element.900), channel_id=1, source_target_pairs={{4,0},{8,4},{12,8},{16,12},{20,16},{24,20},{28,24},{32,28},{36,32}... | collective-permute-start | bytes 196616 | tf_op jit(solution)/shard_map/ppermute | solution.py:17
  27.9 2.5 copy-start.2
  145.6 3.8 collective-permute-start.1
  245.0 3.8 collective-permute-start.2
  345.2 3.8 collective-permute-start.3
  444.2 3.8 collective-permute-start.4
  544.8 3.8 collective-permute-start.5
  643.4 3.8 collective-permute-start.6
  743.2 3.8 collective-permute-start.7
Sparse Core Ops, SparseCore 0:
  9.1 31.5 all-gather.49
where the time goes:
time: 861 us; the launch traced here: 851 us
  blocking collectives  658 us (76%)
  matrix products  72.6 us (8%)
  local copies, waits for them, and re-layouts  33.3 us (4%)
  between operations  31.2 us (4%)
  loops' own time  21.6 us (3%)
  starting transfers between devices  20.6 us (2%)
  waiting for transfers between devices  13 us (2%)
    all_gather x48, blocking collectives, carried_in(): pieces = jax.tree.map(lambda part: lax.all_gather(part, axis), subtotal)  641 us
    dynamic_update_slice x32, local copies, waits for them, and re-layouts, advance(): lax.dynamic_update_slice_in_dim(current, reflect(segment, householder, tr...  29.2 us
    dot_general x136, matrix products, compose(): jnp.dot(later[0], earlier[1], precision=highest, preferred_element_type=j...  27.4 us
    another operation x8, loops' own time, sweep_apply(): return lax.fori_loop(0, house_set.shape[0], advance, extended)  21.6 us
    ppermute x8, starting transfers between devices, passed_along(): return lax.ppermute(block, axis, route)  20.6 us
    dot_general x96, matrix products, compose(): jnp.dot(later[0], earlier[0], precision=highest, preferred_element_type=j...  19.2 us
  transfers between devices with their start and end apart: 9, of which 7 were waited for; matrix products, arithmetic and copies ran while one was open for 0% of the time, Pallas kernels for 0%

commit v1 on v0

v1 whole, which is shorter than its diff:
```python
import functools

import jax
import jax.numpy as jnp
from jax import lax
from jax.experimental import pallas as pl
from jax.experimental.pallas import tpu as pltpu
from jax.sharding import Mesh
from jax.sharding import PartitionSpec as P

ROW = ("x", "z", "core")
ROW_COL = ("x", "z", "core", "col")
W = 64
S = 2 * W
H = 4 * W
CHIPS, PLANES = 8, 4
F32 = jnp.float32


def dot(a, b):
    return jnp.dot(a, b, precision=lax.Precision.HIGHEST, preferred_element_type=F32)


def call(body, outs, *args, smem=0, scratch=(), flops=20_000_000):
    spaces = [pl.BlockSpec(memory_space=pltpu.SMEM)] * smem
    spaces += [pl.BlockSpec(memory_space=pltpu.VMEM)] * (len(args) - smem)
    single = not isinstance(outs, list)
    shapes = [jax.ShapeDtypeStruct(o, F32) for o in ([outs] if single else outs)]
    specs = [pl.BlockSpec(memory_space=pltpu.VMEM)] * len(shapes)
    return pl.pallas_call(
        body,
        out_shape=shapes[0] if single else shapes,
        in_specs=spaces,
        out_specs=specs[0] if single else specs,
        scratch_shapes=list(scratch),
        cost_estimate=pl.CostEstimate(flops=flops, bytes_accessed=1_000_000, transcendentals=0),
        compiler_params=pltpu.CompilerParams(vmem_limit_bytes=32 * 1024 * 1024),
    )(*args)


def eye(n):
    r = lax.broadcasted_iota(jnp.int32, (n, n), 0)
    c = lax.broadcasted_iota(jnp.int32, (n, n), 1)
    return jnp.where(r == c, 1.0, 0.0).astype(F32)


def row_index():
    x, z, core = lax.axis_index("x"), lax.axis_index("z"), lax.axis_index("core")
    return (x * CHIPS + z) * 2 + core


def is_last(g):
    return g == PLANES * CHIPS * 2 - 1


def block_kernel(positions, order, house, tri, out):
    for i, p in enumerate(positions):
        v = house[order[p]]
        t = tri[order[p]]
        inner = lax.dot_general(
            t, v, (((1,), (1,)), ((), ())), precision=lax.Precision.HIGHEST, preferred_element_type=F32
        )
        h = eye(S) - dot(v, inner)
        for c in range(out.shape[0]):
            out[c, i] = h


def chain(wins, blocks, count, offset, carry):
    kept = carry
    for j in range(count):
        rest = [win[pl.ds(offset + (j + 1) * W, W), :] for win in wins]
        out = dot(blocks(j), jnp.concatenate([carry, jnp.concatenate(rest, 1)], 0))
        for k, win in enumerate(wins):
            win[pl.ds(offset + j * W, W), :] = out[:W, k * S : (k + 1) * S]
        carry = out[W:]
        if j == 3:
            kept = carry
    return kept


def maps_kernel(phases, order, offsets, blocks, halo, maps, response, win):
    last = is_last(row_index())
    r = lax.broadcasted_iota(jnp.int32, (W, S), 0)
    c = lax.broadcasted_iota(jnp.int32, (W, S), 1)
    for i, n in enumerate(phases):
        off_a, off_b = offsets[order[2 * n]], offsets[order[2 * n + 1]]
        win[...] = jnp.zeros_like(win)

        def first(j, i=i):
            return blocks[j, 2 * i] if j < 4 else halo[j - 4, i]

        def second(j, i=i):
            return blocks[j, 2 * i + 1]

        maps[i, :W] = chain([win], first, 6, off_a, jnp.where(r == c, 1.0, 0.0).astype(F32))
        win[H:, :] = jnp.where(last, 0.0, win[H:, :])
        maps[i, W:] = chain([win], second, 4, off_b, jnp.where(r + W == c, 1.0, 0.0).astype(F32))
        response[i] = win[pl.ds(off_b, H), :]


def values_kernel(n, i, order, offsets, own, halo_rows, blocks, halo, partial, win):
    g = row_index()
    last, leading = is_last(g), g == 0
    off_a, off_b = offsets[order[2 * n]], offsets[order[2 * n + 1]]
    win[:H, :] = own[:H, :]
    before = offsets[order[2 * n - 1]]
    rows = lax.broadcasted_iota(jnp.int32, (H, 1), 0)
    win[H:, :] = jnp.where((rows < before) & ~last, own[H:, :], halo_rows[...])

    def first(j):
        return blocks[j, 2 * i] if j < 4 else halo[j - 4, i]

    def second(j):
        return blocks[j, 2 * i + 1]

    partial[:W] = chain([win], first, 6, off_a, jnp.where(leading, win[pl.ds(off_a, W), :], 0.0))
    win[H:, :] = jnp.where(last, 0.0, win[H:, :])
    partial[W:] = chain([win], second, 4, off_b, jnp.where(leading, win[pl.ds(off_b, W), :], 0.0))


def join_maps_kernel(mine, theirs, half):
    core = lax.axis_index("core")
    start = pl.multiple_of(core * W, W)
    for i in range(mine.shape[0]):
        front = jnp.where(core == 1, theirs[i], mine[i])
        back = jnp.where(core == 1, mine[i, pl.ds(start, W), :], theirs[i, pl.ds(start, W), :])
        value = dot(back, front)
        if len(half.shape) == 4:
            for c in range(half.shape[0]):
                half[c, i] = value
        else:
            half[i] = value


def join_values_kernel(i, mine, theirs, partial, other, half):
    core = lax.axis_index("core")
    start = pl.multiple_of(core * W, W)
    rows = pl.ds(start, W)
    front = jnp.where(core == 1, other[...], partial[...])
    back = jnp.where(core == 1, partial[rows, :], other[rows, :])
    later = jnp.where(core == 1, mine[i, rows, :], theirs[i, rows, :])
    half[...] = dot(later, front) + back


def compose_kernel(theirs, own, swapped, entering, at_chip, whole):
    z, core = lax.axis_index("z"), lax.axis_index("core")
    for i in range(theirs.shape[0]):
        entry = jnp.where(core == 1, theirs[i], eye(S))
        to_here, to_end = jnp.zeros((S, S), F32), eye(S)
        for k in reversed(range(CHIPS)):
            both = jnp.concatenate([to_here, to_end], 0)
            entering[i, :, k * S : (k + 1) * S] = both
            low = jnp.where(core == 1, swapped[k, i], own[k, i])
            high = jnp.where(core == 1, own[k, i], swapped[k, i])
            step = jnp.concatenate([low, high], 0)
            both = dot(both, step)
            to_here = jnp.where(k == z, entry, both[:S])
            to_end = both[S:]
        at_chip[i] = to_here
        for x in range(PLANES):
            whole[x, i] = to_end


def across_kernel(at_chip, whole, towards):
    x = lax.axis_index("x")
    for i in range(at_chip.shape[0]):
        value = jnp.zeros((S, S), F32)
        for k in reversed(range(PLANES)):
            towards[i, :, k * S : (k + 1) * S] = value
            if k:
                value = dot(value, whole[k, i])
            value = jnp.where(k == x, at_chip[i], value)


def enter_kernel(i, entering, gathered, other, carry, out):
    core = lax.axis_index("core")
    both = dot(entering[i], gathered[...])
    carry[...] = both[:S] + jnp.where(core == 1, other[...], 0.0)
    for x in range(PLANES):
        out[x] = both[S:]


def finish_kernel(n, i, order, offsets, carry, towards, crossing, response, window, out):
    off_b = offsets[order[2 * n + 1]]
    total = carry[...] + dot(towards[i], crossing[...])
    out[...] = window[...]
    rows = pl.ds(off_b, H)
    out[rows, :] = out[rows, :] + dot(response[i], total)


def last_kernel(n, order, offsets, window, before, out):
    g = row_index()
    off_b = offsets[order[2 * n + 1]]
    rows = lax.broadcasted_iota(jnp.int32, (W, 1), 0)
    out[...] = window[:H, :]
    out[:W, :] = jnp.where((rows < off_b) & (g != 0), before[...], window[:W, :])


def open_kernel(order, offsets, own, halo_rows, blocks, halo, partial, window, response, win):
    g = row_index()
    last, leading = is_last(g), g == 0
    off_a, off_b = offsets[order[0]], offsets[order[1]]
    win[...] = jnp.zeros_like(win)
    window[:H, :] = own[...]
    window[H:, :] = halo_rows[...]
    r = lax.broadcasted_iota(jnp.int32, (W, S), 0)
    c = lax.broadcasted_iota(jnp.int32, (W, S), 1)
    ones = jnp.where(r == c, 1.0, 0.0).astype(F32)
    carry = jnp.concatenate([jnp.where(leading, window[pl.ds(off_a, W), :], 0.0), ones], 1)
    wins = [window, win]
    partial[:W] = chain(wins, lambda j: blocks[j, 0] if j < 4 else halo[j - 4, 0], 6, off_a, carry)
    for part in wins:
        part[H:, :] = jnp.where(last, 0.0, part[H:, :])
    ones = jnp.where(r + W == c, 1.0, 0.0).astype(F32)
    carry = jnp.concatenate([jnp.where(leading, window[pl.ds(off_b, W), :], 0.0), ones], 1)
    partial[W:] = chain(wins, lambda j: blocks[j, 1], 4, off_b, carry)
    response[...] = win[pl.ds(off_b, H), :]


def open_join_kernel(partial, other, half):
    core = lax.axis_index("core")
    rows = pl.ds(pl.multiple_of(core * W, W), W)
    front = jnp.where(core == 1, other[...], partial[...])
    back = jnp.where(core == 1, partial[rows, :], other[rows, :])
    own = jnp.concatenate([back[:, :S], jnp.zeros((W, S), F32)], 1)
    value = dot(back[:, S:], front) + own
    for c in range(half.shape[0]):
        half[c] = value


def open_enter_kernel(other, own, swapped, carry, at_chip, out):
    z, core = lax.axis_index("z"), lax.axis_index("core")
    entry = jnp.where(core == 1, other[:, S:], eye(S))
    add = jnp.where(core == 1, other[:, :S], 0.0)
    to_here, to_end = jnp.zeros((S, S), F32), eye(S)
    total = jnp.zeros((2 * S, S), F32)
    for k in reversed(range(CHIPS)):
        low = jnp.where(core == 1, swapped[k], own[k])
        high = jnp.where(core == 1, own[k], swapped[k])
        both = dot(jnp.concatenate([to_here, to_end], 0), jnp.concatenate([low, high], 0))
        total = total + both[:, :S]
        to_here = jnp.where(k == z, entry, both[:S, S:])
        to_end = both[S:, S:]
    carry[...] = total[:S] + add
    at_chip[...] = to_here
    value = jnp.concatenate([total[S:], to_end], 1)
    for x in range(PLANES):
        out[x] = value


def open_finish_kernel(order, offsets, carry, at_chip, crossing, response, window, out):
    x = lax.axis_index("x")
    off_b = offsets[order[1]]
    total = carry[...]
    value = jnp.zeros((S, S), F32)
    for k in reversed(range(PLANES)):
        step = dot(value, crossing[k])
        total = total + step[:, :S]
        value = jnp.where(k == x, at_chip[...], step[:, S:])
    out[...] = window[...]
    rows = pl.ds(off_b, H)
    out[rows, :] = out[rows, :] + dot(response[...], total)


def from_next(block):
    size = lax.axis_size(ROW)
    return lax.ppermute(block, ROW, [(i + 1, i) for i in range(size - 1)])


def from_previous(block):
    size = lax.axis_size(ROW)
    return lax.ppermute(block, ROW, [(i, i + 1) for i in range(size - 1)])


def swap(block):
    return lax.ppermute(block, "core", [(0, 1), (1, 0)])


def local(eigvecs, reflectors, factors, order, offsets):
    columns = eigvecs.shape[1]
    house, tri = reflectors[:, 0], factors[:, 0]
    phases = order.shape[0] // 2
    cols = lax.axis_size("col")

    def gather_blocks(ns, house=house, tri=tri):
        positions = [2 * n + k for n in ns for k in (0, 1)]
        copies = call(
            functools.partial(block_kernel, positions),
            (cols, len(positions), S, S),
            order, house, tri, smem=1,
        )
        return lax.all_to_all(copies, "col", 0, 0)

    def maps_of(ns, blocks):
        halo = from_next(blocks[:2, ::2])
        maps, response = call(
            functools.partial(maps_kernel, ns),
            [(len(ns), S, S), (len(ns), H, S)],
            order, offsets, blocks, halo, smem=2,
            scratch=[pltpu.VMEM((2 * H, S), F32)],
        )
        return halo, maps, response

    def compose(maps):
        count = maps.shape[0]
        theirs = swap(maps)
        copies = call(join_maps_kernel, (CHIPS, count, W, S), maps, theirs)
        own = lax.all_to_all(copies, "z", 0, 0)
        entering, at_chip, whole = call(
            compose_kernel,
            [(count, 2 * S, CHIPS * S), (count, S, S), (PLANES, count, S, S)],
            theirs, own, swap(own),
        )
        whole = lax.all_to_all(whole, "x", 0, 0)
        towards = call(across_kernel, (count, S, PLANES * S), at_chip, whole)
        return theirs, entering, towards

    halo_rows = from_next(eigvecs)
    blocks = gather_blocks([0])
    rest = list(range(1, phases))
    (later_house, later_tri), blocks = lax.optimization_barrier(((house, tri), blocks))
    later_blocks = gather_blocks(rest, later_house, later_tri)
    halo = from_next(blocks[:2, ::2])
    partial, window, response = call(
        open_kernel,
        [(S, 2 * S), (2 * H, columns), (H, S)],
        order, offsets, eigvecs, halo_rows, blocks, halo, smem=2,
        scratch=[pltpu.VMEM((2 * H, S), F32)],
    )
    other = swap(partial)
    own = lax.all_to_all(call(open_join_kernel, (CHIPS, W, 2 * S), partial, other), "z", 0, 0)
    later = maps_of(rest, later_blocks)
    carry, at_chip, out = call(
        open_enter_kernel, [(S, columns), (S, S), (PLANES, S, 2 * S)], other, own, swap(own)
    )
    crossing = lax.all_to_all(out, "x", 0, 0)
    window = call(
        open_finish_kernel, (2 * H, columns),
        order, offsets, carry, at_chip, crossing, response, window, smem=2,
    )
    halo, maps, response = later
    blocks = later_blocks
    theirs, entering, towards = compose(maps)

    for n in rest:
        i = n - 1
        halo_rows = from_next(window[:H])
        partial, window = call(
            functools.partial(values_kernel, n, i),
            [(S, columns), (2 * H, columns)],
            order, offsets, window, halo_rows, blocks, halo, smem=2,
        )
        other = swap(partial)
        half = call(
            functools.partial(join_values_kernel, i), (W, columns), maps, theirs, partial, other
        )
        gathered = lax.all_gather(half, ("z", "core"), axis=0, tiled=True)
        carry, out = call(
            functools.partial(enter_kernel, i),
            [(S, columns), (PLANES, S, columns)],
            entering, gathered, other,
        )
        crossing = lax.all_to_all(out, "x", 0, 0).reshape(PLANES * S, columns)
        window = call(
            functools.partial(finish_kernel, n, i), (2 * H, columns),
            order, offsets, carry, towards, crossing, response, window, smem=2,
        )
    before = from_previous(window[H : H + W])
    return call(
        functools.partial(last_kernel, phases - 1), (H, columns),
        order, offsets, window, before, smem=2,
    )


def solution(mesh):
    torus = Mesh(mesh.devices.reshape(PLANES, CHIPS, 2, mesh.shape["col"]), ROW_COL)
    placed = (P(ROW, "col"), P(None, ROW_COL, None, None), P(None, ROW_COL, None, None), P(), P())
    return jax.shard_map(
        local, mesh=torus, in_specs=placed, out_specs=P(ROW, "col"), check_vma=False
    )
```

time: 861 us -> 283 us (0.33); the launches traced: 851 us -> 281 us
  blocking collectives: 658 us -> 88.6 us
  matrix products: 72.6 us -> 0 us
  Pallas kernels: 0 us -> 52.2 us
  waiting for transfers between devices: 13 us -> 58.5 us
  starting transfers between devices: 20.6 us -> 58.1 us
  between operations: 31.2 us -> 0.41 us
  loops' own time: 21.6 us -> 0 us
  local copies, waits for them, and re-layouts: 33.3 us -> 23.5 us
    all_gather x49 -> x3, blocking collectives: 658 us -> 53.3 us  [local(): gathered = lax.all_gather(half, ('z', 'core'), axis=0, tiled=True)]
    dot_general x336 -> x0, matrix products: 72.6 us -> none  [the longest x136 27.4 us: compose(): jnp.dot(later[0], earlier[1], precision=highest, preferred_element_type=j...]
    pallas_call x0 -> x23, Pallas kernels: none -> 52.2 us  [call(): pl.pallas_call(body, out_shape=shapes[0] if single else shapes, in_specs=...]
    all_to_all x0 -> x3, blocking collectives: none -> 35.3 us  [the longest x2 21.6 us: local(): crossing = lax.all_to_all(out, 'x', 0, 0).reshape(PLANES * S, columns)]
    all_to_all x0 -> x6, starting transfers between devices: none -> 32 us  [the longest x1 8.35 us: local(): lax.all_to_all(call(open_join_kernel, (CHIPS, W, 2 * S), partial, other),...]
    dynamic_update_slice x32 -> x0, local copies, waits for them, and re-layouts: 29.2 us -> none  [advance(): lax.dynamic_update_slice_in_dim(current, reflect(segment, householder, tr...]
    all_to_all x0 -> x6, waiting for transfers between devices: none -> 26.4 us  [the longest x1 23.6 us: compose(): own = lax.all_to_all(copies, 'z', 0, 0)]
    unnamed x8 -> x67, local copies, waits for them, and re-layouts: 0.18 us -> 23.4 us
  transfers between devices with their start and end apart: 9 -> 20, of which waited for: 7 -> 13; matrix products, arithmetic and copies ran while one was open for 0% -> 0% of each run, Pallas kernels for 0% -> 12%
where the time goes in v1:
time: 283 us; the launch traced here: 281 us
  blocking collectives  88.6 us (31%)
  waiting for transfers between devices  58.5 us (21%)
  starting transfers between devices  58.1 us (21%)
  Pallas kernels  52.2 us (18%)
  local copies, waits for them, and re-layouts  23.5 us (8%)
    all_gather x3, blocking collectives, local(): gathered = lax.all_gather(half, ('z', 'core'), axis=0, tiled=True)  53.3 us
    pallas_call x23, Pallas kernels, call(): pl.pallas_call(body, out_shape=shapes[0] if single else shapes, in_specs=...  52.2 us
    all_to_all x1, waiting for transfers between devices, compose(): own = lax.all_to_all(copies, 'z', 0, 0)  23.6 us
    unnamed x67, local copies, waits for them, and re-layouts  23.4 us
    all_to_all x2, blocking collectives, local(): crossing = lax.all_to_all(out, 'x', 0, 0).reshape(PLANES * S, columns)  21.6 us
    ppermute x6, waiting for transfers between devices, from_next(): return lax.ppermute(block, ROW, [(i + 1, i) for i in range(size - 1)])  21.6 us
    ppermute x6, starting transfers between devices, from_next(): return lax.ppermute(block, ROW, [(i + 1, i) for i in range(size - 1)])  18 us
    all_to_all x1, blocking collectives, gather_blocks(): return lax.all_to_all(copies, 'col', 0, 0)  13.7 us
  transfers between devices with their start and end apart: 20, of which 13 were waited for; matrix products, arithmetic and copies ran while one was open for 0% of the time, Pallas kernels for 12%

profile of v1, /device:TPU:2, one launch (start us, length us, event | category | flops | bytes accessed | tf_op | source)
XLA Modules:
  0.0 281.4 jit_solution(8384762917970768831)
XLA Ops:
  0.0 1.2 copy.6
  2.8 1.5 shard_map.55
  4.3 13.7 %all_to_all.45.blocks = f32[4,2,128,128]{3,2,1,0:T(8,128)S(1)} all-to-all(f32[4,2,128,128]{3,2,1,0:T(8,128)S(1)} %shard_map.55), channel_id=1, replica_groups=mesh['x'=4,'z'=8,'core'=2,'col'=4] {'col'}, dimensions={0} | all-to-all | bytes 1048576 | tf_op jit(solution)/shard_map/all_to_all | solution.py:292
  18.1 4.3 %shard_map.56 = f32[4,6,128,128]{3,2,1,0:T(8,128)} custom-call(s32[8]{0:T(128)S(1)} %copy-done.24, f32[8,128,64]{2,1,0:T(8,128)S(1)} %bitcast.6, f32[8,64,64]{2,1,0:T(8,128)S(1)} %bitcast.8), custom_call_target="tpu_custom_call" | custom-call | flops 20000000 | bytes 1000000 | tf_op jit(solution)/shard_map/pallas_call | solution.py:30
  22.4 3.7 %all-to-all-start.1 = ((f32[4,6,128,128]{3,2,1,0:T(8,128)}), f32[4,6,128,128]{3,2,1,0:T(8,128)S(1)}, u32[]{:S(2)}, u32[]{:S(2)}) async-start(f32[4,6,128,128]{3,2,1,0:T(8,128)} %shard_map.56), calls=%async_computation.1 | async-start | bytes 3145728 | tf_op jit(solution)/shard_map/all_to_all | solution.py:292
  26.1 6.0 %collective-permute-start.3 = (f32[256,128]{1,0:T(8,128)S(1)}, f32[256,128]{1,0:T(8,128)S(1)}, u32[]{:S(2)}, u32[]{:S(2)}) collective-permute-start(f32[256,128]{1,0:T(8,128)S(1)} %copy-done.23), channel_id=1, source_target_pairs={{4,0},{8,4},{12,8},{16,12},{20,16},{24,20},{28,24},{32,28},{36,32}... | collective-permute-start | bytes 393224 | tf_op jit(solution)/shard_map/ppermute | solution.py:267
  32.2 3.7 %collective-permute-start.4 = (f32[2,1,128,128]{3,2,1,0:T(8,128)S(1)}, f32[2,1,128,128]{3,2,1,0:T(8,128)S(1)}, u32[]{:S(2)}, u32[]{:S(2)}) collective-permute-start(f32[2,1,128,128]{3,2,1,0:T(8,128)S(1)} %slice.20), channel_id=1, source_target_pairs={{4,0},{8,4},{12,8},{16,12},{20,16},{24,20},{28,24},{32,28},{36,32}... | collective-permute-start | bytes 393224 | tf_op jit(solution)/shard_map/ppermute | solution.py:267
  35.9 2.5 collective-permute-done.4.halo
  38.4 3.9 %shard_map.60 = (f32[128,256]{1,0:T(8,128)S(1)}, f32[512,128]{1,0:T(8,128)S(1)}, f32[256,128]{1,0:T(8,128)S(1)}) custom-call(s32[8]{0:T(128)S(1)} %copy-done.24, s32[8]{0:T(128)S(1)} %copy-done.32, f32[256,128]{1,0:T(8,128)S(1)} %copy-done.23, f32[256,128]{1,0:T(8,128)S(1)} %collective-permute-done.3.halo_rows, f32[4,2,128,128]{3,2,1,0:T(8,128)S(1)} %all_to_all.45.blocks, ...), custom_call_target="tpu_custom_call" | custom-call | flops 20000000 | bytes 1000000 | tf_op jit(solution)/shard_map/pallas_call | solution.py:30
  43.6 1.3 collective-permute-done.5.other
  46.0 8.3 %all-to-all-start.3 = ((f32[8,64,256]{2,1,0:T(8,128)}), f32[8,64,256]{2,1,0:T(8,128)S(1)}, u32[]{:S(2)}, u32[]{:S(2)}) async-start(f32[8,64,256]{2,1,0:T(8,128)} %shard_map.61), calls=%async_computation.3 | async-start | bytes 1048576 | tf_op jit(solution)/shard_map/all_to_all | solution.py:331
  54.4 2.0 collective-permute-start
  56.4 11.6 %collective-permute-done.halo = f32[2,3,128,128]{3,2,1,0:T(8,128)S(1)} collective-permute-done((f32[2,3,128,128]{3,2,1,0:T(8,128)S(1)}, f32[2,3,128,128]{3,2,1,0:T(8,128)S(1)}, u32[]{:S(2)}, u32[]{:S(2)}) %collective-permute-start) | collective-permute-done | bytes 393248 | tf_op jit(solution)/shard_map/ppermute | solution.py:267
  68.0 7.4 %shard_map.57 = (f32[3,128,128]{2,1,0:T(8,128)S(1)}, f32[3,256,128]{2,1,0:T(8,128)S(1)}) custom-call(s32[8]{0:T(128)S(1)} %copy-done.24, s32[8]{0:T(128)S(1)} %copy-done.32, f32[4,6,128,128]{3,2,1,0:T(8,128)S(1)} %all-to-all-done.1.blocks, f32[2,3,128,128]{3,2,1,0:T(8,128)S(1)} %collective-permute-done.halo), custom_call_target="tpu_custom_call" | custom-call | flops 20000000 | bytes 1000000 | tf_op jit(solution)/shard_map/pallas_call | solution.py:30
  75.4 2.1 collective-permute-start.1
  80.7 5.8 %all-to-all-start.2 = ((f32[8,3,64,128]{3,2,1,0:T(8,128)}), f32[8,3,64,128]{3,2,1,0:T(8,128)S(1)}, u32[]{:S(2)}, u32[]{:S(2)}) async-start(f32[8,3,64,128]{3,2,1,0:T(8,128)} %copy-done.5), calls=%async_computation.2 | async-start | bytes 1572864 | tf_op jit(solution)/shard_map/all_to_all | solution.py:308
  86.5 23.6 %all-to-all-done.2.own = f32[8,3,64,128]{3,2,1,0:T(8,128)S(1)} async-done(((f32[8,3,64,128]{3,2,1,0:T(8,128)}), f32[8,3,64,128]{3,2,1,0:T(8,128)S(1)}, u32[]{:S(2)}, u32[]{:S(2)}) %all-to-all-start.2) | async-done | bytes 786464 | tf_op jit(solution)/shard_map/all_to_all | solution.py:308
  112.1 4.8 %shard_map.62 = (f32[128,128]{1,0:T(8,128)S(1)}, f32[128,128]{1,0:T(8,128)S(1)}, f32[4,128,256]{2,1,0:T(8,128)S(1)}) custom-call(f32[128,256]{1,0:T(8,128)S(1)} %copy-done.13, f32[8,64,256]{2,1,0:T(8,128)S(1)} %copy-done.7, f32[8,64,256]{2,1,0:T(8,128)} %collective-permute-done.6.swapped), custom_call_target="tpu_custom_call" | custom-call | flops 20000000 | bytes 1000000 | tf_op jit(solution)/shard_map/pallas_call | solution.py:30
  119.0 4.8 %all-to-all-start.4 = ((f32[4,128,256]{2,1,0:T(8,128)}), f32[4,128,256]{2,1,0:T(8,128)}, u32[]{:S(2)}, u32[]{:S(2)}) async-start(f32[4,128,256]{2,1,0:T(8,128)} %copy-done.11), calls=%async_computation.4 | async-start | bytes 1048576 | tf_op jit(solution)/shard_map/all_to_all | solution.py:336
  123.8 7.4 %shard_map.59 = (f32[3,256,1024]{2,1,0:T(8,128)S(1)}, f32[3,128,128]{2,1,0:T(8,128)S(1)}, f32[4,3,128,128]{3,2,1,0:T(8,128)S(1)}) custom-call(f32[3,128,128]{2,1,0:T(8,128)S(1)} %collective-permute-done.1.theirs, f32[8,3,64,128]{3,2,1,0:T(8,128)S(1)} %all-to-all-done.2.own, f32[8,3,64,128]{3,2,1,0:T(8,128)} %collective-permute-done.2.swapped), custom_call_target="tpu_custom_call" | custom-call | flops 20000000 | bytes 1000000 | tf_op jit(solution)/shard_map/pallas_call | solution.py:30
  131.2 1.6 copy-done
  134.4 4.8 %all-to-all-start.5 = ((f32[4,3,128,128]{3,2,1,0:T(8,128)}), f32[4,3,128,128]{3,2,1,0:T(8,128)S(1)}, u32[]{:S(2)}, u32[]{:S(2)}) async-start(f32[4,3,128,128]{3,2,1,0:T(8,128)} %copy-done.10), calls=%async_computation.5 | async-start | bytes 1572864 | tf_op jit(solution)/shard_map/all_to_all | solution.py:314
  142.8 2.5 shard_map.63.own
  145.3 2.2 collective-permute-start.7
  147.5 2.5 collective-permute-done.7.halo_rows
  150.0 2.9 %shard_map.64 = (f32[128,128]{1,0:T(8,128)S(1)}, f32[512,128]{1,0:T(8,128)S(1)}) custom-call(s32[8]{0:T(128)S(1)} %copy-done.25, s32[8]{0:T(128)S(1)} %copy-done.32, f32[512,128]{1,0:T(8,128)S(1)} %shard_map.63.own, f32[256,128]{1,0:T(8,128)S(1)} %collective-permute-done.7.halo_rows, f32[4,6,128,128]{3,2,1,0:T(8,128)S(1)} %all-to-all-done.1.blocks, ...), custom_call_target="tpu_custom_call" | custom-call | flops 20000000 | bytes 1000000 | tf_op jit(solution)/shard_map/pallas_call | solution.py:30
  153.6 1.3 collective-permute-start.8
  156.0 18.6 %all_gather.9.gathered = f32[1024,128]{1,0:T(8,128)S(1)} all-gather(f32[64,128]{1,0:T(8,128)S(1)} %shard_map.65), channel_id=1, replica_groups=mesh['x'=4,'z'=8,'core'=2,'col'=4] {'z','core'}, dimensions={0}, use_global_device_ids=true | all-gather | bytes 557056 | tf_op jit(solution)/shard_map/all_gather | solution.py:357
  177.9 4.6 %all-to-all-start.6 = ((f32[4,128,128]{2,1,0:T(8,128)}), f32[4,128,128]{2,1,0:T(8,128)}, u32[]{:S(2)}, u32[]{:S(2)}) async-start(f32[4,128,128]{2,1,0:T(8,128)} %copy-done.16), calls=%async_computation.6 | async-start | bytes 524288 | tf_op jit(solution)/shard_map/all_to_all | solution.py:363
  184.5 1.2 shard_map.67.towards
  185.8 2.8 all-to-all-done.6
  190.4 1.7 shard_map.68.own
  192.1 2.2 collective-permute-start.9
  194.3 2.5 collective-permute-done.9.halo_rows
  196.8 2.9 %shard_map.69 = (f32[128,128]{1,0:T(8,128)S(1)}, f32[512,128]{1,0:T(8,128)S(1)}) custom-call(s32[8]{0:T(128)S(1)} %copy-done.25, s32[8]{0:T(128)S(1)} %copy-done.32, f32[512,128]{1,0:T(8,128)S(1)} %shard_map.68.own, f32[256,128]{1,0:T(8,128)S(1)} %collective-permute-done.9.halo_rows, f32[4,6,128,128]{3,2,1,0:T(8,128)S(1)} %all-to-all-done.1.blocks, ...), custom_call_target="tpu_custom_call" | custom-call | flops 20000000 | bytes 1000000 | tf_op jit(solution)/shard_map/pallas_call | solution.py:30
  199.7 1.4 collective-permute-start.10
  202.2 17.1 %all_gather.10.gathered = f32[1024,128]{1,0:T(8,128)S(1)} all-gather(f32[64,128]{1,0:T(8,128)S(1)} %shard_map.70), channel_id=1, replica_groups=mesh['x'=4,'z'=8,'core'=2,'col'=4] {'z','core'}, dimensions={0}, use_global_device_ids=true | all-gather | bytes 557056 | tf_op jit(solution)/shard_map/all_gather | solution.py:357
  220.3 10.9 %all_to_all.46 = f32[4,128,128]{2,1,0:T(8,128)S(1)} all-to-all(f32[4,128,128]{2,1,0:T(8,128)S(1)} %get-tuple-element.51), channel_id=1, replica_groups=mesh['x'=4,'z'=8,'core'=2,'col'=4] {'x'}, dimensions={0} | all-to-all | bytes 524288 | tf_op jit(solution)/shard_map/all_to_all | solution.py:363
  231.3 1.3 shard_map.72.own
  232.6 1.9 collective-permute-start.11
  234.5 2.5 collective-permute-done.11.halo_rows
  237.0 2.9 %shard_map.73 = (f32[128,128]{1,0:T(8,128)S(1)}, f32[512,128]{1,0:T(8,128)S(1)}) custom-call(s32[8]{0:T(128)S(1)} %copy-done.25, s32[8]{0:T(128)S(1)} %copy-done.32, f32[512,128]{1,0:T(8,128)S(1)} %shard_map.72.own, f32[256,128]{1,0:T(8,128)S(1)} %collective-permute-done.11.halo_rows, f32[4,6,128,128]{3,2,1,0:T(8,128)S(1)} %all-to-all-done.1.blocks, ...), custom_call_target="tpu_custom_call" | custom-call | flops 20000000 | bytes 1000000 | tf_op jit(solution)/shard_map/pallas_call | solution.py:30
  242.2 17.6 %all_gather.11.gathered = f32[1024,128]{1,0:T(8,128)S(1)} all-gather(f32[64,128]{1,0:T(8,128)S(1)} %shard_map.74), channel_id=1, replica_groups=mesh['x'=4,'z'=8,'core'=2,'col'=4] {'z','core'}, dimensions={0}, use_global_device_ids=true | all-gather | bytes 557056 | tf_op jit(solution)/shard_map/all_gather | solution.py:357
  260.8 10.7 %all_to_all.47 = f32[4,128,128]{2,1,0:T(8,128)S(1)} all-to-all(f32[4,128,128]{2,1,0:T(8,128)S(1)} %get-tuple-element.55), channel_id=1, replica_groups=mesh['x'=4,'z'=8,'core'=2,'col'=4] {'x'}, dimensions={0} | all-to-all | bytes 524288 | tf_op jit(solution)/shard_map/all_to_all | solution.py:363
  271.5 1.3 shard_map.76.window
  272.8 1.9 collective-permute-start.13
  274.7 5.4 %collective-permute-done.13.before = f32[64,128]{1,0:T(8,128)S(1)} collective-permute-done((f32[64,128]{1,0:T(8,128)S(1)}, f32[64,128]{1,0:T(8,128)S(1)}, u32[]{:S(2)}, u32[]{:S(2)}) %collective-permute-start.13) | collective-permute-done | bytes 32800 | tf_op jit(solution)/shard_map/ppermute | solution.py:272
  280.2 1.2 shard_map.77
  (94 shorter events, 30.8 us)
Async XLA Ops:
  0.0 18.1 %copy-start.9 = (f32[8,1,64,64]{3,2,1,0:T(8,128)S(1)}, f32[8,1,64,64]{3,2,1,0:T(8,128)}, u32[]{:S(2)}) copy-start(f32[8,1,64,64]{3,2,1,0:T(8,128)} %param.7) | copy-start | bytes 393220
  1.2 1.0 copy-start.8
  22.4 3.7 %copy-start.23 = (f32[256,128]{1,0:T(8,128)S(1)}, f32[256,128]{1,0:T(8,128)}, u32[]{:S(2)}) copy-start(f32[256,128]{1,0:T(8,128)} %own.1) | copy-start | bytes 393220
  22.4 16.0 %copy-start.32 = (s32[8]{0:T(128)S(1)}, s32[8]{0:T(128)}, u32[]{:S(2)}) copy-start(s32[8]{0:T(128)} %offsets.19) | copy-start | bytes 100
  22.4 23.6 %all-to-all-start.1 = ((f32[4,6,128,128]{3,2,1,0:T(8,128)}), f32[4,6,128,128]{3,2,1,0:T(8,128)S(1)}, u32[]{:S(2)}, u32[]{:S(2)}) async-start(f32[4,6,128,128]{3,2,1,0:T(8,128)} %shard_map.56), calls=%async_computation.1 | async-start | bytes 3145728 | tf_op jit(solution)/shard_map/all_to_all | solution.py:292
  26.1 9.8 %collective-permute-start.3 = (f32[256,128]{1,0:T(8,128)S(1)}, f32[256,128]{1,0:T(8,128)S(1)}, u32[]{:S(2)}, u32[]{:S(2)}) collective-permute-start(f32[256,128]{1,0:T(8,128)S(1)} %copy-done.23), channel_id=1, source_target_pairs={{4,0},{8,4},{12,8},{16,12},{20,16},{24,20},{28,24},{32,28},{36,32}... | collective-permute-start | bytes 393224 | tf_op jit(solution)/shard_map/ppermute | solution.py:267
  32.2 6.2 %collective-permute-start.4 = (f32[2,1,128,128]{3,2,1,0:T(8,128)S(1)}, f32[2,1,128,128]{3,2,1,0:T(8,128)S(1)}, u32[]{:S(2)}, u32[]{:S(2)}) collective-permute-start(f32[2,1,128,128]{3,2,1,0:T(8,128)S(1)} %slice.20), channel_id=1, source_target_pairs={{4,0},{8,4},{12,8},{16,12},{20,16},{24,20},{28,24},{32,28},{36,32}... | collective-permute-start | bytes 393224 | tf_op jit(solution)/shard_map/ppermute | solution.py:267
  42.3 0.7 copy-start.17
  43.6 1.3 collective-permute-start.5
  45.0 9.4 %copy-start.12 = (f32[128,256]{1,0:T(8,128)}, f32[128,256]{1,0:T(8,128)S(1)}, u32[]{:S(2)}) copy-start(f32[128,256]{1,0:T(8,128)S(1)} %collective-permute-done.5.other) | copy-start | bytes 393220
  46.0 33.8 %all-to-all-start.3 = ((f32[8,64,256]{2,1,0:T(8,128)}), f32[8,64,256]{2,1,0:T(8,128)S(1)}, u32[]{:S(2)}, u32[]{:S(2)}) async-start(f32[8,64,256]{2,1,0:T(8,128)} %shard_map.61), calls=%async_computation.3 | async-start | bytes 1048576 | tf_op jit(solution)/shard_map/all_to_all | solution.py:331
  54.4 13.6 %collective-permute-start = (f32[2,3,128,128]{3,2,1,0:T(8,128)S(1)}, f32[2,3,128,128]{3,2,1,0:T(8,128)S(1)}, u32[]{:S(2)}, u32[]{:S(2)}) collective-permute-start(f32[2,3,128,128]{3,2,1,0:T(8,128)S(1)} %slice.19), channel_id=1, source_target_pairs={{4,0},{8,4},{12,8},{16,12},{20,16},{24,20},{28,24},{32,28},{36,32}... | collective-permute-start | bytes 1179656 | tf_op jit(solution)/shard_map/ppermute | solution.py:267
  75.4 3.2 %collective-permute-start.1 = (f32[3,128,128]{2,1,0:T(8,128)S(1)}, f32[3,128,128]{2,1,0:T(8,128)S(1)}, u32[]{:S(2)}, u32[]{:S(2)}) collective-permute-start(f32[3,128,128]{2,1,0:T(8,128)S(1)} %get-tuple-element.33.mine), channel_id=1, source_target_pairs={{0,4},{4,0},{1,5},{5,1},{2,6},{6,2},{3,7},{7,3},{8,12},{12,8},{9,1... | collective-permute-start | bytes 589832 | tf_op jit(solution)/shard_map/ppermute | solution.py:276
  78.9 0.9 copy-start.5
  79.8 0.8 copy-start.6
  80.7 29.4 %all-to-all-start.2 = ((f32[8,3,64,128]{3,2,1,0:T(8,128)}), f32[8,3,64,128]{3,2,1,0:T(8,128)S(1)}, u32[]{:S(2)}, u32[]{:S(2)}) async-start(f32[8,3,64,128]{3,2,1,0:T(8,128)} %copy-done.5), calls=%async_computation.2 | async-start | bytes 1572864 | tf_op jit(solution)/shard_map/all_to_all | solution.py:308
  86.4 23.7 %collective-permute-start.6 = (f32[8,64,256]{2,1,0:T(8,128)}, f32[8,64,256]{2,1,0:T(8,128)}, u32[]{:S(2)}, u32[]{:S(2)}) collective-permute-start(f32[8,64,256]{2,1,0:T(8,128)} %copy-done.6), channel_id=1, source_target_pairs={{0,4},{4,0},{1,5},{5,1},{2,6},{6,2},{3,7},{7,3},{8,12},{12,8},{9,1... | collective-permute-start | bytes 1572872 | tf_op jit(solution)/shard_map/ppermute | solution.py:276
  110.1 13.7 %collective-permute-start.2 = (f32[8,3,64,128]{3,2,1,0:T(8,128)S(1)}, f32[8,3,64,128]{3,2,1,0:T(8,128)}, u32[]{:S(2)}, u32[]{:S(2)}) collective-permute-start(f32[8,3,64,128]{3,2,1,0:T(8,128)S(1)} %all-to-all-done.2.own), channel_id=1, source_target_pairs={{0,4},{4,0},{1,5},{5,1},{2,6},{6,2},{3,7},{7,3},{8,12},{12,8},{9,1... | collective-permute-start | bytes 2359304 | tf_op jit(solution)/shard_map/ppermute | solution.py:276
  110.1 1.0 copy-start.7
  111.2 0.9 copy-start.13
  116.9 0.8 copy-start.11
  119.0 15.5 %all-to-all-start.4 = ((f32[4,128,256]{2,1,0:T(8,128)}), f32[4,128,256]{2,1,0:T(8,128)}, u32[]{:S(2)}, u32[]{:S(2)}) async-start(f32[4,128,256]{2,1,0:T(8,128)} %copy-done.11), calls=%async_computation.4 | async-start | bytes 1048576 | tf_op jit(solution)/shard_map/all_to_all | solution.py:336
  123.8 15.5 %copy-start.25 = (s32[8]{0:T(128)S(1)}, s32[8]{0:T(128)}, u32[]{:S(2)}) copy-start(s32[8]{0:T(128)} %order.23) | copy-start | bytes 100
  131.2 1.6 copy-start
  132.9 0.9 copy-start.10
  133.7 0.7 copy-start.19
  134.4 42.6 %all-to-all-start.5 = ((f32[4,3,128,128]{3,2,1,0:T(8,128)}), f32[4,3,128,128]{3,2,1,0:T(8,128)S(1)}, u32[]{:S(2)}, u32[]{:S(2)}) async-start(f32[4,3,128,128]{3,2,1,0:T(8,128)} %copy-done.10), calls=%async_computation.5 | async-start | bytes 1572864 | tf_op jit(solution)/shard_map/all_to_all | solution.py:314
  139.2 1.0 copy-start.18
  140.2 0.9 copy-start.22
  141.1 0.8 copy-start.27
  141.9 0.8 copy-start.29
  145.3 29.3 %copy-start.1 = (f32[3,256,1024]{2,1,0:T(8,128)S(1)}, f32[3,256,1024]{2,1,0:T(8,128)}, u32[]{:S(2)}) copy-start(f32[3,256,1024]{2,1,0:T(8,128)} %copy-done) | copy-start | bytes 9437188
  145.3 4.7 %collective-permute-start.7 = (f32[256,128]{1,0:T(8,128)S(1)}, f32[256,128]{1,0:T(8,128)S(1)}, u32[]{:S(2)}, u32[]{:S(2)}) collective-permute-start(f32[256,128]{1,0:T(8,128)S(1)} %slice.25), channel_id=1, source_target_pairs={{4,0},{8,4},{12,8},{16,12},{20,16},{24,20},{28,24},{32,28},{36,32}... | collective-permute-start | bytes 393224 | tf_op jit(solution)/shard_map/ppermute | solution.py:267
  152.9 0.7 copy-start.14
  153.6 2.2 collective-permute-start.8
  175.7 0.7 copy-start.16
  177.0 0.9 copy-start.3
  177.9 10.7 %all-to-all-start.6 = ((f32[4,128,128]{2,1,0:T(8,128)}), f32[4,128,128]{2,1,0:T(8,128)}, u32[]{:S(2)}, u32[]{:S(2)}) async-start(f32[4,128,128]{2,1,0:T(8,128)} %copy-done.16), calls=%async_computation.6 | async-start | bytes 524288 | tf_op jit(solution)/shard_map/all_to_all | solution.py:363
  182.5 1.1 copy-start.4
  183.6 0.9 copy-start.20
  188.6 1.0 copy-start.15
  189.5 0.8 copy-start.31
  192.1 27.2 %copy-start.2 = (f32[3,256,1024]{2,1,0:T(8,128)S(1)}, f32[3,256,1024]{2,1,0:T(8,128)}, u32[]{:S(2)}) copy-start(f32[3,256,1024]{2,1,0:T(8,128)} %copy-done) | copy-start | bytes 9437188
  192.1 4.7 %collective-permute-start.9 = (f32[256,128]{1,0:T(8,128)S(1)}, f32[256,128]{1,0:T(8,128)S(1)}, u32[]{:S(2)}, u32[]{:S(2)}) collective-permute-start(f32[256,128]{1,0:T(8,128)S(1)} %slice.26), channel_id=1, source_target_pairs={{4,0},{8,4},{12,8},{16,12},{20,16},{24,20},{28,24},{32,28},{36,32}... | collective-permute-start | bytes 393224 | tf_op jit(solution)/shard_map/ppermute | solution.py:267
  199.7 2.3 collective-permute-start.10
  232.6 4.4 %collective-permute-start.11 = (f32[256,128]{1,0:T(8,128)S(1)}, f32[256,128]{1,0:T(8,128)S(1)}, u32[]{:S(2)}, u32[]{:S(2)}) collective-permute-start(f32[256,128]{1,0:T(8,128)S(1)} %slice.27), channel_id=1, source_target_pairs={{4,0},{8,4},{12,8},{16,12},{20,16},{24,20},{28,24},{32,28},{36,32}... | collective-permute-start | bytes 393224 | tf_op jit(solution)/shard_map/ppermute | solution.py:267
  239.9 2.1 collective-permute-start.12
  272.8 7.3 %collective-permute-start.13 = (f32[64,128]{1,0:T(8,128)S(1)}, f32[64,128]{1,0:T(8,128)S(1)}, u32[]{:S(2)}, u32[]{:S(2)}) collective-permute-start(f32[64,128]{1,0:T(8,128)S(1)} %slice.28), channel_id=1, source_target_pairs={{0,4},{4,8},{8,12},{12,16},{16,20},{20,24},{24,28},{28,32},{32,36}... | collective-permute-start | bytes 98312 | tf_op jit(solution)/shard_map/ppermute | solution.py:272
  (5 other events, 3.2 us)

commit v2 on v0

v2 whole, which is shorter than its diff:
```python
import functools

import jax
import jax.numpy as jnp
from jax import lax
from jax.experimental import pallas as pl
from jax.experimental.pallas import tpu as pltpu
from jax.sharding import Mesh
from jax.sharding import PartitionSpec as P

ROW = ("x", "z", "core")
ROW_COL = ("x", "z", "core", "col")
W = 64
S = 2 * W
H = 4 * W
CHIPS, PLANES = 8, 4
SHARE = (S + S - W // 2) // 2
F32 = jnp.float32


def exact(a, b, dims=(((1,), (0,)), ((), ()))):
    return lax.dot_general(a, b, dims, precision=lax.Precision.HIGHEST, preferred_element_type=F32)


def halves(a):
    high = a.astype(jnp.bfloat16)
    return high, (a - high.astype(F32)).astype(jnp.bfloat16)


def dot(a, b):
    a_high, a_low = halves(a)
    b_high, b_low = halves(b)
    return jnp.dot(
        jnp.concatenate([a_high, a_high, a_low], 1),
        jnp.concatenate([b_high, b_low, b_high], 0),
        preferred_element_type=F32,
    )


def call(body, outs, *args, smem=0, scratch=(), flops=20_000_000):
    spaces = [pl.BlockSpec(memory_space=pltpu.SMEM)] * smem
    spaces += [pl.BlockSpec(memory_space=pltpu.VMEM)] * (len(args) - smem)
    single = not isinstance(outs, list)
    shapes = [jax.ShapeDtypeStruct(o, F32) for o in ([outs] if single else outs)]
    specs = [pl.BlockSpec(memory_space=pltpu.VMEM)] * len(shapes)
    return pl.pallas_call(
        body,
        out_shape=shapes[0] if single else shapes,
        in_specs=spaces,
        out_specs=specs[0] if single else specs,
        scratch_shapes=list(scratch),
        cost_estimate=pl.CostEstimate(flops=flops, bytes_accessed=1_000_000, transcendentals=0),
        compiler_params=pltpu.CompilerParams(vmem_limit_bytes=32 * 1024 * 1024),
    )(*args)


def eye(n):
    r = lax.broadcasted_iota(jnp.int32, (n, n), 0)
    c = lax.broadcasted_iota(jnp.int32, (n, n), 1)
    return jnp.where(r == c, 1.0, 0.0).astype(F32)


def row_index():
    x, z, core = lax.axis_index("x"), lax.axis_index("z"), lax.axis_index("core")
    return (x * CHIPS + z) * 2 + core


def is_last(g):
    return g == PLANES * CHIPS * 2 - 1


def block_kernel(positions, order, house, tri, out):
    for i, p in enumerate(positions):
        v = house[order[p], 0]
        t = tri[order[p], 0]
        h = eye(S) - exact(v, exact(t, v, (((1,), (1,)), ((), ()))))
        if len(out.shape) == 4:
            for c in range(out.shape[0]):
                out[c, i] = h
        else:
            out[i] = h


def pick_kernel(part0, part1, part2, part3, blocks, head):
    parts = (part0, part1, part2, part3)
    for j in range(4):
        back = lax.rem(lax.axis_index("col") + 4 - j, 4)
        for i in range(part0.shape[0]):
            block = part0[i]
            for k in (1, 2, 3):
                block = jnp.where(back == k, parts[k][i], block)
            blocks[j, i] = block
            if j < 2 and i % 2 == 0:
                head[j, i // 2] = block


def chain(wins, blocks, count, offset, carry):
    kept = carry
    for j in range(count):
        rest = [win[pl.ds(offset + (j + 1) * W, W), :] for win in wins]
        out = dot(blocks(j), jnp.concatenate([carry, jnp.concatenate(rest, 1)], 0))
        for k, win in enumerate(wins):
            win[pl.ds(offset + j * W, W), :] = out[:W, k * S : (k + 1) * S]
        carry = out[W:]
        if j == 3:
            kept = carry
    return kept


def phase_kernel(n, i, order, offsets, own, halo_rows, blocks, halo, partial, window, response, win):
    g = row_index()
    last, leading = is_last(g), g == 0
    off_a, off_b = offsets[order[2 * n]], offsets[order[2 * n + 1]]
    win[...] = jnp.zeros_like(win)
    window[:H, :] = own[:H, :]
    if n:
        before = offsets[order[2 * n - 1]]
        rows = lax.broadcasted_iota(jnp.int32, (H, 1), 0)
        window[H:, :] = jnp.where((rows < before) & ~last, own[H:, :], halo_rows[...])
    else:
        window[H:, :] = halo_rows[...]
    r = lax.broadcasted_iota(jnp.int32, (W, S), 0)
    c = lax.broadcasted_iota(jnp.int32, (W, S), 1)
    wins = [window, win]

    def first(j):
        return blocks[j, 2 * i] if j < 4 else halo[j - 4, i]

    def second(j):
        return blocks[j, 2 * i + 1]

    ones = jnp.where(r == c, 1.0, 0.0).astype(F32)
    carry = jnp.concatenate([jnp.where(leading, window[pl.ds(off_a, W), :], 0.0), ones], 1)
    partial[:W] = chain(wins, first, 6, off_a, carry)
    for part in wins:
        part[H:, :] = jnp.where(last, 0.0, part[H:, :])
    ones = jnp.where(r + W == c, 1.0, 0.0).astype(F32)
    carry = jnp.concatenate([jnp.where(leading, window[pl.ds(off_b, W), :], 0.0), ones], 1)
    partial[W:] = chain(wins, second, 4, off_b, carry)
    response[...] = win[pl.ds(off_b, H), :]


def packed(step):
    return jnp.concatenate([step[:W // 2, :W], step[W // 2 : W, :W]], 1)


def unpacked(top, bottom):
    square = jnp.concatenate([top[:, :W], top[:, W:]], 0)
    return jnp.concatenate([jnp.concatenate([square, jnp.zeros_like(square)], 1), bottom], 0)


CUT = SHARE - W // 2


def join_kernel(partial, other, share):
    upper = lax.axis_index("core") == 1
    front = jnp.where(upper, other[...], partial[...])
    back = jnp.where(upper, partial[...], other[...])
    value = dot(back[:, S:], front)
    rows, step = value[:, :S] + back[:, :S], value[:, S:]
    low = jnp.concatenate([packed(step), rows[:CUT]], 0)
    high = jnp.concatenate([step[W:], rows[CUT:]], 0)
    share[...] = jnp.where(upper, high, low)


def enter_kernel(other, shares, carry, at_chip, out):
    z, upper = lax.axis_index("z"), lax.axis_index("core") == 1
    entry = jnp.where(upper, other[:, S:], eye(S))
    add = jnp.where(upper, other[:, :S], 0.0)
    to_here, to_end = jnp.zeros((S, S), F32), eye(S)
    total = jnp.zeros((2 * S, S), F32)
    for k in reversed(range(CHIPS)):
        low = shares[2 * k * SHARE : (2 * k + 1) * SHARE]
        high = shares[(2 * k + 1) * SHARE : (2 * k + 2) * SHARE]
        step = unpacked(low[: W // 2], high[:W])
        rows = jnp.concatenate([low[W // 2 :], high[W:]], 0)
        both = dot(jnp.concatenate([to_here, to_end], 0), jnp.concatenate([rows, step], 1))
        total = total + both[:, :S]
        to_here = jnp.where(k == z, entry, both[:S, S:])
        to_end = both[S:, S:]
    carry[...] = total[:S] + add
    at_chip[...] = to_here
    value = jnp.concatenate([total[S:], packed(to_end), to_end[W:]], 0)
    for x in range(PLANES):
        out[x] = value


def finish_kernel(n, order, offsets, carry, at_chip, crossing, response, window, out):
    x = lax.axis_index("x")
    off_b = offsets[order[2 * n + 1]]
    total = carry[...]
    value = jnp.zeros((S, S), F32)
    for k in reversed(range(PLANES)):
        step = unpacked(crossing[k, S : S + W // 2], crossing[k, S + W // 2 :])
        both = dot(value, jnp.concatenate([crossing[k, :S], step], 1))
        total = total + both[:, :S]
        value = jnp.where(k == x, at_chip[...], both[:, S:])
    out[...] = window[...]
    rows = pl.ds(off_b, H)
    out[rows, :] = out[rows, :] + dot(response[...], total)


def last_kernel(n, order, offsets, window, before, out):
    g = row_index()
    off_b = offsets[order[2 * n + 1]]
    rows = lax.broadcasted_iota(jnp.int32, (W, 1), 0)
    out[...] = window[:H, :]
    out[:W, :] = jnp.where((rows < off_b) & (g != 0), before[...], window[:W, :])


def from_next(block):
    size = lax.axis_size(ROW)
    return lax.ppermute(block, ROW, [(i + 1, i) for i in range(size - 1)])


def from_previous(block):
    size = lax.axis_size(ROW)
    return lax.ppermute(block, ROW, [(i, i + 1) for i in range(size - 1)])


def swap(block):
    return lax.ppermute(block, "core", [(0, 1), (1, 0)])


def local(eigvecs, reflectors, factors, order, offsets):
    columns = eigvecs.shape[1]
    phases = order.shape[0] // 2
    cols = lax.axis_size("col")

    halo_rows = from_next(eigvecs)
    block = call(
        functools.partial(block_kernel, [0, 1]), (cols, 2, S, S), order, reflectors, factors, smem=1
    )
    blocks = lax.all_to_all(block, "col", 0, 0)
    later = call(
        functools.partial(block_kernel, list(range(2, 2 * phases))),
        (2 * phases - 2, S, S),
        order, reflectors, factors, smem=1,
    )
    halo = from_next(blocks[:2, ::2])
    later, halo, halo_rows = lax.optimization_barrier((later, halo, halo_rows))
    parts = [later] + [
        lax.ppermute(later, "col", [(c, (c + d) % cols) for c in range(cols)]) for d in (1, 2, 3)
    ]
    window = eigvecs
    for n in range(phases):
        partial, window, response = call(
            functools.partial(phase_kernel, n, max(n - 1, 0)),
            [(S, 2 * S), (2 * H, columns), (H, S)],
            order, offsets, window, halo_rows, blocks, halo, smem=2,
            scratch=[pltpu.VMEM((2 * H, S), F32)],
        )
        other = swap(partial)
        share = call(join_kernel, (SHARE, columns), partial, other)
        shares = lax.all_gather(share, ("z", "core"), axis=0, tiled=True)
        carry, at_chip, out = call(
            enter_kernel,
            [(S, columns), (S, S), (PLANES, 2 * SHARE, S)],
            other, shares,
        )
        crossing = lax.all_to_all(out, "x", 0, 0)
        if n == 0:
            crossing, parts = lax.optimization_barrier((crossing, parts))
            blocks, head = call(
                pick_kernel,
                [(cols, 2 * phases - 2, S, S), (2, phases - 1, S, S)],
                *parts,
            )
            halo = from_next(head)
        window = call(
            functools.partial(finish_kernel, n), (2 * H, columns),
            order, offsets, carry, at_chip, crossing, response, window, smem=2,
        )
        if n < phases - 1:
            halo_rows = from_next(window[:H])
    before = from_previous(window[H : H + W])
    return call(
        functools.partial(last_kernel, phases - 1), (H, columns),
        order, offsets, window, before, smem=2,
    )


def solution(mesh):
    torus = Mesh(mesh.devices.reshape(PLANES, CHIPS, 2, mesh.shape["col"]), ROW_COL)
    placed = (P(ROW, "col"), P(None, ROW_COL, None, None), P(None, ROW_COL, None, None), P(), P())
    return jax.shard_map(
        local, mesh=torus, in_specs=placed, out_specs=P(ROW, "col"), check_vma=False
    )
```

time: 861 us -> 216 us (0.25); the launches traced: 851 us -> 215 us
  blocking collectives: 658 us -> 115 us
  matrix products: 72.6 us -> 0 us
  Pallas kernels: 0 us -> 32.2 us
  between operations: 31.2 us -> 0.26 us
  local copies, waits for them, and re-layouts: 33.3 us -> 2.87 us
  loops' own time: 21.6 us -> 0 us
  starting transfers between devices: 20.6 us -> 38.3 us
  waiting for transfers between devices: 13 us -> 26.8 us
    all_gather x49 -> x4, blocking collectives: 658 us -> 76.5 us  [local(): shares = lax.all_gather(share, ('z', 'core'), axis=0, tiled=True)]
    dot_general x336 -> x0, matrix products: 72.6 us -> none  [the longest x136 27.4 us: compose(): jnp.dot(later[0], earlier[1], precision=highest, preferred_element_type=j...]
    all_to_all x0 -> x3, blocking collectives: none -> 38.2 us  [local(): crossing = lax.all_to_all(out, 'x', 0, 0)]
    pallas_call x0 -> x20, Pallas kernels: none -> 32.2 us  [call(): pl.pallas_call(body, out_shape=shapes[0] if single else shapes, in_specs=...]
    dynamic_update_slice x32 -> x0, local copies, waits for them, and re-layouts: 29.2 us -> none  [advance(): lax.dynamic_update_slice_in_dim(current, reflect(segment, householder, tr...]
    another operation x8 -> x0, loops' own time: 21.6 us -> none  [sweep_apply(): return lax.fori_loop(0, house_set.shape[0], advance, extended)]
    all_to_all x0 -> x2, waiting for transfers between devices: none -> 10.4 us  [the longest x1 7.82 us: local(): crossing = lax.all_to_all(out, 'x', 0, 0)]
    all_to_all x0 -> x2, starting transfers between devices: none -> 9.43 us  [the longest x1 4.83 us: local(): crossing = lax.all_to_all(out, 'x', 0, 0)]
  transfers between devices with their start and end apart: 9 -> 16, of which waited for: 7 -> 9; matrix products, arithmetic and copies ran while one was open for 0% -> 0% of each run, Pallas kernels for 0% -> 3%
where the time goes in v2:
time: 216 us; the launch traced here: 215 us
  blocking collectives  115 us (53%)
  starting transfers between devices  38.3 us (18%)
  Pallas kernels  32.2 us (15%)
  waiting for transfers between devices  26.8 us (12%)
  local copies, waits for them, and re-layouts  2.87 us (1%)
    all_gather x4, blocking collectives, local(): shares = lax.all_gather(share, ('z', 'core'), axis=0, tiled=True)  76.5 us
    all_to_all x3, blocking collectives, local(): crossing = lax.all_to_all(out, 'x', 0, 0)  38.2 us
    pallas_call x20, Pallas kernels, call(): pl.pallas_call(body, out_shape=shapes[0] if single else shapes, in_specs=...  32.2 us
    ppermute x6, starting transfers between devices, from_next(): return lax.ppermute(block, ROW, [(i + 1, i) for i in range(size - 1)])  20.5 us
    ppermute x6, waiting for transfers between devices, from_next(): return lax.ppermute(block, ROW, [(i + 1, i) for i in range(size - 1)])  8.05 us
    all_to_all x1, waiting for transfers between devices, local(): crossing = lax.all_to_all(out, 'x', 0, 0)  7.82 us
    ppermute x1, waiting for transfers between devices, from_previous(): return lax.ppermute(block, ROW, [(i, i + 1) for i in range(size - 1)])  5.41 us
    all_to_all x1, starting transfers between devices, local(): crossing = lax.all_to_all(out, 'x', 0, 0)  4.83 us
  transfers between devices with their start and end apart: 16, of which 9 were waited for; matrix products, arithmetic and copies ran while one was open for 0% of the time, Pallas kernels for 3%

profile of v2, /device:TPU:2, one launch (start us, length us, event | category | flops | bytes accessed | tf_op | source)
XLA Modules:
  0.0 215.1 jit_solution(12942751312239526276)
XLA Ops:
  0.0 1.2 copy.6.house
  1.2 0.9 copy-done
  2.2 0.7 copy-done.3
  2.8 2.3 %shard_map.56 = f32[4,2,128,128]{3,2,1,0:T(8,128)} custom-call(s32[8]{0:T(128)S(1)} %copy-done.3, f32[8,1,128,64]{3,2,1,0:T(8,128)S(1)} %copy.6.house, f32[8,1,64,64]{3,2,1,0:T(8,128)S(1)} %copy-done), custom_call_target="tpu_custom_call" | custom-call | flops 20000000 | bytes 1000000 | tf_op jit(solution)/shard_map/pallas_call | solution.py:46
  5.1 4.6 %all-to-all-start = ((f32[4,2,128,128]{3,2,1,0:T(8,128)}), f32[4,2,128,128]{3,2,1,0:T(8,128)S(1)}, u32[]{:S(2)}, u32[]{:S(2)}) async-start(f32[4,2,128,128]{3,2,1,0:T(8,128)} %shard_map.56), calls=%async_computation | async-start | bytes 1048576 | tf_op jit(solution)/shard_map/all_to_all | solution.py:234
  9.7 6.9 %collective-permute-start.1 = (f32[256,128]{1,0:T(8,128)S(1)}, f32[256,128]{1,0:T(8,128)S(1)}, u32[]{:S(2)}, u32[]{:S(2)}) collective-permute-start(f32[256,128]{1,0:T(8,128)S(1)} %copy-done.2), channel_id=1, source_target_pairs={{4,0},{8,4},{12,8},{16,12},{20,16},{24,20},{28,24},{32,28},{36,32}... | collective-permute-start | bytes 393224 | tf_op jit(solution)/shard_map/ppermute | solution.py:213
  16.6 2.6 %all-to-all-done.blocks = f32[4,2,128,128]{3,2,1,0:T(8,128)S(1)} async-done(((f32[4,2,128,128]{3,2,1,0:T(8,128)}), f32[4,2,128,128]{3,2,1,0:T(8,128)S(1)}, u32[]{:S(2)}, u32[]{:S(2)}) %all-to-all-start) | async-done | bytes 524320 | tf_op jit(solution)/shard_map/all_to_all | solution.py:234
  19.2 5.7 %collective-permute-start = (f32[2,1,128,128]{3,2,1,0:T(8,128)S(1)}, f32[2,1,128,128]{3,2,1,0:T(8,128)S(1)}, u32[]{:S(2)}, u32[]{:S(2)}) collective-permute-start(f32[2,1,128,128]{3,2,1,0:T(8,128)S(1)} %slice.21), channel_id=1, source_target_pairs={{4,0},{8,4},{12,8},{16,12},{20,16},{24,20},{28,24},{32,28},{36,32}... | collective-permute-start | bytes 393224 | tf_op jit(solution)/shard_map/ppermute | solution.py:213
  25.0 3.1 %shard_map.55.part0 = f32[6,128,128]{2,1,0:T(8,128)S(1)} custom-call(s32[8]{0:T(128)S(1)} %copy-done.4, f32[8,1,128,64]{3,2,1,0:T(8,128)S(1)} %copy.6.house, f32[8,1,64,64]{3,2,1,0:T(8,128)S(1)} %copy-done.1), custom_call_target="tpu_custom_call" | custom-call | flops 20000000 | bytes 1000000 | tf_op jit(solution)/shard_map/pallas_call | solution.py:46
  28.2 2.7 %shard_map.57 = (f32[128,256]{1,0:T(8,128)S(1)}, f32[512,128]{1,0:T(8,128)S(1)}, f32[256,128]{1,0:T(8,128)S(1)}) custom-call(s32[8]{0:T(128)S(1)} %copy-done.4, s32[8]{0:T(128)S(1)} %copy-done.5, f32[256,128]{1,0:T(8,128)S(1)} %copy-done.2, f32[256,128]{1,0:T(8,128)S(1)} %collective-permute-done.1.halo_rows, f32[4,2,128,128]{3,2,1,0:T(8,128)S(1)} %all-to-all-done.blocks, ...), custom_call_target="tpu_custom_call" | custom-call | flops 20000000 | bytes 1000000 | tf_op jit(solution)/shard_map/pallas_call | solution.py:46
  31.0 1.2 collective-permute-start.5
  32.2 1.5 collective-permute-start.4
  33.9 20.2 %all_gather.12.shares = f32[1792,128]{1,0:T(8,128)S(1)} all-gather(f32[112,128]{1,0:T(8,128)S(1)} %shard_map.58), channel_id=1, replica_groups=mesh['x'=4,'z'=8,'core'=2,'col'=4] {'z','core'}, dimensions={0}, use_global_device_ids=true | all-gather | bytes 974848 | tf_op jit(solution)/shard_map/all_gather | solution.py:255
  54.2 2.5 %shard_map.59 = (f32[128,128]{1,0:T(8,128)S(1)}, f32[128,128]{1,0:T(8,128)S(1)}, f32[4,224,128]{2,1,0:T(8,128)}) custom-call(f32[128,256]{1,0:T(8,128)S(1)} %collective-permute-done.2.other, f32[1792,128]{1,0:T(8,128)S(1)} %all_gather.12.shares), custom_call_target="tpu_custom_call" | custom-call | flops 20000000 | bytes 1000000 | tf_op jit(solution)/shard_map/pallas_call | solution.py:46
  56.7 4.8 %all-to-all-start.1 = ((f32[4,224,128]{2,1,0:T(8,128)}), f32[4,224,128]{2,1,0:T(8,128)S(1)}, u32[]{:S(2)}, u32[]{:S(2)}) async-start(f32[4,224,128]{2,1,0:T(8,128)} %get-tuple-element.44), calls=%async_computation.1 | async-start | bytes 917504 | tf_op jit(solution)/shard_map/all_to_all | solution.py:261
  61.5 7.8 %all-to-all-done.1.crossing = f32[4,224,128]{2,1,0:T(8,128)S(1)} async-done(((f32[4,224,128]{2,1,0:T(8,128)}), f32[4,224,128]{2,1,0:T(8,128)S(1)}, u32[]{:S(2)}, u32[]{:S(2)}) %all-to-all-start.1) | async-done | bytes 458784 | tf_op jit(solution)/shard_map/all_to_all | solution.py:261
  69.6 1.9 collective-permute-start.7
  71.5 1.5 shard_map.60.own
  73.0 2.1 collective-permute-start.6
  75.2 3.0 %collective-permute-done.6.halo_rows = f32[256,128]{1,0:T(8,128)S(1)} collective-permute-done((f32[256,128]{1,0:T(8,128)S(1)}, f32[256,128]{1,0:T(8,128)S(1)}, u32[]{:S(2)}, u32[]{:S(2)}) %collective-permute-start.6) | collective-permute-done | bytes 131104 | tf_op jit(solution)/shard_map/ppermute | solution.py:213
  78.2 2.7 %shard_map.62 = (f32[128,256]{1,0:T(8,128)S(1)}, f32[512,128]{1,0:T(8,128)S(1)}, f32[256,128]{1,0:T(8,128)S(1)}) custom-call(s32[8]{0:T(128)S(1)} %copy-done.4, s32[8]{0:T(128)S(1)} %copy-done.5, f32[512,128]{1,0:T(8,128)S(1)} %shard_map.60.own, f32[256,128]{1,0:T(8,128)S(1)} %collective-permute-done.6.halo_rows, ...), custom_call_target="tpu_custom_call" | custom-call | flops 20000000 | bytes 1000000 | tf_op jit(solution)/shard_map/pallas_call | solution.py:46
  80.9 1.7 collective-permute-start.8
  82.6 1.0 collective-permute-done.8.other
  83.9 18.0 %all_gather.13.shares = f32[1792,128]{1,0:T(8,128)S(1)} all-gather(f32[112,128]{1,0:T(8,128)S(1)} %shard_map.63), channel_id=1, replica_groups=mesh['x'=4,'z'=8,'core'=2,'col'=4] {'z','core'}, dimensions={0}, use_global_device_ids=true | all-gather | bytes 974848 | tf_op jit(solution)/shard_map/all_gather | solution.py:255
  101.8 1.7 shard_map.64
  103.5 13.0 %all_to_all.25.crossing = f32[4,224,128]{2,1,0:T(8,128)S(1)} all-to-all(f32[4,224,128]{2,1,0:T(8,128)S(1)} %get-tuple-element.58), channel_id=1, replica_groups=mesh['x'=4,'z'=8,'core'=2,'col'=4] {'x'}, dimensions={0} | all-to-all | bytes 917504 | tf_op jit(solution)/shard_map/all_to_all | solution.py:261
  116.5 1.5 shard_map.65.own
  118.0 1.9 collective-permute-start.9
  120.0 2.5 %collective-permute-done.9.halo_rows = f32[256,128]{1,0:T(8,128)S(1)} collective-permute-done((f32[256,128]{1,0:T(8,128)S(1)}, f32[256,128]{1,0:T(8,128)S(1)}, u32[]{:S(2)}, u32[]{:S(2)}) %collective-permute-start.9) | collective-permute-done | bytes 131104 | tf_op jit(solution)/shard_map/ppermute | solution.py:213
  122.5 2.7 %shard_map.66 = (f32[128,256]{1,0:T(8,128)S(1)}, f32[512,128]{1,0:T(8,128)S(1)}, f32[256,128]{1,0:T(8,128)S(1)}) custom-call(s32[8]{0:T(128)S(1)} %copy-done.4, s32[8]{0:T(128)S(1)} %copy-done.5, f32[512,128]{1,0:T(8,128)S(1)} %shard_map.65.own, f32[256,128]{1,0:T(8,128)S(1)} %collective-permute-done.9.halo_rows, ...), custom_call_target="tpu_custom_call" | custom-call | flops 20000000 | bytes 1000000 | tf_op jit(solution)/shard_map/pallas_call | solution.py:46
  125.2 1.0 collective-permute-start.10
  126.2 1.0 collective-permute-done.10.other
  127.4 19.1 %all_gather.14.shares = f32[1792,128]{1,0:T(8,128)S(1)} all-gather(f32[112,128]{1,0:T(8,128)S(1)} %shard_map.67), channel_id=1, replica_groups=mesh['x'=4,'z'=8,'core'=2,'col'=4] {'z','core'}, dimensions={0}, use_global_device_ids=true | all-gather | bytes 974848 | tf_op jit(solution)/shard_map/all_gather | solution.py:255
  146.6 1.7 shard_map.68
  148.3 12.6 %all_to_all.26.crossing = f32[4,224,128]{2,1,0:T(8,128)S(1)} all-to-all(f32[4,224,128]{2,1,0:T(8,128)S(1)} %get-tuple-element.64), channel_id=1, replica_groups=mesh['x'=4,'z'=8,'core'=2,'col'=4] {'x'}, dimensions={0} | all-to-all | bytes 917504 | tf_op jit(solution)/shard_map/all_to_all | solution.py:261
  160.9 1.5 shard_map.69.own
  162.4 1.9 collective-permute-start.11
  164.3 2.5 %collective-permute-done.11.halo_rows = f32[256,128]{1,0:T(8,128)S(1)} collective-permute-done((f32[256,128]{1,0:T(8,128)S(1)}, f32[256,128]{1,0:T(8,128)S(1)}, u32[]{:S(2)}, u32[]{:S(2)}) %collective-permute-start.11) | collective-permute-done | bytes 131104 | tf_op jit(solution)/shard_map/ppermute | solution.py:213
  166.8 2.7 %shard_map.70 = (f32[128,256]{1,0:T(8,128)S(1)}, f32[512,128]{1,0:T(8,128)S(1)}, f32[256,128]{1,0:T(8,128)S(1)}) custom-call(s32[8]{0:T(128)S(1)} %copy-done.4, s32[8]{0:T(128)S(1)} %copy-done.5, f32[512,128]{1,0:T(8,128)S(1)} %shard_map.69.own, f32[256,128]{1,0:T(8,128)S(1)} %collective-permute-done.11.halo_rows, ...), custom_call_target="tpu_custom_call" | custom-call | flops 20000000 | bytes 1000000 | tf_op jit(solution)/shard_map/pallas_call | solution.py:46
  169.5 0.9 collective-permute-start.12
  170.4 1.0 collective-permute-done.12.other
  171.6 19.1 %all_gather.15.shares = f32[1792,128]{1,0:T(8,128)S(1)} all-gather(f32[112,128]{1,0:T(8,128)S(1)} %shard_map.71), channel_id=1, replica_groups=mesh['x'=4,'z'=8,'core'=2,'col'=4] {'z','core'}, dimensions={0}, use_global_device_ids=true | all-gather | bytes 974848 | tf_op jit(solution)/shard_map/all_gather | solution.py:255
  190.8 1.7 shard_map.72
  192.5 12.6 %all_to_all.27.crossing = f32[4,224,128]{2,1,0:T(8,128)S(1)} all-to-all(f32[4,224,128]{2,1,0:T(8,128)S(1)} %get-tuple-element.70), channel_id=1, replica_groups=mesh['x'=4,'z'=8,'core'=2,'col'=4] {'x'}, dimensions={0} | all-to-all | bytes 917504 | tf_op jit(solution)/shard_map/all_to_all | solution.py:261
  205.1 1.5 shard_map.73.window
  206.6 1.9 collective-permute-start.13
  208.5 5.4 %collective-permute-done.13.before = f32[64,128]{1,0:T(8,128)S(1)} collective-permute-done((f32[64,128]{1,0:T(8,128)S(1)}, f32[64,128]{1,0:T(8,128)S(1)}, u32[]{:S(2)}, u32[]{:S(2)}) %collective-permute-start.13) | collective-permute-done | bytes 32800 | tf_op jit(solution)/shard_map/ppermute | solution.py:218
  213.9 1.2 shard_map.74
  (29 shorter events, 1.5 us)
Async XLA Ops:
  0.0 25.0 %copy-start.4 = (s32[8]{0:T(128)S(1)}, s32[8]{0:T(128)}, u32[]{:S(2)}) copy-start(s32[8]{0:T(128)} %order.21) | copy-start | bytes 100
  0.0 25.0 %copy-start.1 = (f32[8,1,64,64]{3,2,1,0:T(8,128)S(1)}, f32[8,1,64,64]{3,2,1,0:T(8,128)}, u32[]{:S(2)}) copy-start(f32[8,1,64,64]{3,2,1,0:T(8,128)} %tri.3) | copy-start | bytes 393220
  0.0 9.7 %copy-start.2 = (f32[256,128]{1,0:T(8,128)S(1)}, f32[256,128]{1,0:T(8,128)}, u32[]{:S(2)}) copy-start(f32[256,128]{1,0:T(8,128)} %own.1) | copy-start | bytes 393220
  1.2 1.0 copy-start
  2.2 0.7 copy-start.3
  5.1 23.0 %copy-start.5 = (s32[8]{0:T(128)S(1)}, s32[8]{0:T(128)}, u32[]{:S(2)}) copy-start(s32[8]{0:T(128)} %offsets.17) | copy-start | bytes 100
  5.1 14.1 %all-to-all-start = ((f32[4,2,128,128]{3,2,1,0:T(8,128)}), f32[4,2,128,128]{3,2,1,0:T(8,128)S(1)}, u32[]{:S(2)}, u32[]{:S(2)}) async-start(f32[4,2,128,128]{3,2,1,0:T(8,128)} %shard_map.56), calls=%async_computation | async-start | bytes 1048576 | tf_op jit(solution)/shard_map/all_to_all | solution.py:234
  9.7 18.4 %collective-permute-start.1 = (f32[256,128]{1,0:T(8,128)S(1)}, f32[256,128]{1,0:T(8,128)S(1)}, u32[]{:S(2)}, u32[]{:S(2)}) collective-permute-start(f32[256,128]{1,0:T(8,128)S(1)} %copy-done.2), channel_id=1, source_target_pairs={{4,0},{8,4},{12,8},{16,12},{20,16},{24,20},{28,24},{32,28},{36,32}... | collective-permute-start | bytes 393224 | tf_op jit(solution)/shard_map/ppermute | solution.py:213
  19.2 8.9 %collective-permute-start = (f32[2,1,128,128]{3,2,1,0:T(8,128)S(1)}, f32[2,1,128,128]{3,2,1,0:T(8,128)S(1)}, u32[]{:S(2)}, u32[]{:S(2)}) collective-permute-start(f32[2,1,128,128]{3,2,1,0:T(8,128)S(1)} %slice.21), channel_id=1, source_target_pairs={{4,0},{8,4},{12,8},{16,12},{20,16},{24,20},{28,24},{32,28},{36,32}... | collective-permute-start | bytes 393224 | tf_op jit(solution)/shard_map/ppermute | solution.py:213
  30.9 2.8 %collective-permute-start.2 = (f32[128,256]{1,0:T(8,128)S(1)}, f32[128,256]{1,0:T(8,128)S(1)}, u32[]{:S(2)}, u32[]{:S(2)}) collective-permute-start(f32[128,256]{1,0:T(8,128)S(1)} %get-tuple-element.41.partial), channel_id=1, source_target_pairs={{0,4},{4,0},{1,5},{5,1},{2,6},{6,2},{3,7},{7,3},{8,12},{12,8},{9,1... | collective-permute-start | bytes 393224 | tf_op jit(solution)/shard_map/ppermute | solution.py:222
  31.0 30.5 %collective-permute-start.5 = (f32[6,128,128]{2,1,0:T(8,128)S(1)}, f32[6,128,128]{2,1,0:T(8,128)S(1)}, u32[]{:S(2)}, u32[]{:S(2)}) collective-permute-start(f32[6,128,128]{2,1,0:T(8,128)S(1)} %shard_map.55.part0), channel_id=1, source_target_pairs={{0,3},{1,0},{2,1},{3,2},{4,7},{5,4},{6,5},{7,6},{8,11},{9,8},{10,9... | collective-permute-start | bytes 1179656 | tf_op jit(solution)/shard_map/ppermute | solution.py:243
  32.2 29.3 %collective-permute-start.4 = (f32[6,128,128]{2,1,0:T(8,128)S(1)}, f32[6,128,128]{2,1,0:T(8,128)S(1)}, u32[]{:S(2)}, u32[]{:S(2)}) collective-permute-start(f32[6,128,128]{2,1,0:T(8,128)S(1)} %shard_map.55.part0), channel_id=1, source_target_pairs={{0,2},{1,3},{2,0},{3,1},{4,6},{5,7},{6,4},{7,5},{8,10},{9,11},{10,... | collective-permute-start | bytes 1179656 | tf_op jit(solution)/shard_map/ppermute | solution.py:243
  33.7 27.8 %collective-permute-start.3 = (f32[6,128,128]{2,1,0:T(8,128)S(1)}, f32[6,128,128]{2,1,0:T(8,128)S(1)}, u32[]{:S(2)}, u32[]{:S(2)}) collective-permute-start(f32[6,128,128]{2,1,0:T(8,128)S(1)} %shard_map.55.part0), channel_id=1, source_target_pairs={{0,1},{1,2},{2,3},{3,0},{4,5},{5,6},{6,7},{7,4},{8,9},{9,10},{10,1... | collective-permute-start | bytes 1179656 | tf_op jit(solution)/shard_map/ppermute | solution.py:243
  56.7 12.7 %all-to-all-start.1 = ((f32[4,224,128]{2,1,0:T(8,128)}), f32[4,224,128]{2,1,0:T(8,128)S(1)}, u32[]{:S(2)}, u32[]{:S(2)}) async-start(f32[4,224,128]{2,1,0:T(8,128)} %get-tuple-element.44), calls=%async_computation.1 | async-start | bytes 917504 | tf_op jit(solution)/shard_map/all_to_all | solution.py:261
  69.6 8.6 %collective-permute-start.7 = (f32[2,3,128,128]{3,2,1,0:T(8,128)S(1)}, f32[2,3,128,128]{3,2,1,0:T(8,128)S(1)}, u32[]{:S(2)}, u32[]{:S(2)}) collective-permute-start(f32[2,3,128,128]{3,2,1,0:T(8,128)S(1)} %get-tuple-element.54), channel_id=1, source_target_pairs={{4,0},{8,4},{12,8},{16,12},{20,16},{24,20},{28,24},{32,28},{36,32}... | collective-permute-start | bytes 1179656 | tf_op jit(solution)/shard_map/ppermute | solution.py:213
  73.0 5.2 %collective-permute-start.6 = (f32[256,128]{1,0:T(8,128)S(1)}, f32[256,128]{1,0:T(8,128)S(1)}, u32[]{:S(2)}, u32[]{:S(2)}) collective-permute-start(f32[256,128]{1,0:T(8,128)S(1)} %slice.22), channel_id=1, source_target_pairs={{4,0},{8,4},{12,8},{16,12},{20,16},{24,20},{28,24},{32,28},{36,32}... | collective-permute-start | bytes 393224 | tf_op jit(solution)/shard_map/ppermute | solution.py:213
  80.9 2.7 %collective-permute-start.8 = (f32[128,256]{1,0:T(8,128)S(1)}, f32[128,256]{1,0:T(8,128)S(1)}, u32[]{:S(2)}, u32[]{:S(2)}) collective-permute-start(f32[128,256]{1,0:T(8,128)S(1)} %get-tuple-element.55.partial), channel_id=1, source_target_pairs={{0,4},{4,0},{1,5},{5,1},{2,6},{6,2},{3,7},{7,3},{8,12},{12,8},{9,1... | collective-permute-start | bytes 393224 | tf_op jit(solution)/shard_map/ppermute | solution.py:222
  118.0 4.4 %collective-permute-start.9 = (f32[256,128]{1,0:T(8,128)S(1)}, f32[256,128]{1,0:T(8,128)S(1)}, u32[]{:S(2)}, u32[]{:S(2)}) collective-permute-start(f32[256,128]{1,0:T(8,128)S(1)} %slice.23), channel_id=1, source_target_pairs={{4,0},{8,4},{12,8},{16,12},{20,16},{24,20},{28,24},{32,28},{36,32}... | collective-permute-start | bytes 393224 | tf_op jit(solution)/shard_map/ppermute | solution.py:213
  125.2 2.0 collective-permute-start.10
  162.4 4.4 %collective-permute-start.11 = (f32[256,128]{1,0:T(8,128)S(1)}, f32[256,128]{1,0:T(8,128)S(1)}, u32[]{:S(2)}, u32[]{:S(2)}) collective-permute-start(f32[256,128]{1,0:T(8,128)S(1)} %slice.24), channel_id=1, source_target_pairs={{4,0},{8,4},{12,8},{16,12},{20,16},{24,20},{28,24},{32,28},{36,32}... | collective-permute-start | bytes 393224 | tf_op jit(solution)/shard_map/ppermute | solution.py:213
  169.5 1.9 collective-permute-start.12
  206.6 7.3 %collective-permute-start.13 = (f32[64,128]{1,0:T(8,128)S(1)}, f32[64,128]{1,0:T(8,128)S(1)}, u32[]{:S(2)}, u32[]{:S(2)}) collective-permute-start(f32[64,128]{1,0:T(8,128)S(1)} %slice.25), channel_id=1, source_target_pairs={{0,4},{4,8},{8,12},{12,16},{16,20},{20,24},{24,28},{28,32},{32,36}... | collective-permute-start | bytes 98312 | tf_op jit(solution)/shard_map/ppermute | solution.py:218

commit v3 on v2

--- a/solution.py
+++ b/solution.py
@@ -18,8 +18,14 @@
 F32 = jnp.float32
 
 
-def exact(a, b, dims=(((1,), (0,)), ((), ()))):
-    return lax.dot_general(a, b, dims, precision=lax.Precision.HIGHEST, preferred_element_type=F32)
+def exact(a, b, axis):
+    return lax.dot_general(
+        a,
+        b,
+        (((axis,), (0,)), ((), ())),
+        precision=lax.Precision.HIGHEST,
+        preferred_element_type=F32,
+    )
 
 
 def halves(a):
@@ -37,9 +43,10 @@
     )
 
 
-def call(body, outs, *args, smem=0, scratch=(), flops=20_000_000):
+def call(body, outs, *args, smem=0, hbm=0, scratch=(), flops=20_000_000, limit=32):
     spaces = [pl.BlockSpec(memory_space=pltpu.SMEM)] * smem
-    spaces += [pl.BlockSpec(memory_space=pltpu.VMEM)] * (len(args) - smem)
+    spaces += [pl.BlockSpec(memory_space=pltpu.HBM)] * hbm
+    spaces += [pl.BlockSpec(memory_space=pltpu.VMEM)] * (len(args) - smem - hbm)
     single = not isinstance(outs, list)
     shapes = [jax.ShapeDtypeStruct(o, F32) for o in ([outs] if single else outs)]
     specs = [pl.BlockSpec(memory_space=pltpu.VMEM)] * len(shapes)
@@ -50,7 +57,7 @@
         out_specs=specs[0] if single else specs,
         scratch_shapes=list(scratch),
         cost_estimate=pl.CostEstimate(flops=flops, bytes_accessed=1_000_000, transcendentals=0),
-        compiler_params=pltpu.CompilerParams(vmem_limit_bytes=32 * 1024 * 1024),
+        compiler_params=pltpu.CompilerParams(vmem_limit_bytes=limit * 1024 * 1024),
     )(*args)
 
 
@@ -69,16 +76,35 @@
     return g == PLANES * CHIPS * 2 - 1
 
 
-def block_kernel(positions, order, house, tri, out):
+def block_kernel(positions, order, house, tri, out, v, t, sems):
+    copies = []
     for i, p in enumerate(positions):
-        v = house[order[p], 0]
-        t = tri[order[p], 0]
-        h = eye(S) - exact(v, exact(t, v, (((1,), (1,)), ((), ()))))
+        copies.append(pltpu.make_async_copy(house.at[order[p], 0], v.at[i], sems.at[i, 0]))
+        copies.append(pltpu.make_async_copy(tri.at[order[p], 0], t.at[i], sems.at[i, 1]))
+    for copy in copies:
+        copy.start()
+    for copy in copies:
+        copy.wait()
+    for i in range(len(positions)):
+        h = eye(S) - exact(v[i], exact(t[i], v[i], 1), 0)
         if len(out.shape) == 4:
             for c in range(out.shape[0]):
                 out[c, i] = h
         else:
             out[i] = h
+
+
+def make_blocks(positions, shape, order, house, tri):
+    count = len(positions)
+    return call(
+        functools.partial(block_kernel, positions), shape, order, house, tri, smem=1, hbm=2,
+        limit=60,
+        scratch=[
+            pltpu.VMEM((count, W, S), F32),
+            pltpu.VMEM((count, W, W), F32),
+            pltpu.SemaphoreType.DMA((count, 2)),
+        ],
+    )
 
 
 def pick_kernel(part0, part1, part2, part3, blocks, head):
@@ -96,9 +122,12 @@
 
 def chain(wins, blocks, count, offset, carry):
     kept = carry
+    added = []
     for j in range(count):
         rest = [win[pl.ds(offset + (j + 1) * W, W), :] for win in wins]
-        out = dot(blocks(j), jnp.concatenate([carry, jnp.concatenate(rest, 1)], 0))
+        added.append(dot(blocks(j)[:, W:], jnp.concatenate(rest, 1)))
+    for j in range(count):
+        out = dot(blocks(j)[:, :W], carry) + added[j]
         for k, win in enumerate(wins):
             win[pl.ds(offset + j * W, W), :] = out[:W, k * S : (k + 1) * S]
         carry = out[W:]
@@ -167,13 +196,15 @@
     z, upper = lax.axis_index("z"), lax.axis_index("core") == 1
     entry = jnp.where(upper, other[:, S:], eye(S))
     add = jnp.where(upper, other[:, :S], 0.0)
-    to_here, to_end = jnp.zeros((S, S), F32), eye(S)
-    total = jnp.zeros((2 * S, S), F32)
     for k in reversed(range(CHIPS)):
         low = shares[2 * k * SHARE : (2 * k + 1) * SHARE]
         high = shares[(2 * k + 1) * SHARE : (2 * k + 2) * SHARE]
         step = unpacked(low[: W // 2], high[:W])
         rows = jnp.concatenate([low[W // 2 :], high[W:]], 0)
+        if k == CHIPS - 1:
+            total = jnp.concatenate([jnp.zeros_like(rows), rows], 0)
+            to_here, to_end = jnp.where(k == z, entry, 0.0), step
+            continue
         both = dot(jnp.concatenate([to_here, to_end], 0), jnp.concatenate([rows, step], 1))
         total = total + both[:, :S]
         to_here = jnp.where(k == z, entry, both[:S, S:])
@@ -189,8 +220,8 @@
     x = lax.axis_index("x")
     off_b = offsets[order[2 * n + 1]]
     total = carry[...]
-    value = jnp.zeros((S, S), F32)
-    for k in reversed(range(PLANES)):
+    value = jnp.where(x == PLANES - 1, at_chip[...], 0.0)
+    for k in reversed(range(PLANES - 1)):
         step = unpacked(crossing[k, S : S + W // 2], crossing[k, S + W // 2 :])
         both = dot(value, jnp.concatenate([crossing[k, :S], step], 1))
         total = total + both[:, :S]
@@ -228,17 +259,14 @@
     cols = lax.axis_size("col")
 
     halo_rows = from_next(eigvecs)
-    block = call(
-        functools.partial(block_kernel, [0, 1]), (cols, 2, S, S), order, reflectors, factors, smem=1
-    )
+    reflectors = jnp.swapaxes(reflectors, 2, 3)
+    block = make_blocks([0, 1], (cols, 2, S, S), order, reflectors, factors)
     blocks = lax.all_to_all(block, "col", 0, 0)
-    later = call(
-        functools.partial(block_kernel, list(range(2, 2 * phases))),
-        (2 * phases - 2, S, S),
-        order, reflectors, factors, smem=1,
-    )
+    later = make_blocks(
+        list(range(2, 2 * phases)), (2 * phases - 2, S, S), order, reflectors, factors
+    )
+    later, blocks = lax.optimization_barrier((later, blocks))
     halo = from_next(blocks[:2, ::2])
-    later, halo, halo_rows = lax.optimization_barrier((later, halo, halo_rows))
     parts = [later] + [
         lax.ppermute(later, "col", [(c, (c + d) % cols) for c in range(cols)]) for d in (1, 2, 3)
     ]

time: 216 us -> 212 us (0.981)
  local copies, waits for them, and re-layouts: 2.87 us -> 0.06 us
    unnamed x13 -> x8, local copies, waits for them, and re-layouts: 2.82 us -> 0.02 us
    ppermute x6, waiting for transfers between devices: 8.05 us -> 10.7 us  [from_next(): return lax.ppermute(block, ROW, [(i + 1, i) for i in range(size - 1)])]
    all_to_all x1, waiting for transfers between devices: 2.58 us -> 0.01 us  [local(): blocks = lax.all_to_all(block, 'col', 0, 0)]
where the time goes in v3:
time: 212 us; the launch traced here: 211 us
  blocking collectives  116 us (55%)
  starting transfers between devices  37.2 us (18%)
  Pallas kernels  30.6 us (14%)
  waiting for transfers between devices  26.9 us (13%)
    all_gather x4, blocking collectives, local(): shares = lax.all_gather(share, ('z', 'core'), axis=0, tiled=True)  77.5 us
    all_to_all x3, blocking collectives, local(): crossing = lax.all_to_all(out, 'x', 0, 0)  38.2 us
    pallas_call x20, Pallas kernels, call(): pl.pallas_call(body, out_shape=shapes[0] if single else shapes, in_specs=...  30.6 us
    ppermute x6, starting transfers between devices, from_next(): return lax.ppermute(block, ROW, [(i + 1, i) for i in range(size - 1)])  19.6 us
    ppermute x6, waiting for transfers between devices, from_next(): return lax.ppermute(block, ROW, [(i + 1, i) for i in range(size - 1)])  10.7 us
    all_to_all x1, waiting for transfers between devices, local(): crossing = lax.all_to_all(out, 'x', 0, 0)  7.82 us
    ppermute x1, waiting for transfers between devices, from_previous(): return lax.ppermute(block, ROW, [(i, i + 1) for i in range(size - 1)])  5.41 us
    all_to_all x1, starting transfers between devices, local(): crossing = lax.all_to_all(out, 'x', 0, 0)  4.82 us
  transfers between devices with their start and end apart: 16, of which 9 were waited for; matrix products, arithmetic and copies ran while one was open for 0% of the time, Pallas kernels for 3%

profile of v3, /device:TPU:2, one launch (start us, length us, event | category | flops | bytes accessed | tf_op | source)
XLA Modules:
  0.0 210.8 jit_solution(18188178363460537116)
XLA Ops:
  0.0 2.9 %shard_map.56 = f32[4,2,128,128]{3,2,1,0:T(8,128)} custom-call(s32[8]{0:T(128)} %order.21, f32[8,1,64,128]{3,2,1,0:T(8,128)} %bitcast.1, f32[8,1,64,64]{3,2,1,0:T(8,128)} %tri.3), custom_call_target="tpu_custom_call" | custom-call | flops 20000000 | bytes 1000000 | tf_op jit(solution)/shard_map/pallas_call | solution.py:53
  2.9 4.5 %all-to-all-start = ((f32[4,2,128,128]{3,2,1,0:T(8,128)}), f32[4,2,128,128]{3,2,1,0:T(8,128)S(1)}, u32[]{:S(2)}, u32[]{:S(2)}) async-start(f32[4,2,128,128]{3,2,1,0:T(8,128)} %shard_map.56), calls=%async_computation | async-start | bytes 1048576 | tf_op jit(solution)/shard_map/all_to_all | solution.py:264
  7.4 6.9 %collective-permute-start = (f32[256,128]{1,0:T(8,128)S(1)}, f32[256,128]{1,0:T(8,128)S(1)}, u32[]{:S(2)}, u32[]{:S(2)}) collective-permute-start(f32[256,128]{1,0:T(8,128)S(1)} %copy-done.1), channel_id=1, source_target_pairs={{4,0},{8,4},{12,8},{16,12},{20,16},{24,20},{28,24},{32,28},{36,32}... | collective-permute-start | bytes 393224 | tf_op jit(solution)/shard_map/ppermute | solution.py:244
  14.3 3.5 %shard_map.55.part0 = f32[6,128,128]{2,1,0:T(8,128)} custom-call(s32[8]{0:T(128)} %order.21, f32[8,1,64,128]{3,2,1,0:T(8,128)} %bitcast.2, f32[8,1,64,64]{3,2,1,0:T(8,128)} %tri.3), custom_call_target="tpu_custom_call" | custom-call | flops 20000000 | bytes 1000000 | tf_op jit(solution)/shard_map/pallas_call | solution.py:53
  17.8 4.8 %collective-permute-start.1 = (f32[2,1,128,128]{3,2,1,0:T(8,128)S(1)}, f32[2,1,128,128]{3,2,1,0:T(8,128)S(1)}, u32[]{:S(2)}, u32[]{:S(2)}) collective-permute-start(f32[2,1,128,128]{3,2,1,0:T(8,128)S(1)} %slice.16), channel_id=1, source_target_pairs={{4,0},{8,4},{12,8},{16,12},{20,16},{24,20},{28,24},{32,28},{36,32}... | collective-permute-start | bytes 393224 | tf_op jit(solution)/shard_map/ppermute | solution.py:244
  22.7 2.5 %collective-permute-done.1.halo = f32[2,1,128,128]{3,2,1,0:T(8,128)S(1)} collective-permute-done((f32[2,1,128,128]{3,2,1,0:T(8,128)S(1)}, f32[2,1,128,128]{3,2,1,0:T(8,128)S(1)}, u32[]{:S(2)}, u32[]{:S(2)}) %collective-permute-start.1) | collective-permute-done | bytes 131104 | tf_op jit(solution)/shard_map/ppermute | solution.py:244
  25.1 2.5 %shard_map.57 = (f32[128,256]{1,0:T(8,128)S(1)}, f32[512,128]{1,0:T(8,128)S(1)}, f32[256,128]{1,0:T(8,128)S(1)}) custom-call(s32[8]{0:T(128)S(1)} %copy-done.2, s32[8]{0:T(128)S(1)} %copy-done.3, f32[256,128]{1,0:T(8,128)S(1)} %copy-done.1, f32[256,128]{1,0:T(8,128)S(1)} %collective-permute-done.halo_rows, f32[4,2,128,128]{3,2,1,0:T(8,128)S(1)} %all-to-all-done.blocks, ...), custom_call_target="tpu_custom_call" | custom-call | flops 20000000 | bytes 1000000 | tf_op jit(solution)/shard_map/pallas_call | solution.py:53
  27.7 1.3 collective-permute-start.5
  29.0 1.4 collective-permute-start.4
  30.4 0.3 collective-permute-start.3
  30.8 0.2 shard_map.58
  31.0 20.9 %all_gather.12.shares = f32[1792,128]{1,0:T(8,128)S(1)} all-gather(f32[112,128]{1,0:T(8,128)S(1)} %shard_map.58), channel_id=1, replica_groups=mesh['x'=4,'z'=8,'core'=2,'col'=4] {'z','core'}, dimensions={0}, use_global_device_ids=true | all-gather | bytes 974848 | tf_op jit(solution)/shard_map/all_gather | solution.py:283
  51.9 2.2 %shard_map.59 = (f32[128,128]{1,0:T(8,128)S(1)}, f32[128,128]{1,0:T(8,128)S(1)}, f32[4,224,128]{2,1,0:T(8,128)}) custom-call(f32[128,256]{1,0:T(8,128)S(1)} %collective-permute-done.2.other, f32[1792,128]{1,0:T(8,128)S(1)} %all_gather.12.shares), custom_call_target="tpu_custom_call" | custom-call | flops 20000000 | bytes 1000000 | tf_op jit(solution)/shard_map/pallas_call | solution.py:53
  54.2 4.8 %all-to-all-start.1 = ((f32[4,224,128]{2,1,0:T(8,128)}), f32[4,224,128]{2,1,0:T(8,128)S(1)}, u32[]{:S(2)}, u32[]{:S(2)}) async-start(f32[4,224,128]{2,1,0:T(8,128)} %get-tuple-element.42), calls=%async_computation.1 | async-start | bytes 917504 | tf_op jit(solution)/shard_map/all_to_all | solution.py:289
  59.0 7.8 %all-to-all-done.1.crossing = f32[4,224,128]{2,1,0:T(8,128)S(1)} async-done(((f32[4,224,128]{2,1,0:T(8,128)}), f32[4,224,128]{2,1,0:T(8,128)S(1)}, u32[]{:S(2)}, u32[]{:S(2)}) %all-to-all-start.1) | async-done | bytes 458784 | tf_op jit(solution)/shard_map/all_to_all | solution.py:289
  66.9 0.3 shard_map.61
  67.2 1.9 collective-permute-start.7
  69.1 1.3 shard_map.60.own
  70.4 2.1 %collective-permute-start.6 = (f32[256,128]{1,0:T(8,128)S(1)}, f32[256,128]{1,0:T(8,128)S(1)}, u32[]{:S(2)}, u32[]{:S(2)}) collective-permute-start(f32[256,128]{1,0:T(8,128)S(1)} %slice.21), channel_id=1, source_target_pairs={{4,0},{8,4},{12,8},{16,12},{20,16},{24,20},{28,24},{32,28},{36,32}... | collective-permute-start | bytes 393224 | tf_op jit(solution)/shard_map/ppermute | solution.py:244
  72.5 3.2 %collective-permute-done.6.halo_rows = f32[256,128]{1,0:T(8,128)S(1)} collective-permute-done((f32[256,128]{1,0:T(8,128)S(1)}, f32[256,128]{1,0:T(8,128)S(1)}, u32[]{:S(2)}, u32[]{:S(2)}) %collective-permute-start.6) | collective-permute-done | bytes 131104 | tf_op jit(solution)/shard_map/ppermute | solution.py:244
  75.8 2.5 %shard_map.62 = (f32[128,256]{1,0:T(8,128)S(1)}, f32[512,128]{1,0:T(8,128)S(1)}, f32[256,128]{1,0:T(8,128)S(1)}) custom-call(s32[8]{0:T(128)S(1)} %copy-done.2, s32[8]{0:T(128)S(1)} %copy-done.3, f32[512,128]{1,0:T(8,128)S(1)} %shard_map.60.own, f32[256,128]{1,0:T(8,128)S(1)} %collective-permute-done.6.halo_rows, ...), custom_call_target="tpu_custom_call" | custom-call | flops 20000000 | bytes 1000000 | tf_op jit(solution)/shard_map/pallas_call | solution.py:53
  78.2 1.5 collective-permute-start.8
  79.8 1.0 collective-permute-done.8.other
  81.0 18.1 %all_gather.13.shares = f32[1792,128]{1,0:T(8,128)S(1)} all-gather(f32[112,128]{1,0:T(8,128)S(1)} %shard_map.63), channel_id=1, replica_groups=mesh['x'=4,'z'=8,'core'=2,'col'=4] {'z','core'}, dimensions={0}, use_global_device_ids=true | all-gather | bytes 974848 | tf_op jit(solution)/shard_map/all_gather | solution.py:283
  99.1 1.5 shard_map.64
  100.6 13.0 %all_to_all.25.crossing = f32[4,224,128]{2,1,0:T(8,128)S(1)} all-to-all(f32[4,224,128]{2,1,0:T(8,128)S(1)} %get-tuple-element.56), channel_id=1, replica_groups=mesh['x'=4,'z'=8,'core'=2,'col'=4] {'x'}, dimensions={0} | all-to-all | bytes 917504 | tf_op jit(solution)/shard_map/all_to_all | solution.py:289
  113.6 1.3 shard_map.65.own
  114.9 1.9 collective-permute-start.9
  116.8 2.5 %collective-permute-done.9.halo_rows = f32[256,128]{1,0:T(8,128)S(1)} collective-permute-done((f32[256,128]{1,0:T(8,128)S(1)}, f32[256,128]{1,0:T(8,128)S(1)}, u32[]{:S(2)}, u32[]{:S(2)}) %collective-permute-start.9) | collective-permute-done | bytes 131104 | tf_op jit(solution)/shard_map/ppermute | solution.py:244
  119.3 2.5 %shard_map.66 = (f32[128,256]{1,0:T(8,128)S(1)}, f32[512,128]{1,0:T(8,128)S(1)}, f32[256,128]{1,0:T(8,128)S(1)}) custom-call(s32[8]{0:T(128)S(1)} %copy-done.2, s32[8]{0:T(128)S(1)} %copy-done.3, f32[512,128]{1,0:T(8,128)S(1)} %shard_map.65.own, f32[256,128]{1,0:T(8,128)S(1)} %collective-permute-done.9.halo_rows, ...), custom_call_target="tpu_custom_call" | custom-call | flops 20000000 | bytes 1000000 | tf_op jit(solution)/shard_map/pallas_call | solution.py:53
  121.8 0.9 collective-permute-start.10
  122.7 1.0 collective-permute-done.10.other
  123.9 19.3 %all_gather.14.shares = f32[1792,128]{1,0:T(8,128)S(1)} all-gather(f32[112,128]{1,0:T(8,128)S(1)} %shard_map.67), channel_id=1, replica_groups=mesh['x'=4,'z'=8,'core'=2,'col'=4] {'z','core'}, dimensions={0}, use_global_device_ids=true | all-gather | bytes 974848 | tf_op jit(solution)/shard_map/all_gather | solution.py:283
  143.3 1.5 shard_map.68
  144.7 12.6 %all_to_all.26.crossing = f32[4,224,128]{2,1,0:T(8,128)S(1)} all-to-all(f32[4,224,128]{2,1,0:T(8,128)S(1)} %get-tuple-element.62), channel_id=1, replica_groups=mesh['x'=4,'z'=8,'core'=2,'col'=4] {'x'}, dimensions={0} | all-to-all | bytes 917504 | tf_op jit(solution)/shard_map/all_to_all | solution.py:289
  157.3 1.3 shard_map.69.own
  158.7 1.9 collective-permute-start.11
  160.6 2.5 %collective-permute-done.11.halo_rows = f32[256,128]{1,0:T(8,128)S(1)} collective-permute-done((f32[256,128]{1,0:T(8,128)S(1)}, f32[256,128]{1,0:T(8,128)S(1)}, u32[]{:S(2)}, u32[]{:S(2)}) %collective-permute-start.11) | collective-permute-done | bytes 131104 | tf_op jit(solution)/shard_map/ppermute | solution.py:244
  163.1 2.5 %shard_map.70 = (f32[128,256]{1,0:T(8,128)S(1)}, f32[512,128]{1,0:T(8,128)S(1)}, f32[256,128]{1,0:T(8,128)S(1)}) custom-call(s32[8]{0:T(128)S(1)} %copy-done.2, s32[8]{0:T(128)S(1)} %copy-done.3, f32[512,128]{1,0:T(8,128)S(1)} %shard_map.69.own, f32[256,128]{1,0:T(8,128)S(1)} %collective-permute-done.11.halo_rows, ...), custom_call_target="tpu_custom_call" | custom-call | flops 20000000 | bytes 1000000 | tf_op jit(solution)/shard_map/pallas_call | solution.py:53
  165.6 0.9 collective-permute-start.12
  166.4 1.0 collective-permute-done.12.other
  167.7 19.1 %all_gather.15.shares = f32[1792,128]{1,0:T(8,128)S(1)} all-gather(f32[112,128]{1,0:T(8,128)S(1)} %shard_map.71), channel_id=1, replica_groups=mesh['x'=4,'z'=8,'core'=2,'col'=4] {'z','core'}, dimensions={0}, use_global_device_ids=true | all-gather | bytes 974848 | tf_op jit(solution)/shard_map/all_gather | solution.py:283
  186.8 1.5 shard_map.72
  188.3 12.6 %all_to_all.27.crossing = f32[4,224,128]{2,1,0:T(8,128)S(1)} all-to-all(f32[4,224,128]{2,1,0:T(8,128)S(1)} %get-tuple-element.68), channel_id=1, replica_groups=mesh['x'=4,'z'=8,'core'=2,'col'=4] {'x'}, dimensions={0} | all-to-all | bytes 917504 | tf_op jit(solution)/shard_map/all_to_all | solution.py:289
  200.9 1.3 shard_map.73.window
  202.2 1.9 collective-permute-start.13
  204.1 5.4 %collective-permute-done.13.before = f32[64,128]{1,0:T(8,128)S(1)} collective-permute-done((f32[64,128]{1,0:T(8,128)S(1)}, f32[64,128]{1,0:T(8,128)S(1)}, u32[]{:S(2)}, u32[]{:S(2)}) %collective-permute-start.13) | collective-permute-done | bytes 32800 | tf_op jit(solution)/shard_map/ppermute | solution.py:249
  209.5 1.2 shard_map.74
  (24 shorter events, 0.9 us)
Async XLA Ops:
  0.0 7.4 %copy-start.1 = (f32[256,128]{1,0:T(8,128)S(1)}, f32[256,128]{1,0:T(8,128)}, u32[]{:S(2)}) copy-start(f32[256,128]{1,0:T(8,128)} %own.1) | copy-start | bytes 393220
  0.0 25.1 %copy-start.2 = (s32[8]{0:T(128)S(1)}, s32[8]{0:T(128)}, u32[]{:S(2)}) copy-start(s32[8]{0:T(128)} %order.21) | copy-start | bytes 100
  0.0 25.1 %copy-start.3 = (s32[8]{0:T(128)S(1)}, s32[8]{0:T(128)}, u32[]{:S(2)}) copy-start(s32[8]{0:T(128)} %offsets.17) | copy-start | bytes 100
  2.9 14.8 %all-to-all-start = ((f32[4,2,128,128]{3,2,1,0:T(8,128)}), f32[4,2,128,128]{3,2,1,0:T(8,128)S(1)}, u32[]{:S(2)}, u32[]{:S(2)}) async-start(f32[4,2,128,128]{3,2,1,0:T(8,128)} %shard_map.56), calls=%async_computation | async-start | bytes 1048576 | tf_op jit(solution)/shard_map/all_to_all | solution.py:264
  7.4 15.2 %collective-permute-start = (f32[256,128]{1,0:T(8,128)S(1)}, f32[256,128]{1,0:T(8,128)S(1)}, u32[]{:S(2)}, u32[]{:S(2)}) collective-permute-start(f32[256,128]{1,0:T(8,128)S(1)} %copy-done.1), channel_id=1, source_target_pairs={{4,0},{8,4},{12,8},{16,12},{20,16},{24,20},{28,24},{32,28},{36,32}... | collective-permute-start | bytes 393224 | tf_op jit(solution)/shard_map/ppermute | solution.py:244
  17.8 7.4 %collective-permute-start.1 = (f32[2,1,128,128]{3,2,1,0:T(8,128)S(1)}, f32[2,1,128,128]{3,2,1,0:T(8,128)S(1)}, u32[]{:S(2)}, u32[]{:S(2)}) collective-permute-start(f32[2,1,128,128]{3,2,1,0:T(8,128)S(1)} %slice.16), channel_id=1, source_target_pairs={{4,0},{8,4},{12,8},{16,12},{20,16},{24,20},{28,24},{32,28},{36,32}... | collective-permute-start | bytes 393224 | tf_op jit(solution)/shard_map/ppermute | solution.py:244
  27.6 39.2 %copy-start = (f32[6,128,128]{2,1,0:T(8,128)S(1)}, f32[6,128,128]{2,1,0:T(8,128)}, u32[]{:S(2)}) copy-start(f32[6,128,128]{2,1,0:T(8,128)} %shard_map.55.part0) | copy-start | bytes 1179652
  27.6 3.1 %collective-permute-start.2 = (f32[128,256]{1,0:T(8,128)S(1)}, f32[128,256]{1,0:T(8,128)S(1)}, u32[]{:S(2)}, u32[]{:S(2)}) collective-permute-start(f32[128,256]{1,0:T(8,128)S(1)} %get-tuple-element.39.partial), channel_id=1, source_target_pairs={{0,4},{4,0},{1,5},{5,1},{2,6},{6,2},{3,7},{7,3},{8,12},{12,8},{9,1... | collective-permute-start | bytes 393224 | tf_op jit(solution)/shard_map/ppermute | solution.py:253
  27.7 31.3 %collective-permute-start.5 = (f32[6,128,128]{2,1,0:T(8,128)}, f32[6,128,128]{2,1,0:T(8,128)S(1)}, u32[]{:S(2)}, u32[]{:S(2)}) collective-permute-start(f32[6,128,128]{2,1,0:T(8,128)} %shard_map.55.part0), channel_id=1, source_target_pairs={{0,3},{1,0},{2,1},{3,2},{4,7},{5,4},{6,5},{7,6},{8,11},{9,8},{10,9... | collective-permute-start | bytes 1179656 | tf_op jit(solution)/shard_map/ppermute | solution.py:271
  29.0 30.0 %collective-permute-start.4 = (f32[6,128,128]{2,1,0:T(8,128)}, f32[6,128,128]{2,1,0:T(8,128)S(1)}, u32[]{:S(2)}, u32[]{:S(2)}) collective-permute-start(f32[6,128,128]{2,1,0:T(8,128)} %shard_map.55.part0), channel_id=1, source_target_pairs={{0,2},{1,3},{2,0},{3,1},{4,6},{5,7},{6,4},{7,5},{8,10},{9,11},{10,... | collective-permute-start | bytes 1179656 | tf_op jit(solution)/shard_map/ppermute | solution.py:271
  30.4 28.6 %collective-permute-start.3 = (f32[6,128,128]{2,1,0:T(8,128)}, f32[6,128,128]{2,1,0:T(8,128)S(1)}, u32[]{:S(2)}, u32[]{:S(2)}) collective-permute-start(f32[6,128,128]{2,1,0:T(8,128)} %shard_map.55.part0), channel_id=1, source_target_pairs={{0,1},{1,2},{2,3},{3,0},{4,5},{5,6},{6,7},{7,4},{8,9},{9,10},{10,1... | collective-permute-start | bytes 1179656 | tf_op jit(solution)/shard_map/ppermute | solution.py:271
  54.2 12.7 %all-to-all-start.1 = ((f32[4,224,128]{2,1,0:T(8,128)}), f32[4,224,128]{2,1,0:T(8,128)S(1)}, u32[]{:S(2)}, u32[]{:S(2)}) async-start(f32[4,224,128]{2,1,0:T(8,128)} %get-tuple-element.42), calls=%async_computation.1 | async-start | bytes 917504 | tf_op jit(solution)/shard_map/all_to_all | solution.py:289
  67.2 8.6 %collective-permute-start.7 = (f32[2,3,128,128]{3,2,1,0:T(8,128)S(1)}, f32[2,3,128,128]{3,2,1,0:T(8,128)S(1)}, u32[]{:S(2)}, u32[]{:S(2)}) collective-permute-start(f32[2,3,128,128]{3,2,1,0:T(8,128)S(1)} %get-tuple-element.52), channel_id=1, source_target_pairs={{4,0},{8,4},{12,8},{16,12},{20,16},{24,20},{28,24},{32,28},{36,32}... | collective-permute-start | bytes 1179656 | tf_op jit(solution)/shard_map/ppermute | solution.py:244
  70.4 5.4 %collective-permute-start.6 = (f32[256,128]{1,0:T(8,128)S(1)}, f32[256,128]{1,0:T(8,128)S(1)}, u32[]{:S(2)}, u32[]{:S(2)}) collective-permute-start(f32[256,128]{1,0:T(8,128)S(1)} %slice.21), channel_id=1, source_target_pairs={{4,0},{8,4},{12,8},{16,12},{20,16},{24,20},{28,24},{32,28},{36,32}... | collective-permute-start | bytes 393224 | tf_op jit(solution)/shard_map/ppermute | solution.py:244
  78.2 2.5 %collective-permute-start.8 = (f32[128,256]{1,0:T(8,128)S(1)}, f32[128,256]{1,0:T(8,128)S(1)}, u32[]{:S(2)}, u32[]{:S(2)}) collective-permute-start(f32[128,256]{1,0:T(8,128)S(1)} %get-tuple-element.53.partial), channel_id=1, source_target_pairs={{0,4},{4,0},{1,5},{5,1},{2,6},{6,2},{3,7},{7,3},{8,12},{12,8},{9,1... | collective-permute-start | bytes 393224 | tf_op jit(solution)/shard_map/ppermute | solution.py:253
  114.9 4.4 %collective-permute-start.9 = (f32[256,128]{1,0:T(8,128)S(1)}, f32[256,128]{1,0:T(8,128)S(1)}, u32[]{:S(2)}, u32[]{:S(2)}) collective-permute-start(f32[256,128]{1,0:T(8,128)S(1)} %slice.22), channel_id=1, source_target_pairs={{4,0},{8,4},{12,8},{16,12},{20,16},{24,20},{28,24},{32,28},{36,32}... | collective-permute-start | bytes 393224 | tf_op jit(solution)/shard_map/ppermute | solution.py:244
  121.8 1.9 collective-permute-start.10
  158.7 4.4 %collective-permute-start.11 = (f32[256,128]{1,0:T(8,128)S(1)}, f32[256,128]{1,0:T(8,128)S(1)}, u32[]{:S(2)}, u32[]{:S(2)}) collective-permute-start(f32[256,128]{1,0:T(8,128)S(1)} %slice.23), channel_id=1, source_target_pairs={{4,0},{8,4},{12,8},{16,12},{20,16},{24,20},{28,24},{32,28},{36,32}... | collective-permute-start | bytes 393224 | tf_op jit(solution)/shard_map/ppermute | solution.py:244
  165.6 1.9 collective-permute-start.12
  202.2 7.3 %collective-permute-start.13 = (f32[64,128]{1,0:T(8,128)S(1)}, f32[64,128]{1,0:T(8,128)S(1)}, u32[]{:S(2)}, u32[]{:S(2)}) collective-permute-start(f32[64,128]{1,0:T(8,128)S(1)} %slice.24), channel_id=1, source_target_pairs={{0,4},{4,8},{8,12},{12,16},{16,20},{20,24},{24,28},{28,32},{32,36}... | collective-permute-start | bytes 98312 | tf_op jit(solution)/shard_map/ppermute | solution.py:249

commit v4 on v3

--- a/solution.py
+++ b/solution.py
@@ -120,12 +120,16 @@
                 head[j, i // 2] = block
 
 
-def chain(wins, blocks, count, offset, carry):
+def chain(wins, blocks, count, offset, carry, fresh=0):
     kept = carry
     added = []
+    used = wins[: len(wins) - fresh]
     for j in range(count):
-        rest = [win[pl.ds(offset + (j + 1) * W, W), :] for win in wins]
-        added.append(dot(blocks(j)[:, W:], jnp.concatenate(rest, 1)))
+        rest = [win[pl.ds(offset + (j + 1) * W, W), :] for win in used]
+        add = dot(blocks(j)[:, W:], jnp.concatenate(rest, 1))
+        if fresh:
+            add = jnp.concatenate([add, jnp.zeros((S, fresh * S), F32)], 1)
+        added.append(add)
     for j in range(count):
         out = dot(blocks(j)[:, :W], carry) + added[j]
         for k, win in enumerate(wins):
@@ -160,7 +164,7 @@
 
     ones = jnp.where(r == c, 1.0, 0.0).astype(F32)
     carry = jnp.concatenate([jnp.where(leading, window[pl.ds(off_a, W), :], 0.0), ones], 1)
-    partial[:W] = chain(wins, first, 6, off_a, carry)
+    partial[:W] = chain(wins, first, 6, off_a, carry, fresh=1)
     for part in wins:
         part[H:, :] = jnp.where(last, 0.0, part[H:, :])
     ones = jnp.where(r + W == c, 1.0, 0.0).astype(F32)
@@ -192,26 +196,35 @@
     share[...] = jnp.where(upper, high, low)
 
 
+def after(later, earlier):
+    own = jnp.concatenate([later[:, :S], jnp.zeros((S, S), F32)], 1)
+    return dot(later[:, S:], earlier) + own
+
+
 def enter_kernel(other, shares, carry, at_chip, out):
     z, upper = lax.axis_index("z"), lax.axis_index("core") == 1
-    entry = jnp.where(upper, other[:, S:], eye(S))
-    add = jnp.where(upper, other[:, :S], 0.0)
-    for k in reversed(range(CHIPS)):
+    same = jnp.concatenate([jnp.zeros((S, S), F32), eye(S)], 1)
+    chips = []
+    for k in range(CHIPS):
         low = shares[2 * k * SHARE : (2 * k + 1) * SHARE]
         high = shares[(2 * k + 1) * SHARE : (2 * k + 2) * SHARE]
         step = unpacked(low[: W // 2], high[:W])
         rows = jnp.concatenate([low[W // 2 :], high[W:]], 0)
-        if k == CHIPS - 1:
-            total = jnp.concatenate([jnp.zeros_like(rows), rows], 0)
-            to_here, to_end = jnp.where(k == z, entry, 0.0), step
-            continue
-        both = dot(jnp.concatenate([to_here, to_end], 0), jnp.concatenate([rows, step], 1))
-        total = total + both[:, :S]
-        to_here = jnp.where(k == z, entry, both[:S, S:])
-        to_end = both[S:, S:]
-    carry[...] = total[:S] + add
-    at_chip[...] = to_here
-    value = jnp.concatenate([total[S:], packed(to_end), to_end[W:]], 0)
+        chips.append(jnp.concatenate([rows, step], 1))
+    pairs = [after(chips[k + 1], chips[k]) for k in range(0, CHIPS, 2)]
+    four, two, one = z >= 4, lax.rem(z, 4) >= 2, lax.rem(z, 2) == 1
+    single = jnp.where(
+        four, jnp.where(two, chips[6], chips[4]), jnp.where(two, chips[2], chips[0])
+    )
+    nearest = after(jnp.where(upper, other[...], same), jnp.where(one, single, same))
+    pair = jnp.where(two, jnp.where(four, pairs[2], pairs[0]), same)
+    front = after(pairs[1], pairs[0])
+    back = after(pairs[3], pairs[2])
+    here = after(after(nearest, pair), jnp.where(four, front, same))
+    carry[...] = here[:, :S]
+    at_chip[...] = here[:, S:]
+    total = after(back, front)
+    value = jnp.concatenate([total[:, :S], packed(total[:, S:]), total[W:, S:]], 0)
     for x in range(PLANES):
         out[x] = value
 
@@ -219,14 +232,18 @@
 def finish_kernel(n, order, offsets, carry, at_chip, crossing, response, window, out):
     x = lax.axis_index("x")
     off_b = offsets[order[2 * n + 1]]
-    total = carry[...]
-    value = jnp.where(x == PLANES - 1, at_chip[...], 0.0)
-    for k in reversed(range(PLANES - 1)):
+
+    def plane(k):
         step = unpacked(crossing[k, S : S + W // 2], crossing[k, S + W // 2 :])
-        both = dot(value, jnp.concatenate([crossing[k, :S], step], 1))
-        total = total + both[:, :S]
-        value = jnp.where(k == x, at_chip[...], both[:, S:])
+        return crossing[k, :S], step
+
+    (rows0, _), (rows1, step1), (rows2, step2) = plane(0), plane(1), plane(2)
     out[...] = window[...]
+    entry = jnp.where(x == 0, 0.0, at_chip[...])
+    third = dot(entry, jnp.concatenate([rows2, step2], 1))
+    through = jnp.where(x == 3, third[:, S:], entry)
+    arrived = jnp.where(x == 1, rows0, rows1 + dot(step1, rows0))
+    total = carry[...] + dot(through, arrived) + jnp.where(x == 3, third[:, :S], 0.0)
     rows = pl.ds(off_b, H)
     out[rows, :] = out[rows, :] + dot(response[...], total)
 
@@ -286,6 +303,8 @@
             [(S, columns), (S, S), (PLANES, 2 * SHARE, S)],
             other, shares,
         )
+        if n == 0:
+            out, parts = lax.optimization_barrier((out, parts))
         crossing = lax.all_to_all(out, "x", 0, 0)
         if n == 0:
             crossing, parts = lax.optimization_barrier((crossing, parts))

time: 212 us -> 208 us (0.981)
  blocking collectives: 116 us -> 128 us
  waiting for transfers between devices: 26.9 us -> 18.6 us
  Pallas kernels: 30.6 us -> 26.5 us
  starting transfers between devices: 37.2 us -> 33.7 us
    all_to_all x3 -> x4, blocking collectives: 38.2 us -> 49.6 us  [local(): crossing = lax.all_to_all(out, 'x', 0, 0)]
    all_to_all x1 -> x0, waiting for transfers between devices: 7.82 us -> none  [local(): crossing = lax.all_to_all(out, 'x', 0, 0)]
    all_to_all x1 -> x0, starting transfers between devices: 4.82 us -> none  [local(): crossing = lax.all_to_all(out, 'x', 0, 0)]
    pallas_call x20, Pallas kernels: 30.6 us -> 26.5 us  [call(): pl.pallas_call(body, out_shape=shapes[0] if single else shapes, in_specs=...]
  transfers between devices with their start and end apart: 16 -> 15, of which waited for: 9 -> 8; matrix products, arithmetic and copies ran while one was open for 0% -> 0% of each run, Pallas kernels for 3% -> 3%
where the time goes in v4:
time: 208 us; the launch traced here: 207 us
  blocking collectives  128 us (62%)
  starting transfers between devices  33.7 us (16%)
  Pallas kernels  26.5 us (13%)
  waiting for transfers between devices  18.6 us (9%)
    all_gather x4, blocking collectives, local(): shares = lax.all_gather(share, ('z', 'core'), axis=0, tiled=True)  78.6 us
    all_to_all x4, blocking collectives, local(): crossing = lax.all_to_all(out, 'x', 0, 0)  49.6 us
    pallas_call x20, Pallas kernels, call(): pl.pallas_call(body, out_shape=shapes[0] if single else shapes, in_specs=...  26.5 us
    ppermute x6, starting transfers between devices, from_next(): return lax.ppermute(block, ROW, [(i + 1, i) for i in range(size - 1)])  21.6 us
    ppermute x6, waiting for transfers between devices, from_next(): return lax.ppermute(block, ROW, [(i + 1, i) for i in range(size - 1)])  9.99 us
    ppermute x1, waiting for transfers between devices, from_previous(): return lax.ppermute(block, ROW, [(i, i + 1) for i in range(size - 1)])  5.41 us
    all_to_all x1, starting transfers between devices, local(): blocks = lax.all_to_all(block, 'col', 0, 0)  4.48 us
  transfers between devices with their start and end apart: 15, of which 8 were waited for; matrix products, arithmetic and copies ran while one was open for 0% of the time, Pallas kernels for 3%

profile of v4, /device:TPU:2, one launch (start us, length us, event | category | flops | bytes accessed | tf_op | source)
XLA Modules:
  0.0 207.2 jit_solution(16310295678517142054)
XLA Ops:
  0.0 2.9 %shard_map.56 = f32[4,2,128,128]{3,2,1,0:T(8,128)} custom-call(s32[8]{0:T(128)} %order.21, f32[8,1,64,128]{3,2,1,0:T(8,128)} %bitcast.1, f32[8,1,64,64]{3,2,1,0:T(8,128)} %tri.3), custom_call_target="tpu_custom_call" | custom-call | flops 20000000 | bytes 1000000 | tf_op jit(solution)/shard_map/pallas_call | solution.py:53
  2.9 4.5 %all-to-all-start = ((f32[4,2,128,128]{3,2,1,0:T(8,128)}), f32[4,2,128,128]{3,2,1,0:T(8,128)S(1)}, u32[]{:S(2)}, u32[]{:S(2)}) async-start(f32[4,2,128,128]{3,2,1,0:T(8,128)} %shard_map.56), calls=%async_computation | async-start | bytes 1048576 | tf_op jit(solution)/shard_map/all_to_all | solution.py:281
  7.4 6.9 %collective-permute-start = (f32[256,128]{1,0:T(8,128)S(1)}, f32[256,128]{1,0:T(8,128)S(1)}, u32[]{:S(2)}, u32[]{:S(2)}) collective-permute-start(f32[256,128]{1,0:T(8,128)S(1)} %copy-done.1), channel_id=1, source_target_pairs={{4,0},{8,4},{12,8},{16,12},{20,16},{24,20},{28,24},{32,28},{36,32}... | collective-permute-start | bytes 393224 | tf_op jit(solution)/shard_map/ppermute | solution.py:261
  14.3 3.4 %shard_map.55.part0 = f32[6,128,128]{2,1,0:T(8,128)} custom-call(s32[8]{0:T(128)} %order.21, f32[8,1,64,128]{3,2,1,0:T(8,128)} %bitcast.2, f32[8,1,64,64]{3,2,1,0:T(8,128)} %tri.3), custom_call_target="tpu_custom_call" | custom-call | flops 20000000 | bytes 1000000 | tf_op jit(solution)/shard_map/pallas_call | solution.py:53
  17.8 4.9 %collective-permute-start.1 = (f32[2,1,128,128]{3,2,1,0:T(8,128)S(1)}, f32[2,1,128,128]{3,2,1,0:T(8,128)S(1)}, u32[]{:S(2)}, u32[]{:S(2)}) collective-permute-start(f32[2,1,128,128]{3,2,1,0:T(8,128)S(1)} %slice.16), channel_id=1, source_target_pairs={{4,0},{8,4},{12,8},{16,12},{20,16},{24,20},{28,24},{32,28},{36,32}... | collective-permute-start | bytes 393224 | tf_op jit(solution)/shard_map/ppermute | solution.py:261
  22.6 2.5 %collective-permute-done.1.halo = f32[2,1,128,128]{3,2,1,0:T(8,128)S(1)} collective-permute-done((f32[2,1,128,128]{3,2,1,0:T(8,128)S(1)}, f32[2,1,128,128]{3,2,1,0:T(8,128)S(1)}, u32[]{:S(2)}, u32[]{:S(2)}) %collective-permute-start.1) | collective-permute-done | bytes 131104 | tf_op jit(solution)/shard_map/ppermute | solution.py:261
  25.1 2.5 %shard_map.57 = (f32[128,256]{1,0:T(8,128)S(1)}, f32[512,128]{1,0:T(8,128)S(1)}, f32[256,128]{1,0:T(8,128)S(1)}) custom-call(s32[8]{0:T(128)S(1)} %copy-done.2, s32[8]{0:T(128)S(1)} %copy-done.3, f32[256,128]{1,0:T(8,128)S(1)} %copy-done.1, f32[256,128]{1,0:T(8,128)S(1)} %collective-permute-done.halo_rows, f32[4,2,128,128]{3,2,1,0:T(8,128)S(1)} %all-to-all-done.blocks, ...), custom_call_target="tpu_custom_call" | custom-call | flops 20000000 | bytes 1000000 | tf_op jit(solution)/shard_map/pallas_call | solution.py:53
  27.7 1.3 collective-permute-start.5
  29.0 1.4 collective-permute-start.4
  30.4 0.3 collective-permute-start.3
  30.8 0.2 shard_map.58
  31.0 20.9 %all_gather.12.shares = f32[1792,128]{1,0:T(8,128)S(1)} all-gather(f32[112,128]{1,0:T(8,128)S(1)} %shard_map.58), channel_id=1, replica_groups=mesh['x'=4,'z'=8,'core'=2,'col'=4] {'z','core'}, dimensions={0}, use_global_device_ids=true | all-gather | bytes 974848 | tf_op jit(solution)/shard_map/all_gather | solution.py:300
  51.9 0.8 shard_map.59
  52.7 12.5 %all_to_all.25.crossing = f32[4,224,128]{2,1,0:T(8,128)S(1)} all-to-all(f32[4,224,128]{2,1,0:T(8,128)S(1)} %get-tuple-element.49), channel_id=1, replica_groups=mesh['x'=4,'z'=8,'core'=2,'col'=4] {'x'}, dimensions={0} | all-to-all | bytes 917504 | tf_op jit(solution)/shard_map/all_to_all | solution.py:308
  65.2 0.3 shard_map.61
  65.5 2.5 %collective-permute-start.7 = (f32[2,3,128,128]{3,2,1,0:T(8,128)S(1)}, f32[2,3,128,128]{3,2,1,0:T(8,128)S(1)}, u32[]{:S(2)}, u32[]{:S(2)}) collective-permute-start(f32[2,3,128,128]{3,2,1,0:T(8,128)S(1)} %get-tuple-element.62), channel_id=1, source_target_pairs={{4,0},{8,4},{12,8},{16,12},{20,16},{24,20},{28,24},{32,28},{36,32}... | collective-permute-start | bytes 1179656 | tf_op jit(solution)/shard_map/ppermute | solution.py:261
  68.0 1.2 shard_map.60.own
  69.2 3.5 %collective-permute-start.6 = (f32[256,128]{1,0:T(8,128)S(1)}, f32[256,128]{1,0:T(8,128)S(1)}, u32[]{:S(2)}, u32[]{:S(2)}) collective-permute-start(f32[256,128]{1,0:T(8,128)S(1)} %slice.21), channel_id=1, source_target_pairs={{4,0},{8,4},{12,8},{16,12},{20,16},{24,20},{28,24},{32,28},{36,32}... | collective-permute-start | bytes 393224 | tf_op jit(solution)/shard_map/ppermute | solution.py:261
  72.8 2.5 %collective-permute-done.6.halo_rows = f32[256,128]{1,0:T(8,128)S(1)} collective-permute-done((f32[256,128]{1,0:T(8,128)S(1)}, f32[256,128]{1,0:T(8,128)S(1)}, u32[]{:S(2)}, u32[]{:S(2)}) %collective-permute-start.6) | collective-permute-done | bytes 131104 | tf_op jit(solution)/shard_map/ppermute | solution.py:261
  75.3 2.5 %shard_map.62 = (f32[128,256]{1,0:T(8,128)S(1)}, f32[512,128]{1,0:T(8,128)S(1)}, f32[256,128]{1,0:T(8,128)S(1)}) custom-call(s32[8]{0:T(128)S(1)} %copy-done.2, s32[8]{0:T(128)S(1)} %copy-done.3, f32[512,128]{1,0:T(8,128)S(1)} %shard_map.60.own, f32[256,128]{1,0:T(8,128)S(1)} %collective-permute-done.6.halo_rows, ...), custom_call_target="tpu_custom_call" | custom-call | flops 20000000 | bytes 1000000 | tf_op jit(solution)/shard_map/pallas_call | solution.py:53
  78.0 1.2 collective-permute-done.8.other
  79.2 0.2 shard_map.63
  79.4 19.7 %all_gather.13.shares = f32[1792,128]{1,0:T(8,128)S(1)} all-gather(f32[112,128]{1,0:T(8,128)S(1)} %shard_map.63), channel_id=1, replica_groups=mesh['x'=4,'z'=8,'core'=2,'col'=4] {'z','core'}, dimensions={0}, use_global_device_ids=true | all-gather | bytes 974848 | tf_op jit(solution)/shard_map/all_gather | solution.py:300
  99.2 0.8 shard_map.64
  99.9 11.9 %all_to_all.26.crossing = f32[4,224,128]{2,1,0:T(8,128)S(1)} all-to-all(f32[4,224,128]{2,1,0:T(8,128)S(1)} %get-tuple-element.66), channel_id=1, replica_groups=mesh['x'=4,'z'=8,'core'=2,'col'=4] {'x'}, dimensions={0} | all-to-all | bytes 917504 | tf_op jit(solution)/shard_map/all_to_all | solution.py:308
  111.9 1.2 shard_map.65.own
  113.1 1.9 collective-permute-start.9
  115.0 2.5 %collective-permute-done.9.halo_rows = f32[256,128]{1,0:T(8,128)S(1)} collective-permute-done((f32[256,128]{1,0:T(8,128)S(1)}, f32[256,128]{1,0:T(8,128)S(1)}, u32[]{:S(2)}, u32[]{:S(2)}) %collective-permute-start.9) | collective-permute-done | bytes 131104 | tf_op jit(solution)/shard_map/ppermute | solution.py:261
  117.5 2.5 %shard_map.66 = (f32[128,256]{1,0:T(8,128)S(1)}, f32[512,128]{1,0:T(8,128)S(1)}, f32[256,128]{1,0:T(8,128)S(1)}) custom-call(s32[8]{0:T(128)S(1)} %copy-done.2, s32[8]{0:T(128)S(1)} %copy-done.3, f32[512,128]{1,0:T(8,128)S(1)} %shard_map.65.own, f32[256,128]{1,0:T(8,128)S(1)} %collective-permute-done.9.halo_rows, ...), custom_call_target="tpu_custom_call" | custom-call | flops 20000000 | bytes 1000000 | tf_op jit(solution)/shard_map/pallas_call | solution.py:53
  120.0 1.4 collective-permute-start.10
  121.4 1.0 collective-permute-done.10.other
  122.4 0.2 shard_map.67
  122.6 18.8 %all_gather.14.shares = f32[1792,128]{1,0:T(8,128)S(1)} all-gather(f32[112,128]{1,0:T(8,128)S(1)} %shard_map.67), channel_id=1, replica_groups=mesh['x'=4,'z'=8,'core'=2,'col'=4] {'z','core'}, dimensions={0}, use_global_device_ids=true | all-gather | bytes 974848 | tf_op jit(solution)/shard_map/all_gather | solution.py:300
  141.4 0.8 shard_map.68
  142.2 12.6 %all_to_all.27.crossing = f32[4,224,128]{2,1,0:T(8,128)S(1)} all-to-all(f32[4,224,128]{2,1,0:T(8,128)S(1)} %get-tuple-element.72), channel_id=1, replica_groups=mesh['x'=4,'z'=8,'core'=2,'col'=4] {'x'}, dimensions={0} | all-to-all | bytes 917504 | tf_op jit(solution)/shard_map/all_to_all | solution.py:308
  154.8 1.2 shard_map.69.own
  156.0 1.9 collective-permute-start.11
  157.9 2.5 %collective-permute-done.11.halo_rows = f32[256,128]{1,0:T(8,128)S(1)} collective-permute-done((f32[256,128]{1,0:T(8,128)S(1)}, f32[256,128]{1,0:T(8,128)S(1)}, u32[]{:S(2)}, u32[]{:S(2)}) %collective-permute-start.11) | collective-permute-done | bytes 131104 | tf_op jit(solution)/shard_map/ppermute | solution.py:261
  160.4 2.5 %shard_map.70 = (f32[128,256]{1,0:T(8,128)S(1)}, f32[512,128]{1,0:T(8,128)S(1)}, f32[256,128]{1,0:T(8,128)S(1)}) custom-call(s32[8]{0:T(128)S(1)} %copy-done.2, s32[8]{0:T(128)S(1)} %copy-done.3, f32[512,128]{1,0:T(8,128)S(1)} %shard_map.69.own, f32[256,128]{1,0:T(8,128)S(1)} %collective-permute-done.11.halo_rows, ...), custom_call_target="tpu_custom_call" | custom-call | flops 20000000 | bytes 1000000 | tf_op jit(solution)/shard_map/pallas_call | solution.py:53
  162.9 0.9 collective-permute-start.12
  163.7 1.0 collective-permute-done.12.other
  165.0 19.2 %all_gather.15.shares = f32[1792,128]{1,0:T(8,128)S(1)} all-gather(f32[112,128]{1,0:T(8,128)S(1)} %shard_map.71), channel_id=1, replica_groups=mesh['x'=4,'z'=8,'core'=2,'col'=4] {'z','core'}, dimensions={0}, use_global_device_ids=true | all-gather | bytes 974848 | tf_op jit(solution)/shard_map/all_gather | solution.py:300
  184.1 0.8 shard_map.72
  184.9 12.6 %all_to_all.28.crossing = f32[4,224,128]{2,1,0:T(8,128)S(1)} all-to-all(f32[4,224,128]{2,1,0:T(8,128)S(1)} %get-tuple-element.78), channel_id=1, replica_groups=mesh['x'=4,'z'=8,'core'=2,'col'=4] {'x'}, dimensions={0} | all-to-all | bytes 917504 | tf_op jit(solution)/shard_map/all_to_all | solution.py:308
  197.5 1.2 shard_map.73.window
  198.7 1.9 collective-permute-start.13
  200.6 5.4 %collective-permute-done.13.before = f32[64,128]{1,0:T(8,128)S(1)} collective-permute-done((f32[64,128]{1,0:T(8,128)S(1)}, f32[64,128]{1,0:T(8,128)S(1)}, u32[]{:S(2)}, u32[]{:S(2)}) %collective-permute-start.13) | collective-permute-done | bytes 32800 | tf_op jit(solution)/shard_map/ppermute | solution.py:266
  206.0 1.2 shard_map.74
  (23 shorter events, 0.6 us)
Async XLA Ops:
  0.0 7.4 %copy-start.1 = (f32[256,128]{1,0:T(8,128)S(1)}, f32[256,128]{1,0:T(8,128)}, u32[]{:S(2)}) copy-start(f32[256,128]{1,0:T(8,128)} %own.1) | copy-start | bytes 393220
  0.0 25.1 %copy-start.2 = (s32[8]{0:T(128)S(1)}, s32[8]{0:T(128)}, u32[]{:S(2)}) copy-start(s32[8]{0:T(128)} %order.21) | copy-start | bytes 100
  0.0 25.1 %copy-start.3 = (s32[8]{0:T(128)S(1)}, s32[8]{0:T(128)}, u32[]{:S(2)}) copy-start(s32[8]{0:T(128)} %offsets.17) | copy-start | bytes 100
  2.9 14.8 %all-to-all-start = ((f32[4,2,128,128]{3,2,1,0:T(8,128)}), f32[4,2,128,128]{3,2,1,0:T(8,128)S(1)}, u32[]{:S(2)}, u32[]{:S(2)}) async-start(f32[4,2,128,128]{3,2,1,0:T(8,128)} %shard_map.56), calls=%async_computation | async-start | bytes 1048576 | tf_op jit(solution)/shard_map/all_to_all | solution.py:281
  7.4 15.2 %collective-permute-start = (f32[256,128]{1,0:T(8,128)S(1)}, f32[256,128]{1,0:T(8,128)S(1)}, u32[]{:S(2)}, u32[]{:S(2)}) collective-permute-start(f32[256,128]{1,0:T(8,128)S(1)} %copy-done.1), channel_id=1, source_target_pairs={{4,0},{8,4},{12,8},{16,12},{20,16},{24,20},{28,24},{32,28},{36,32}... | collective-permute-start | bytes 393224 | tf_op jit(solution)/shard_map/ppermute | solution.py:261
  17.8 7.4 %collective-permute-start.1 = (f32[2,1,128,128]{3,2,1,0:T(8,128)S(1)}, f32[2,1,128,128]{3,2,1,0:T(8,128)S(1)}, u32[]{:S(2)}, u32[]{:S(2)}) collective-permute-start(f32[2,1,128,128]{3,2,1,0:T(8,128)S(1)} %slice.16), channel_id=1, source_target_pairs={{4,0},{8,4},{12,8},{16,12},{20,16},{24,20},{28,24},{32,28},{36,32}... | collective-permute-start | bytes 393224 | tf_op jit(solution)/shard_map/ppermute | solution.py:261
  27.6 37.6 %copy-start = (f32[6,128,128]{2,1,0:T(8,128)S(1)}, f32[6,128,128]{2,1,0:T(8,128)}, u32[]{:S(2)}) copy-start(f32[6,128,128]{2,1,0:T(8,128)} %shard_map.55.part0) | copy-start | bytes 1179652
  27.6 3.1 %collective-permute-start.2 = (f32[128,256]{1,0:T(8,128)S(1)}, f32[128,256]{1,0:T(8,128)S(1)}, u32[]{:S(2)}, u32[]{:S(2)}) collective-permute-start(f32[128,256]{1,0:T(8,128)S(1)} %get-tuple-element.44.partial), channel_id=1, source_target_pairs={{0,4},{4,0},{1,5},{5,1},{2,6},{6,2},{3,7},{7,3},{8,12},{12,8},{9,1... | collective-permute-start | bytes 393224 | tf_op jit(solution)/shard_map/ppermute | solution.py:270
  27.7 25.0 %collective-permute-start.5 = (f32[6,128,128]{2,1,0:T(8,128)}, f32[6,128,128]{2,1,0:T(8,128)S(1)}, u32[]{:S(2)}, u32[]{:S(2)}) collective-permute-start(f32[6,128,128]{2,1,0:T(8,128)} %shard_map.55.part0), channel_id=1, source_target_pairs={{0,3},{1,0},{2,1},{3,2},{4,7},{5,4},{6,5},{7,6},{8,11},{9,8},{10,9... | collective-permute-start | bytes 1179656 | tf_op jit(solution)/shard_map/ppermute | solution.py:288
  29.0 23.7 %collective-permute-start.4 = (f32[6,128,128]{2,1,0:T(8,128)}, f32[6,128,128]{2,1,0:T(8,128)S(1)}, u32[]{:S(2)}, u32[]{:S(2)}) collective-permute-start(f32[6,128,128]{2,1,0:T(8,128)} %shard_map.55.part0), channel_id=1, source_target_pairs={{0,2},{1,3},{2,0},{3,1},{4,6},{5,7},{6,4},{7,5},{8,10},{9,11},{10,... | collective-permute-start | bytes 1179656 | tf_op jit(solution)/shard_map/ppermute | solution.py:288
  30.4 22.3 %collective-permute-start.3 = (f32[6,128,128]{2,1,0:T(8,128)}, f32[6,128,128]{2,1,0:T(8,128)S(1)}, u32[]{:S(2)}, u32[]{:S(2)}) collective-permute-start(f32[6,128,128]{2,1,0:T(8,128)} %shard_map.55.part0), channel_id=1, source_target_pairs={{0,1},{1,2},{2,3},{3,0},{4,5},{5,6},{6,7},{7,4},{8,9},{9,10},{10,1... | collective-permute-start | bytes 1179656 | tf_op jit(solution)/shard_map/ppermute | solution.py:288
  65.5 9.8 %collective-permute-start.7 = (f32[2,3,128,128]{3,2,1,0:T(8,128)S(1)}, f32[2,3,128,128]{3,2,1,0:T(8,128)S(1)}, u32[]{:S(2)}, u32[]{:S(2)}) collective-permute-start(f32[2,3,128,128]{3,2,1,0:T(8,128)S(1)} %get-tuple-element.62), channel_id=1, source_target_pairs={{4,0},{8,4},{12,8},{16,12},{20,16},{24,20},{28,24},{32,28},{36,32}... | collective-permute-start | bytes 1179656 | tf_op jit(solution)/shard_map/ppermute | solution.py:261
  69.2 6.0 %collective-permute-start.6 = (f32[256,128]{1,0:T(8,128)S(1)}, f32[256,128]{1,0:T(8,128)S(1)}, u32[]{:S(2)}, u32[]{:S(2)}) collective-permute-start(f32[256,128]{1,0:T(8,128)S(1)} %slice.21), channel_id=1, source_target_pairs={{4,0},{8,4},{12,8},{16,12},{20,16},{24,20},{28,24},{32,28},{36,32}... | collective-permute-start | bytes 393224 | tf_op jit(solution)/shard_map/ppermute | solution.py:261
  77.7 1.4 collective-permute-start.8
  113.1 4.4 %collective-permute-start.9 = (f32[256,128]{1,0:T(8,128)S(1)}, f32[256,128]{1,0:T(8,128)S(1)}, u32[]{:S(2)}, u32[]{:S(2)}) collective-permute-start(f32[256,128]{1,0:T(8,128)S(1)} %slice.22), channel_id=1, source_target_pairs={{4,0},{8,4},{12,8},{16,12},{20,16},{24,20},{28,24},{32,28},{36,32}... | collective-permute-start | bytes 393224 | tf_op jit(solution)/shard_map/ppermute | solution.py:261
  120.0 2.4 %collective-permute-start.10 = (f32[128,256]{1,0:T(8,128)S(1)}, f32[128,256]{1,0:T(8,128)S(1)}, u32[]{:S(2)}, u32[]{:S(2)}) collective-permute-start(f32[128,256]{1,0:T(8,128)S(1)} %get-tuple-element.69.partial), channel_id=1, source_target_pairs={{0,4},{4,0},{1,5},{5,1},{2,6},{6,2},{3,7},{7,3},{8,12},{12,8},{9,1... | collective-permute-start | bytes 393224 | tf_op jit(solution)/shard_map/ppermute | solution.py:270
  156.0 4.4 %collective-permute-start.11 = (f32[256,128]{1,0:T(8,128)S(1)}, f32[256,128]{1,0:T(8,128)S(1)}, u32[]{:S(2)}, u32[]{:S(2)}) collective-permute-start(f32[256,128]{1,0:T(8,128)S(1)} %slice.23), channel_id=1, source_target_pairs={{4,0},{8,4},{12,8},{16,12},{20,16},{24,20},{28,24},{32,28},{36,32}... | collective-permute-start | bytes 393224 | tf_op jit(solution)/shard_map/ppermute | solution.py:261
  162.9 1.9 collective-permute-start.12
  198.7 7.3 %collective-permute-start.13 = (f32[64,128]{1,0:T(8,128)S(1)}, f32[64,128]{1,0:T(8,128)S(1)}, u32[]{:S(2)}, u32[]{:S(2)}) collective-permute-start(f32[64,128]{1,0:T(8,128)S(1)} %slice.24), channel_id=1, source_target_pairs={{0,4},{4,8},{8,12},{12,16},{16,20},{20,24},{24,28},{28,32},{32,36}... | collective-permute-start | bytes 98312 | tf_op jit(solution)/shard_map/ppermute | solution.py:266

commit v5 on v4

--- a/solution.py
+++ b/solution.py
@@ -120,24 +120,41 @@
                 head[j, i // 2] = block
 
 
-def chain(wins, blocks, count, offset, carry, fresh=0):
-    kept = carry
-    added = []
-    used = wins[: len(wins) - fresh]
+def chain(wins, blocks, count, offset, carry, probe):
+    wide = len(wins) * S
+    used = [win for k, win in enumerate(wins) if k * S < probe]
+    added, steps = [], []
     for j in range(count):
         rest = [win[pl.ds(offset + (j + 1) * W, W), :] for win in used]
-        add = dot(blocks(j)[:, W:], jnp.concatenate(rest, 1))
-        if fresh:
-            add = jnp.concatenate([add, jnp.zeros((S, fresh * S), F32)], 1)
-        added.append(add)
+        rest = jnp.concatenate(rest, 1)
+        if j == 0:
+            start = [carry] + [jnp.zeros((W, S), F32)] * (len(used) - 1)
+            start = jnp.concatenate(start, 1)
+            add = dot(blocks(0), jnp.concatenate([start, rest], 0))
+        else:
+            add = dot(blocks(j)[:, W:], rest)
+        add = add[:, :probe]
+        blank = [jnp.zeros((W, wide - probe - W), F32)] if wide - probe - W else []
+        steps.append(jnp.concatenate([add[W:], blocks(j)[W:, :W]] + blank, 1))
+        zero = jnp.zeros((S, wide - probe), F32)
+        added.append(jnp.concatenate([add, zero], 1))
+
+    def join(later, earlier):
+        own = jnp.concatenate([later[:, :probe], jnp.zeros((W, wide - probe), F32)], 1)
+        return dot(later[:, probe : probe + W], earlier) + own
+
+    pairs = [join(steps[k + 1], steps[k]) for k in range(0, count, 2)]
+    r = lax.broadcasted_iota(jnp.int32, (W, wide), 0)
+    c = lax.broadcasted_iota(jnp.int32, (W, wide), 1)
+    entering = [jnp.where(r + probe == c, 1.0, 0.0).astype(F32), steps[0], pairs[0]]
+    entering += [join(steps[2], pairs[0]), join(pairs[1], pairs[0])]
+    if count == 6:
+        entering.append(join(steps[4], entering[4]))
     for j in range(count):
-        out = dot(blocks(j)[:, :W], carry) + added[j]
+        done = dot(blocks(j)[:W, :W], entering[j]) + added[j][:W]
         for k, win in enumerate(wins):
-            win[pl.ds(offset + j * W, W), :] = out[:W, k * S : (k + 1) * S]
-        carry = out[W:]
-        if j == 3:
-            kept = carry
-    return kept
+            win[pl.ds(offset + j * W, W), :] = done[:, k * S : (k + 1) * S]
+    return entering[4]
 
 
 def phase_kernel(n, i, order, offsets, own, halo_rows, blocks, halo, partial, window, response, win):
@@ -152,8 +169,6 @@
         window[H:, :] = jnp.where((rows < before) & ~last, own[H:, :], halo_rows[...])
     else:
         window[H:, :] = halo_rows[...]
-    r = lax.broadcasted_iota(jnp.int32, (W, S), 0)
-    c = lax.broadcasted_iota(jnp.int32, (W, S), 1)
     wins = [window, win]
 
     def first(j):
@@ -162,14 +177,12 @@
     def second(j):
         return blocks[j, 2 * i + 1]
 
-    ones = jnp.where(r == c, 1.0, 0.0).astype(F32)
-    carry = jnp.concatenate([jnp.where(leading, window[pl.ds(off_a, W), :], 0.0), ones], 1)
-    partial[:W] = chain(wins, first, 6, off_a, carry, fresh=1)
+    carry = jnp.where(leading, window[pl.ds(off_a, W), :], 0.0)
+    partial[:W] = chain(wins, first, 6, off_a, carry, S)
     for part in wins:
         part[H:, :] = jnp.where(last, 0.0, part[H:, :])
-    ones = jnp.where(r + W == c, 1.0, 0.0).astype(F32)
-    carry = jnp.concatenate([jnp.where(leading, window[pl.ds(off_b, W), :], 0.0), ones], 1)
-    partial[W:] = chain(wins, second, 4, off_b, carry)
+    carry = jnp.where(leading, window[pl.ds(off_b, W), :], 0.0)
+    partial[W:] = chain(wins, second, 4, off_b, carry, S + W)
     response[...] = win[pl.ds(off_b, H), :]
 
 

time: 208 us -> 207 us (level)
  no operation moved by 1% of the time
where the time goes in v5:
time: 207 us; the launch traced here: 206 us
  blocking collectives  128 us (62%)
  starting transfers between devices  33.9 us (16%)
  Pallas kernels  25.5 us (12%)
  waiting for transfers between devices  18.6 us (9%)
    all_gather x4, blocking collectives, local(): shares = lax.all_gather(share, ('z', 'core'), axis=0, tiled=True)  78.4 us
    all_to_all x4, blocking collectives, local(): crossing = lax.all_to_all(out, 'x', 0, 0)  49.6 us
    pallas_call x20, Pallas kernels, call(): pl.pallas_call(body, out_shape=shapes[0] if single else shapes, in_specs=...  25.5 us
    ppermute x6, starting transfers between devices, from_next(): return lax.ppermute(block, ROW, [(i + 1, i) for i in range(size - 1)])  21.6 us
    ppermute x6, waiting for transfers between devices, from_next(): return lax.ppermute(block, ROW, [(i + 1, i) for i in range(size - 1)])  9.99 us
    ppermute x1, waiting for transfers between devices, from_previous(): return lax.ppermute(block, ROW, [(i, i + 1) for i in range(size - 1)])  5.41 us
    all_to_all x1, starting transfers between devices, local(): blocks = lax.all_to_all(block, 'col', 0, 0)  4.48 us
  transfers between devices with their start and end apart: 15, of which 8 were waited for; matrix products, arithmetic and copies ran while one was open for 0% of the time, Pallas kernels for 3%

profile of v5, /device:TPU:2, one launch (start us, length us, event | category | flops | bytes accessed | tf_op | source)
XLA Modules:
  0.0 206.2 jit_solution(4987746751958527472)
XLA Ops:
  0.0 2.9 %shard_map.56 = f32[4,2,128,128]{3,2,1,0:T(8,128)} custom-call(s32[8]{0:T(128)} %order.21, f32[8,1,64,128]{3,2,1,0:T(8,128)} %bitcast.1, f32[8,1,64,64]{3,2,1,0:T(8,128)} %tri.3), custom_call_target="tpu_custom_call" | custom-call | flops 20000000 | bytes 1000000 | tf_op jit(solution)/shard_map/pallas_call | solution.py:53
  2.9 4.5 %all-to-all-start = ((f32[4,2,128,128]{3,2,1,0:T(8,128)}), f32[4,2,128,128]{3,2,1,0:T(8,128)S(1)}, u32[]{:S(2)}, u32[]{:S(2)}) async-start(f32[4,2,128,128]{3,2,1,0:T(8,128)} %shard_map.56), calls=%async_computation | async-start | bytes 1048576 | tf_op jit(solution)/shard_map/all_to_all | solution.py:294
  7.4 6.9 %collective-permute-start = (f32[256,128]{1,0:T(8,128)S(1)}, f32[256,128]{1,0:T(8,128)S(1)}, u32[]{:S(2)}, u32[]{:S(2)}) collective-permute-start(f32[256,128]{1,0:T(8,128)S(1)} %copy-done.1), channel_id=1, source_target_pairs={{4,0},{8,4},{12,8},{16,12},{20,16},{24,20},{28,24},{32,28},{36,32}... | collective-permute-start | bytes 393224 | tf_op jit(solution)/shard_map/ppermute | solution.py:274
  14.3 3.4 %shard_map.55.part0 = f32[6,128,128]{2,1,0:T(8,128)} custom-call(s32[8]{0:T(128)} %order.21, f32[8,1,64,128]{3,2,1,0:T(8,128)} %bitcast.2, f32[8,1,64,64]{3,2,1,0:T(8,128)} %tri.3), custom_call_target="tpu_custom_call" | custom-call | flops 20000000 | bytes 1000000 | tf_op jit(solution)/shard_map/pallas_call | solution.py:53
  17.8 4.9 %collective-permute-start.1 = (f32[2,1,128,128]{3,2,1,0:T(8,128)S(1)}, f32[2,1,128,128]{3,2,1,0:T(8,128)S(1)}, u32[]{:S(2)}, u32[]{:S(2)}) collective-permute-start(f32[2,1,128,128]{3,2,1,0:T(8,128)S(1)} %slice.16), channel_id=1, source_target_pairs={{4,0},{8,4},{12,8},{16,12},{20,16},{24,20},{28,24},{32,28},{36,32}... | collective-permute-start | bytes 393224 | tf_op jit(solution)/shard_map/ppermute | solution.py:274
  22.6 2.5 %collective-permute-done.1.halo = f32[2,1,128,128]{3,2,1,0:T(8,128)S(1)} collective-permute-done((f32[2,1,128,128]{3,2,1,0:T(8,128)S(1)}, f32[2,1,128,128]{3,2,1,0:T(8,128)S(1)}, u32[]{:S(2)}, u32[]{:S(2)}) %collective-permute-start.1) | collective-permute-done | bytes 131104 | tf_op jit(solution)/shard_map/ppermute | solution.py:274
  25.1 2.2 %shard_map.57 = (f32[128,256]{1,0:T(8,128)S(1)}, f32[512,128]{1,0:T(8,128)S(1)}, f32[256,128]{1,0:T(8,128)S(1)}) custom-call(s32[8]{0:T(128)S(1)} %copy-done.2, s32[8]{0:T(128)S(1)} %copy-done.3, f32[256,128]{1,0:T(8,128)S(1)} %copy-done.1, f32[256,128]{1,0:T(8,128)S(1)} %collective-permute-done.halo_rows, f32[4,2,128,128]{3,2,1,0:T(8,128)S(1)} %all-to-all-done.blocks, ...), custom_call_target="tpu_custom_call" | custom-call | flops 20000000 | bytes 1000000 | tf_op jit(solution)/shard_map/pallas_call | solution.py:53
  27.4 1.3 collective-permute-start.5
  28.8 1.4 collective-permute-start.4
  30.1 0.3 collective-permute-start.3
  30.5 0.2 shard_map.58
  30.7 20.9 %all_gather.12.shares = f32[1792,128]{1,0:T(8,128)S(1)} all-gather(f32[112,128]{1,0:T(8,128)S(1)} %shard_map.58), channel_id=1, replica_groups=mesh['x'=4,'z'=8,'core'=2,'col'=4] {'z','core'}, dimensions={0}, use_global_device_ids=true | all-gather | bytes 974848 | tf_op jit(solution)/shard_map/all_gather | solution.py:313
  51.7 0.8 shard_map.59
  52.5 12.5 %all_to_all.25.crossing = f32[4,224,128]{2,1,0:T(8,128)S(1)} all-to-all(f32[4,224,128]{2,1,0:T(8,128)S(1)} %get-tuple-element.49), channel_id=1, replica_groups=mesh['x'=4,'z'=8,'core'=2,'col'=4] {'x'}, dimensions={0} | all-to-all | bytes 917504 | tf_op jit(solution)/shard_map/all_to_all | solution.py:321
  64.9 0.3 shard_map.61
  65.2 2.5 %collective-permute-start.7 = (f32[2,3,128,128]{3,2,1,0:T(8,128)S(1)}, f32[2,3,128,128]{3,2,1,0:T(8,128)S(1)}, u32[]{:S(2)}, u32[]{:S(2)}) collective-permute-start(f32[2,3,128,128]{3,2,1,0:T(8,128)S(1)} %get-tuple-element.62), channel_id=1, source_target_pairs={{4,0},{8,4},{12,8},{16,12},{20,16},{24,20},{28,24},{32,28},{36,32}... | collective-permute-start | bytes 1179656 | tf_op jit(solution)/shard_map/ppermute | solution.py:274
  67.8 1.2 shard_map.60.own
  68.9 3.5 %collective-permute-start.6 = (f32[256,128]{1,0:T(8,128)S(1)}, f32[256,128]{1,0:T(8,128)S(1)}, u32[]{:S(2)}, u32[]{:S(2)}) collective-permute-start(f32[256,128]{1,0:T(8,128)S(1)} %slice.21), channel_id=1, source_target_pairs={{4,0},{8,4},{12,8},{16,12},{20,16},{24,20},{28,24},{32,28},{36,32}... | collective-permute-start | bytes 393224 | tf_op jit(solution)/shard_map/ppermute | solution.py:274
  72.5 2.5 %collective-permute-done.6.halo_rows = f32[256,128]{1,0:T(8,128)S(1)} collective-permute-done((f32[256,128]{1,0:T(8,128)S(1)}, f32[256,128]{1,0:T(8,128)S(1)}, u32[]{:S(2)}, u32[]{:S(2)}) %collective-permute-start.6) | collective-permute-done | bytes 131104 | tf_op jit(solution)/shard_map/ppermute | solution.py:274
  75.0 2.2 %shard_map.62 = (f32[128,256]{1,0:T(8,128)S(1)}, f32[512,128]{1,0:T(8,128)S(1)}, f32[256,128]{1,0:T(8,128)S(1)}) custom-call(s32[8]{0:T(128)S(1)} %copy-done.2, s32[8]{0:T(128)S(1)} %copy-done.3, f32[512,128]{1,0:T(8,128)S(1)} %shard_map.60.own, f32[256,128]{1,0:T(8,128)S(1)} %collective-permute-done.6.halo_rows, ...), custom_call_target="tpu_custom_call" | custom-call | flops 20000000 | bytes 1000000 | tf_op jit(solution)/shard_map/pallas_call | solution.py:53
  77.5 1.2 collective-permute-done.8.other
  78.7 0.2 shard_map.63
  78.9 19.7 %all_gather.13.shares = f32[1792,128]{1,0:T(8,128)S(1)} all-gather(f32[112,128]{1,0:T(8,128)S(1)} %shard_map.63), channel_id=1, replica_groups=mesh['x'=4,'z'=8,'core'=2,'col'=4] {'z','core'}, dimensions={0}, use_global_device_ids=true | all-gather | bytes 974848 | tf_op jit(solution)/shard_map/all_gather | solution.py:313
  98.6 0.8 shard_map.64
  99.4 11.9 %all_to_all.26.crossing = f32[4,224,128]{2,1,0:T(8,128)S(1)} all-to-all(f32[4,224,128]{2,1,0:T(8,128)S(1)} %get-tuple-element.66), channel_id=1, replica_groups=mesh['x'=4,'z'=8,'core'=2,'col'=4] {'x'}, dimensions={0} | all-to-all | bytes 917504 | tf_op jit(solution)/shard_map/all_to_all | solution.py:321
  111.4 1.2 shard_map.65.own
  112.6 1.9 collective-permute-start.9
  114.5 2.5 %collective-permute-done.9.halo_rows = f32[256,128]{1,0:T(8,128)S(1)} collective-permute-done((f32[256,128]{1,0:T(8,128)S(1)}, f32[256,128]{1,0:T(8,128)S(1)}, u32[]{:S(2)}, u32[]{:S(2)}) %collective-permute-start.9) | collective-permute-done | bytes 131104 | tf_op jit(solution)/shard_map/ppermute | solution.py:274
  117.0 2.2 %shard_map.66 = (f32[128,256]{1,0:T(8,128)S(1)}, f32[512,128]{1,0:T(8,128)S(1)}, f32[256,128]{1,0:T(8,128)S(1)}) custom-call(s32[8]{0:T(128)S(1)} %copy-done.2, s32[8]{0:T(128)S(1)} %copy-done.3, f32[512,128]{1,0:T(8,128)S(1)} %shard_map.65.own, f32[256,128]{1,0:T(8,128)S(1)} %collective-permute-done.9.halo_rows, ...), custom_call_target="tpu_custom_call" | custom-call | flops 20000000 | bytes 1000000 | tf_op jit(solution)/shard_map/pallas_call | solution.py:53
  119.2 1.6 collective-permute-start.10
  120.8 1.0 collective-permute-done.10.other
  121.8 0.2 shard_map.67
  122.1 18.6 %all_gather.14.shares = f32[1792,128]{1,0:T(8,128)S(1)} all-gather(f32[112,128]{1,0:T(8,128)S(1)} %shard_map.67), channel_id=1, replica_groups=mesh['x'=4,'z'=8,'core'=2,'col'=4] {'z','core'}, dimensions={0}, use_global_device_ids=true | all-gather | bytes 974848 | tf_op jit(solution)/shard_map/all_gather | solution.py:313
  140.6 0.8 shard_map.68
  141.4 12.6 %all_to_all.27.crossing = f32[4,224,128]{2,1,0:T(8,128)S(1)} all-to-all(f32[4,224,128]{2,1,0:T(8,128)S(1)} %get-tuple-element.72), channel_id=1, replica_groups=mesh['x'=4,'z'=8,'core'=2,'col'=4] {'x'}, dimensions={0} | all-to-all | bytes 917504 | tf_op jit(solution)/shard_map/all_to_all | solution.py:321
  154.0 1.2 shard_map.69.own
  155.2 1.9 collective-permute-start.11
  157.1 2.5 %collective-permute-done.11.halo_rows = f32[256,128]{1,0:T(8,128)S(1)} collective-permute-done((f32[256,128]{1,0:T(8,128)S(1)}, f32[256,128]{1,0:T(8,128)S(1)}, u32[]{:S(2)}, u32[]{:S(2)}) %collective-permute-start.11) | collective-permute-done | bytes 131104 | tf_op jit(solution)/shard_map/ppermute | solution.py:274
  159.6 2.2 %shard_map.70 = (f32[128,256]{1,0:T(8,128)S(1)}, f32[512,128]{1,0:T(8,128)S(1)}, f32[256,128]{1,0:T(8,128)S(1)}) custom-call(s32[8]{0:T(128)S(1)} %copy-done.2, s32[8]{0:T(128)S(1)} %copy-done.3, f32[512,128]{1,0:T(8,128)S(1)} %shard_map.69.own, f32[256,128]{1,0:T(8,128)S(1)} %collective-permute-done.11.halo_rows, ...), custom_call_target="tpu_custom_call" | custom-call | flops 20000000 | bytes 1000000 | tf_op jit(solution)/shard_map/pallas_call | solution.py:53
  161.9 0.9 collective-permute-start.12
  162.7 1.0 collective-permute-done.12.other
  163.9 19.2 %all_gather.15.shares = f32[1792,128]{1,0:T(8,128)S(1)} all-gather(f32[112,128]{1,0:T(8,128)S(1)} %shard_map.71), channel_id=1, replica_groups=mesh['x'=4,'z'=8,'core'=2,'col'=4] {'z','core'}, dimensions={0}, use_global_device_ids=true | all-gather | bytes 974848 | tf_op jit(solution)/shard_map/all_gather | solution.py:313
  183.1 0.8 shard_map.72
  183.9 12.6 %all_to_all.28.crossing = f32[4,224,128]{2,1,0:T(8,128)S(1)} all-to-all(f32[4,224,128]{2,1,0:T(8,128)S(1)} %get-tuple-element.78), channel_id=1, replica_groups=mesh['x'=4,'z'=8,'core'=2,'col'=4] {'x'}, dimensions={0} | all-to-all | bytes 917504 | tf_op jit(solution)/shard_map/all_to_all | solution.py:321
  196.5 1.2 shard_map.73.window
  197.7 1.9 collective-permute-start.13
  199.6 5.4 %collective-permute-done.13.before = f32[64,128]{1,0:T(8,128)S(1)} collective-permute-done((f32[64,128]{1,0:T(8,128)S(1)}, f32[64,128]{1,0:T(8,128)S(1)}, u32[]{:S(2)}, u32[]{:S(2)}) %collective-permute-start.13) | collective-permute-done | bytes 32800 | tf_op jit(solution)/shard_map/ppermute | solution.py:279
  205.0 1.2 shard_map.74
  (23 shorter events, 0.6 us)
Async XLA Ops:
  0.0 7.4 %copy-start.1 = (f32[256,128]{1,0:T(8,128)S(1)}, f32[256,128]{1,0:T(8,128)}, u32[]{:S(2)}) copy-start(f32[256,128]{1,0:T(8,128)} %own.1) | copy-start | bytes 393220
  0.0 25.1 %copy-start.2 = (s32[8]{0:T(128)S(1)}, s32[8]{0:T(128)}, u32[]{:S(2)}) copy-start(s32[8]{0:T(128)} %order.21) | copy-start | bytes 100
  0.0 25.1 %copy-start.3 = (s32[8]{0:T(128)S(1)}, s32[8]{0:T(128)}, u32[]{:S(2)}) copy-start(s32[8]{0:T(128)} %offsets.17) | copy-start | bytes 100
  2.9 14.8 %all-to-all-start = ((f32[4,2,128,128]{3,2,1,0:T(8,128)}), f32[4,2,128,128]{3,2,1,0:T(8,128)S(1)}, u32[]{:S(2)}, u32[]{:S(2)}) async-start(f32[4,2,128,128]{3,2,1,0:T(8,128)} %shard_map.56), calls=%async_computation | async-start | bytes 1048576 | tf_op jit(solution)/shard_map/all_to_all | solution.py:294
  7.4 15.2 %collective-permute-start = (f32[256,128]{1,0:T(8,128)S(1)}, f32[256,128]{1,0:T(8,128)S(1)}, u32[]{:S(2)}, u32[]{:S(2)}) collective-permute-start(f32[256,128]{1,0:T(8,128)S(1)} %copy-done.1), channel_id=1, source_target_pairs={{4,0},{8,4},{12,8},{16,12},{20,16},{24,20},{28,24},{32,28},{36,32}... | collective-permute-start | bytes 393224 | tf_op jit(solution)/shard_map/ppermute | solution.py:274
  17.8 7.4 %collective-permute-start.1 = (f32[2,1,128,128]{3,2,1,0:T(8,128)S(1)}, f32[2,1,128,128]{3,2,1,0:T(8,128)S(1)}, u32[]{:S(2)}, u32[]{:S(2)}) collective-permute-start(f32[2,1,128,128]{3,2,1,0:T(8,128)S(1)} %slice.16), channel_id=1, source_target_pairs={{4,0},{8,4},{12,8},{16,12},{20,16},{24,20},{28,24},{32,28},{36,32}... | collective-permute-start | bytes 393224 | tf_op jit(solution)/shard_map/ppermute | solution.py:274
  27.3 37.6 %copy-start = (f32[6,128,128]{2,1,0:T(8,128)S(1)}, f32[6,128,128]{2,1,0:T(8,128)}, u32[]{:S(2)}) copy-start(f32[6,128,128]{2,1,0:T(8,128)} %shard_map.55.part0) | copy-start | bytes 1179652
  27.3 3.2 %collective-permute-start.2 = (f32[128,256]{1,0:T(8,128)S(1)}, f32[128,256]{1,0:T(8,128)S(1)}, u32[]{:S(2)}, u32[]{:S(2)}) collective-permute-start(f32[128,256]{1,0:T(8,128)S(1)} %get-tuple-element.44.partial), channel_id=1, source_target_pairs={{0,4},{4,0},{1,5},{5,1},{2,6},{6,2},{3,7},{7,3},{8,12},{12,8},{9,1... | collective-permute-start | bytes 393224 | tf_op jit(solution)/shard_map/ppermute | solution.py:283
  27.4 25.0 %collective-permute-start.5 = (f32[6,128,128]{2,1,0:T(8,128)}, f32[6,128,128]{2,1,0:T(8,128)S(1)}, u32[]{:S(2)}, u32[]{:S(2)}) collective-permute-start(f32[6,128,128]{2,1,0:T(8,128)} %shard_map.55.part0), channel_id=1, source_target_pairs={{0,3},{1,0},{2,1},{3,2},{4,7},{5,4},{6,5},{7,6},{8,11},{9,8},{10,9... | collective-permute-start | bytes 1179656 | tf_op jit(solution)/shard_map/ppermute | solution.py:301
  28.8 23.7 %collective-permute-start.4 = (f32[6,128,128]{2,1,0:T(8,128)}, f32[6,128,128]{2,1,0:T(8,128)S(1)}, u32[]{:S(2)}, u32[]{:S(2)}) collective-permute-start(f32[6,128,128]{2,1,0:T(8,128)} %shard_map.55.part0), channel_id=1, source_target_pairs={{0,2},{1,3},{2,0},{3,1},{4,6},{5,7},{6,4},{7,5},{8,10},{9,11},{10,... | collective-permute-start | bytes 1179656 | tf_op jit(solution)/shard_map/ppermute | solution.py:301
  30.1 22.3 %collective-permute-start.3 = (f32[6,128,128]{2,1,0:T(8,128)}, f32[6,128,128]{2,1,0:T(8,128)S(1)}, u32[]{:S(2)}, u32[]{:S(2)}) collective-permute-start(f32[6,128,128]{2,1,0:T(8,128)} %shard_map.55.part0), channel_id=1, source_target_pairs={{0,1},{1,2},{2,3},{3,0},{4,5},{5,6},{6,7},{7,4},{8,9},{9,10},{10,1... | collective-permute-start | bytes 1179656 | tf_op jit(solution)/shard_map/ppermute | solution.py:301
  65.2 9.8 %collective-permute-start.7 = (f32[2,3,128,128]{3,2,1,0:T(8,128)S(1)}, f32[2,3,128,128]{3,2,1,0:T(8,128)S(1)}, u32[]{:S(2)}, u32[]{:S(2)}) collective-permute-start(f32[2,3,128,128]{3,2,1,0:T(8,128)S(1)} %get-tuple-element.62), channel_id=1, source_target_pairs={{4,0},{8,4},{12,8},{16,12},{20,16},{24,20},{28,24},{32,28},{36,32}... | collective-permute-start | bytes 1179656 | tf_op jit(solution)/shard_map/ppermute | solution.py:274
  68.9 6.0 %collective-permute-start.6 = (f32[256,128]{1,0:T(8,128)S(1)}, f32[256,128]{1,0:T(8,128)S(1)}, u32[]{:S(2)}, u32[]{:S(2)}) collective-permute-start(f32[256,128]{1,0:T(8,128)S(1)} %slice.21), channel_id=1, source_target_pairs={{4,0},{8,4},{12,8},{16,12},{20,16},{24,20},{28,24},{32,28},{36,32}... | collective-permute-start | bytes 393224 | tf_op jit(solution)/shard_map/ppermute | solution.py:274
  77.2 1.4 collective-permute-start.8
  112.6 4.4 %collective-permute-start.9 = (f32[256,128]{1,0:T(8,128)S(1)}, f32[256,128]{1,0:T(8,128)S(1)}, u32[]{:S(2)}, u32[]{:S(2)}) collective-permute-start(f32[256,128]{1,0:T(8,128)S(1)} %slice.22), channel_id=1, source_target_pairs={{4,0},{8,4},{12,8},{16,12},{20,16},{24,20},{28,24},{32,28},{36,32}... | collective-permute-start | bytes 393224 | tf_op jit(solution)/shard_map/ppermute | solution.py:274
  119.2 2.6 %collective-permute-start.10 = (f32[128,256]{1,0:T(8,128)S(1)}, f32[128,256]{1,0:T(8,128)S(1)}, u32[]{:S(2)}, u32[]{:S(2)}) collective-permute-start(f32[128,256]{1,0:T(8,128)S(1)} %get-tuple-element.69.partial), channel_id=1, source_target_pairs={{0,4},{4,0},{1,5},{5,1},{2,6},{6,2},{3,7},{7,3},{8,12},{12,8},{9,1... | collective-permute-start | bytes 393224 | tf_op jit(solution)/shard_map/ppermute | solution.py:283
  155.2 4.4 %collective-permute-start.11 = (f32[256,128]{1,0:T(8,128)S(1)}, f32[256,128]{1,0:T(8,128)S(1)}, u32[]{:S(2)}, u32[]{:S(2)}) collective-permute-start(f32[256,128]{1,0:T(8,128)S(1)} %slice.23), channel_id=1, source_target_pairs={{4,0},{8,4},{12,8},{16,12},{20,16},{24,20},{28,24},{32,28},{36,32}... | collective-permute-start | bytes 393224 | tf_op jit(solution)/shard_map/ppermute | solution.py:274
  161.9 1.8 collective-permute-start.12
  197.7 7.3 %collective-permute-start.13 = (f32[64,128]{1,0:T(8,128)S(1)}, f32[64,128]{1,0:T(8,128)S(1)}, u32[]{:S(2)}, u32[]{:S(2)}) collective-permute-start(f32[64,128]{1,0:T(8,128)S(1)} %slice.24), channel_id=1, source_target_pairs={{0,4},{4,8},{8,12},{12,16},{16,20},{20,24},{24,28},{28,32},{32,36}... | collective-permute-start | bytes 98312 | tf_op jit(solution)/shard_map/ppermute | solution.py:279
